TPU v7x, 256 devices: a 4x2x16 block of a 4x16x16 slice. The times are simulated.
256 devices in a mesh: groups: 2 (over y), rows: 16 (over z), cols: 8 (over x, core).
Axes of the slice: x: 4, y: 2, z: 16, core: 2. Of those that a mesh axis runs over, the one named last changes fastest.
The devices are a block of a 4x16x16 slice.
Arguments:
- tokens: bfloat16 [448, 224, 256], P(('groups', 'rows'), 'cols'), parts along dimension 0, may hold values from -6 to 6
- cotangent: bfloat16 [224, 112, 512], P(('groups', 'rows'), 'cols'), parts along dimension 0, may hold values from -6 to 6
- shift_offsets: int32 [4], replicated, may hold values from 1 to 6
- norm2_gain: float32 [256], replicated, may hold values from 0.1 to 1.9
- qkv2: bfloat16 [256, 768], replicated, may hold values from -0.375 to 0.375
- proj2: bfloat16 [256, 256], replicated, may hold values from -0.375 to 0.375
- merge_gain: float32 [1024], replicated, may hold values from 0.1 to 1.9
- merge_weight: bfloat16 [1024, 512], replicated, may hold values from -0.1875 to 0.1875
- norm3_gain: float32 [512], replicated, may hold values from 0.1 to 1.9
- qkv3: bfloat16 [512, 1536], replicated, may hold values from -0.25 to 0.25
- proj3: bfloat16 [512, 512], replicated, may hold values from -0.25 to 0.25
Outputs:
- merged_out: bfloat16 [224, 112, 512], P(('groups', 'rows'), 'cols'), parts along dimension 0
- tokens_grad: bfloat16 [448, 224, 256], P(('groups', 'rows'), 'cols'), parts along dimension 0
- gain_grads: float32 [3584], P('groups'), parts along dimension 0
- qkv2_grad: bfloat16 [393216], P(('groups', 'rows', 'cols')), parts along dimension 0
- proj2_grad: bfloat16 [131072], P(('groups', 'rows', 'cols')), parts along dimension 0
- merge_grad: bfloat16 [1048576], P(('groups', 'rows', 'cols')), parts along dimension 0
- qkv3_grad: bfloat16 [1572864], P(('groups', 'rows', 'cols')), parts along dimension 0
- proj3_grad: bfloat16 [524288], P(('groups', 'rows', 'cols')), parts along dimension 0
There are 2 independent parts, one for each index of `groups`. A program takes and returns all parts, laid end to end along the dimension named above; an argument that names none is the same for every part. Nothing has to cross between parts.
All inputs are finite; a program needn't handle non-finite values.
Results may differ from a plain program's by a relative error of at most 0.033.
Values may be sent and summed in bfloat16 or wider, within the bound.
No kernel may reach another device: no remote copies, remote signals or barrier semaphores. Data moves between devices by JAX's collectives and lax.ppermute only.
A program may use at most 128 MiB of HBM per device.

v0:
```python
import jax
import jax.numpy as jnp
from jax import lax
from jax.experimental import pallas as pl
from jax.experimental.pallas import tpu as pltpu
from jax.sharding import Mesh
from jax.sharding import PartitionSpec as P


WIN = 7
AREA = WIN * WIN
SLOT = 64
PAIR = 2 * SLOT
TILE = 128
HEAD = 32
EDGE = WIN - 1
COLS = ("cols_0", "cols_1")
ROWS_COLS = ("rows", "cols_0", "cols_1")
GROUPS_ROWS_COLS = ("groups", "rows", "cols_0", "cols_1")

EPSILON = 1e-05
MASKED = -100.0
APART = -1e30
BF = jnp.bfloat16
F32 = jnp.float32


def up16(count):
    return -(-count // 16) * 16


def mm(a, b):
    return lax.dot_general(a, b, (((1,), (0,)), ((), ())), preferred_element_type=F32)


def mm_nt(a, b):
    return lax.dot_general(a, b, (((1,), (1,)), ((), ())), preferred_element_type=F32)


def mm_tn(a, b):
    return lax.dot_general(a, b, (((0,), (0,)), ((), ())), preferred_element_type=F32)


def pick(selection, source):
    return mm(selection, source).astype(BF)


def norm_parts(values):
    centred = values - jnp.mean(values, axis=-1, keepdims=True)
    spread = jnp.mean(centred * centred, axis=-1, keepdims=True)
    scale = lax.rsqrt(spread + EPSILON)
    return centred * scale, scale


def normed(values, gain):
    return (norm_parts(values)[0] * gain).astype(BF)


def norm_back(values, gain, upstream):
    unit, scale = norm_parts(values)
    inner = upstream * gain
    along = jnp.mean(inner * unit, axis=-1, keepdims=True)
    grad = scale * (inner - jnp.mean(inner, axis=-1, keepdims=True) - unit * along)
    return grad.astype(BF), jnp.sum(upstream * unit, axis=0, keepdims=True)


def lane_head(shape):
    return lax.broadcasted_iota(jnp.int32, shape, 1) // HEAD


def stacked(block):
    heads = lane_head((1, TILE))
    parts = [block * (heads == h).astype(F32).astype(BF) for h in range(TILE // HEAD)]
    return jnp.concatenate(parts, axis=0)


def unstacked(tall):
    heads = lane_head((PAIR, TILE))
    out = tall[:PAIR]
    for h in range(1, TILE // HEAD):
        out = jnp.where(heads == h, tall[h * PAIR : (h + 1) * PAIR], out)
    return out


def soft(queries, keys, bias):
    tall = stacked(queries)
    raised = jnp.exp(mm_nt(tall, keys) * HEAD ** (-0.5) + bias)
    return tall, raised / jnp.sum(raised, axis=-1, keepdims=True)


def tiled_bias(bias):
    return jnp.concatenate([bias] * (TILE // HEAD), axis=0)


def thirds(packed, rows, width, t):
    return (packed[rows, p * width + t * TILE : p * width + (t + 1) * TILE] for p in range(3))


def head_grads(tall, share, above, k, v):
    d_share = mm_nt(above, v).astype(BF).astype(F32)
    along = jnp.sum(d_share * share, axis=-1, keepdims=True)
    d_scores = (share * (d_share - along) * HEAD ** (-0.5)).astype(BF)
    return (
        unstacked(mm(d_scores, k)),
        mm_tn(d_scores, tall),
        mm_tn(share.astype(BF), above),
    )


def put_thirds(out, rows, width, t, grads):
    for p, grad in enumerate(grads):
        at = p * width + t * TILE
        out[rows, at : at + TILE] = grad.astype(BF)


def put_pieces(grad, outs, block, lanes, halves=1):
    cores, xs = len(outs), outs[0].shape[0]
    size = grad.shape[0] // (cores * xs * halves)
    width = grad.shape[1]
    for h in range(halves):
        for c in range(cores):
            for x in range(xs):
                at = ((h * cores + c) * xs + x) * size
                lo = lanes + h * width
                outs[c][x, block * size : (block + 1) * size, lo : lo + width] = grad[
                    at : at + size
                ].astype(BF)


def weight_grad(acts, order, upstream, out, lanes, halves=1):
    side = order.shape[0]
    for block in range(acts.shape[1] // side):
        moved = pick_cols(acts[:, block * side : (block + 1) * side], order)
        put_pieces(mm_tn(moved, upstream), out, block, lanes, halves)


def pick_cols(acts, order):
    return mm(acts, order).astype(BF)


def put_edges(values, edges, outs):
    sent = pick(edges, values)
    at = 0
    for out in outs:
        out[...] = sent[at : at + out.shape[0]]
        at += out.shape[0]


def joined(refs):
    return jnp.concatenate([r[...] for r in refs], axis=0)


def div(value, by):
    return (value * (-(-65536 // by))) >> 16


def mod(value, by):
    return value - div(value, by) * by


def lines(count, at=0):
    return lax.broadcasted_iota(jnp.int32, (count, 1), 0) + at


def one_hot(wanted, width):
    return (wanted == lax.broadcasted_iota(jnp.int32, (wanted.shape[0], width), 1)).astype(F32).astype(BF)


def strip(p, height, breadth, place, row0=0, col0=0):
    r, c = div(p, breadth), mod(p, breadth)
    return jnp.where(p < height * breadth, place(r + row0, c + col0), -1)


def input_edges(tokens, cot, tokens_o, cot_o, t0, t1, t2, c0, c1, c2):
    for source, laid, rows_o, cols_o, corner_o in (
        (tokens, tokens_o, t0, t1, t2),
        (cot, cot_o, c0, c1, c2),
    ):
        rows, cols, width = source.shape
        pad = laid.shape[0] // rows
        blank = jnp.zeros((pad - cols, width), BF)
        parts = []
        for r in range(rows):
            parts += [source[r].astype(F32), blank.astype(F32)]
        whole = jnp.concatenate(parts, axis=0).astype(BF)
        laid[...] = whole
        rows_o[...] = whole[: EDGE * pad]

        def place(r, c, pad=pad):
            return r * pad + c

        for out, height in ((cols_o, rows), (corner_o, EDGE)):
            wanted = strip(lines(out.shape[0]), height, EDGE, place)
            out[...] = pick(one_hot(wanted, whole.shape[0]), whole)


def make_tables(tile, tile3, ranks, depths):
    tile_rows, tile_cols = tile
    three_rows, three_cols = tile3
    pad, pad3 = up16(tile_cols), up16(three_cols)
    size3 = three_rows * pad3
    line2, line3 = tile_cols // WIN, three_cols // WIN
    count2 = line2 * (tile_rows // WIN)
    count3 = line3 * (three_rows // WIN)
    er, ec, ex = up16(EDGE * tile_cols), up16(tile_rows * EDGE), up16(EDGE * EDGE)
    tr, hc = up16(EDGE * three_cols), up16(three_rows * EDGE)
    hr = EDGE * pad3
    main_n, rows_n = tile_rows * pad, EDGE * pad
    n2, n3, n4 = count2 * SLOT, count3 * SLOT, 4 * size3
    rows, xs, cores = ranks

    def window_line(p, line):
        w, t = div(p, SLOT), mod(p, SLOT)
        row = div(w, line) * WIN + div(t, WIN)
        col = mod(w, line) * WIN + mod(t, WIN)
        return t < AREA, row, col

    def window_place(row, col, line):
        w = div(row, WIN) * line + div(col, WIN)
        return w * SLOT + mod(row, WIN) * WIN + mod(col, WIN)

    def in_windows2(r, c):
        return window_place(r, c, line2)

    def in_windows3(r, c):
        return window_place(r, c, line3)

    def in_planes(r, c):
        return (mod(c, 2) * 2 + mod(r, 2)) * size3 + div(r, 2) * pad3 + div(c, 2)

    def pick4(low, right, main, strip_rows, strip_cols, corner):
        return jnp.where(low, jnp.where(right, corner, strip_rows), jnp.where(right, strip_cols, main))

    def ahead(p, line, extent, shifts, place, main, breadth, strip_rows, strip_cols):
        valid, row, col = window_line(p, line)
        r, c = row + shifts[0], col + shifts[1]
        a, b = r - extent[0], c - extent[1]
        at = pick4(
            a >= 0,
            b >= 0,
            place(r, c),
            main + a * breadth + c,
            main + strip_rows + r * EDGE + b,
            main + strip_rows + strip_cols + a * EDGE + b,
        )
        return jnp.where(valid, at, -1)

    def behind(real, r, c, place, main, extent, strip_rows, strip_cols):
        at = pick4(
            r < 0,
            c < 0,
            place(jnp.maximum(r, 0), jnp.maximum(c, 0)),
            main + (r + EDGE) * extent[1] + c,
            main + strip_rows + r * EDGE + c + EDGE,
            main + strip_rows + strip_cols + (r + EDGE) * EDGE + c + EDGE,
        )
        return jnp.where(real, at, -1)

    def edges(p, place, extent, first, sizes):
        h = strip(p, EDGE, extent[1], place, first[0], 0)
        v = strip(p - sizes[0], extent[0], EDGE, place, 0, first[1])
        x = strip(p - sizes[0] - sizes[1], EDGE, EDGE, place, first[0], first[1])
        return jnp.where(p < sizes[0], h, jnp.where(p < sizes[0] + sizes[1], v, x))

    def grid_of(q):
        k, m = div(q, size3), mod(q, size3)
        a, b = div(m, pad3), mod(m, pad3)
        return b < three_cols, 2 * a + mod(k, 2), 2 * b + div(k, 2)

    def body(
        offsets, where, sel_a, tail2, sel_tokens, sel_b, head3, sel3, tail3, sel3b, head2, sel_e,
        sel_out, order2, order3, order_m, bias2, bias3,
    ):
        s0, s1, s2, s3 = (offsets[i] for i in range(4))
        row_rank, x_rank, c_rank = (where[i] for i in range(3))
        col_rank = x_rank * cores + c_rank

        def fill(out, wanted_of, block):
            def step(i, carry):
                at = pl.multiple_of(i * block, block)
                out[pl.ds(at, block), :] = one_hot(wanted_of(lines(block, at)), out.shape[1])
                return carry

            lax.fori_loop(0, out.shape[0] // block, step, 0)

        def in_pad(r, c):
            return r * pad + c

        def in_pad3(r, c):
            return r * pad3 + c

        fill(
            sel_a,
            lambda p: ahead(p, line2, tile, (s0, s1), in_pad, main_n, pad, rows_n, ec),
            64,
        )
        fill(
            tail2,
            lambda p: edges(p, in_windows2, tile, (tile_rows - EDGE, tile_cols - EDGE), (er, ec)),
            64,
        )

        def from_grid(q):
            real, r, c = grid_of(q)
            return jnp.where(real, in_pad(r, c), -1)

        fill(sel_tokens, from_grid, 64)

        def back2(q):
            real, r, c = grid_of(q)
            return behind(real, r - s0, c - s1, in_windows2, n2, tile, er, ec)

        fill(sel_b, back2, 64)

        def head_of_three(p):
            v = strip(p - hr, three_rows, EDGE, in_pad3)
            x = strip(p - hr - hc, EDGE, EDGE, in_pad3)
            return jnp.where(p < hr, p, jnp.where(p < hr + hc, v, x))

        fill(head3, head_of_three, 16)
        fill(
            sel3,
            lambda p: ahead(p, line3, tile3, (s2, s3), in_pad3, size3, pad3, hr, hc),
            64,
        )
        fill(
            tail3,
            lambda p: edges(
                p, in_windows3, tile3, (three_rows - EDGE, three_cols - EDGE), (tr, hc)
            ),
            16,
        )

        def back3(m):
            a, b = div(m, pad3), mod(m, pad3)
            return behind(b < three_cols, a - s2, b - s3, in_windows3, n3, tile3, tr, hc)

        fill(sel3b, back3, 16)
        fill(head2, lambda p: edges(p, in_planes, tile, (0, 0), (er, ec)), 64)
        fill(
            sel_e,
            lambda p: ahead(p, line2, tile, (s0, s1), in_planes, n4, tile_cols, er, ec),
            64,
        )

        def to_grid(g):
            return jnp.where(mod(g, pad) < tile_cols, in_planes(div(g, pad), mod(g, pad)), -1)

        fill(sel_out, to_grid, 64)

        for out, depth, halves in ((order2, depths[0], 1), (order3, depths[1], 1), (order_m, depths[2], 2)):
            side = out.shape[0]
            per_row = depth // rows
            near = side // per_row
            sub = depth // (rows * xs * cores)
            part = sub // halves
            at = lax.broadcasted_iota(jnp.int32, (1, side), 1)
            r = mod(div(at, part), near)
            x = mod(div(at, part * near) + x_rank, xs)
            c = mod(div(at, part * near * xs) + 1 + c_rank, cores)
            h = div(at, part * near * xs * cores)
            source = r * per_row + (x * cores + c) * sub + h * part + mod(at, part)
            lanes = lax.broadcasted_iota(jnp.int32, (side, side), 0)
            out[...] = (lanes == source).astype(F32).astype(BF)

        def label(at, extent, shift):
            return jnp.where(at < extent - WIN, 0, jnp.where(at < extent - shift, 1, 2))

        def marks(p, line, extent, shifts):
            valid, row, col = window_line(p, line)
            r = label(row + row_rank * extent[0], extent[0] * rows, shifts[0])
            c = label(col + col_rank * extent[1], extent[1] * xs * cores, shifts[1])
            near = div(p, SLOT) * 2 + jnp.where(valid, 1, 0)
            return near, jnp.where(valid, r * 3 + c, -1)

        def bias(first, line, extent, shifts):
            near_p, mark_p = marks(lines(PAIR, first), line, extent, shifts)
            across = lax.broadcasted_iota(jnp.int32, (1, PAIR), 1) + first
            near_q, mark_q = marks(across, line, extent, shifts)
            same = jnp.where(mark_p == mark_q, 0.0, MASKED)
            return jnp.where(near_p == near_q, same, APART).astype(F32)

        for g in range(bias2.shape[0]):
            bias2[g] = bias(g * PAIR, line2, tile, (s0, s1))
        bias3[...] = bias(0, line3, tile3, (s2, s3))

    shapes = [
        ((n2, main_n + rows_n + ec + ex), BF),
        ((er + ec + ex, n2), BF),
        ((n4, main_n), BF),
        ((n4, n2 + er + ec + ex), BF),
        ((hr + hc + ex, size3), BF),
        ((n3, size3 + hr + hc + ex), BF),
        ((tr + hc + ex, n3), BF),
        ((size3, n3 + tr + hc + ex), BF),
        ((er + ec + ex, n4), BF),
        ((n2, n4 + er + ec + ex), BF),
        ((main_n, n4), BF),
        ((256, 256), BF),
        ((256, 256), BF),
        ((256, 256), BF),
        ((n2 // PAIR, PAIR, PAIR), F32),
        ((PAIR, PAIR), F32),
    ]
    return body, shapes


def two_forward(
    t0, t1, t2, t3, gain, qkv, proj, sel, bias, edges, rolled_o, packed_o, mixed_o, wins_o, e0, e1, e2
):
    tokens = pick(sel[...], joined((t0, t1, t2, t3)))
    rolled = normed(tokens.astype(F32), gain[...])
    rolled_o[...] = rolled
    packed_o[...] = mm(rolled, qkv[...]).astype(BF)
    width = rolled.shape[1]
    for g in range(packed_o.shape[0] // PAIR):
        rows = slice(g * PAIR, (g + 1) * PAIR)
        mask = tiled_bias(bias[g])
        for t in range(width // TILE):
            q, k, v = thirds(packed_o, rows, width, t)
            share = soft(q, k, mask)[1].astype(BF)
            mixed_o[rows, t * TILE : (t + 1) * TILE] = unstacked(mm(share, v)).astype(BF)
    projected = mm(mixed_o[...], proj[...]).astype(BF)
    wins_o[...] = projected
    put_edges(projected, edges[...], (e0, e1, e2))


def merge_forward(
    tokens, w0, w1, w2, w3, sel_tokens, sel_back, gain, weight, gain3, edges,
    two_o, tokens_o, norm_o, merged_o, normed_o, e0, e1, e2,
):
    laid = pick(sel_tokens[...], tokens[...])
    back = pick(sel_back[...], joined((w0, w1, w2, w3)))
    two = (laid.astype(F32) + back.astype(F32)).astype(BF)
    tokens_o[...] = laid
    size = two.shape[0] // 4
    wide = jnp.concatenate([two[k * size : (k + 1) * size] for k in range(4)], axis=1)
    two_o[...] = wide
    merged_norm = normed(wide.astype(F32), gain[...])
    norm_o[...] = merged_norm
    merged = mm(merged_norm, weight[...]).astype(BF)
    merged_o[...] = merged
    three = normed(merged.astype(F32), gain3[...])
    normed_o[...] = three
    put_edges(three, edges[...], (e0, e1, e2))


def three_both(
    n0, n1, n2, n3, c0, c1, c2, c3, qkv, proj, sel, bias, edges,
    both_o, rolled_o, above_o, mixed, d_packed, e0, e1, e2, packed,
):
    rolled = pick(sel[...], joined((n0, n1, n2, n3)))
    above = pick(sel[...], joined((c0, c1, c2, c3)))
    rolled_o[...] = rolled
    above_o[...] = above
    width = rolled.shape[1]
    packed[...] = mm(rolled, qkv[...]).astype(BF)
    d_mixed = mm_nt(above, proj[...]).astype(BF)
    mask = tiled_bias(bias[...])
    rows = slice(0, PAIR)
    for t in range(width // TILE):
        lanes = slice(t * TILE, (t + 1) * TILE)
        q, k, v = thirds(packed, rows, width, t)
        tall, share = soft(q, k, mask)
        mixed[:, lanes] = unstacked(mm(share.astype(BF), v)).astype(BF)
        put_thirds(
            d_packed, rows, width, t, head_grads(tall, share, stacked(d_mixed[:, lanes]), k, v)
        )
    projected = mm(mixed[...], proj[...]).astype(BF)
    d_rolled = mm_nt(d_packed[...], qkv[...]).astype(BF)
    both = jnp.concatenate([projected, d_rolled], axis=1)
    both_o[...] = both
    put_edges(both, edges[...], (e0, e1, e2))


def three_grads(rolled, above, mixed, d_packed, order, send_o, keep_o):
    outs = (send_o, keep_o)
    weight_grad(rolled[...], order[...], d_packed[...], outs, 0)
    weight_grad(mixed[...], order[...], above[...], outs, 3 * rolled.shape[1])


def merge_backward(
    b0, b1, b2, b3, merged, cot, two, sel_back, gain3, gain, weight, edges,
    out_o, d_two_o, d_rows_o, gm_o, g3_o, e0, e1, e2,
):
    back = pick(sel_back[...], joined((b0, b1, b2, b3)))
    width = merged.shape[1]
    base = merged[...].astype(F32)
    out = base + back[:, :width].astype(F32)
    rows, cols = out_o.shape[:2]
    pad = out.shape[0] // rows
    for r in range(rows):
        out_o[r] = out[r * pad : r * pad + cols].astype(BF)
    d_normed = back[:, width:].astype(F32)
    d_merged, g3 = norm_back(base, gain3[...], d_normed)
    g3_o[...] = g3
    d_rows = (cot[...].astype(F32) + d_merged.astype(F32)).astype(BF)
    d_rows_o[...] = d_rows
    d_norm = mm_nt(d_rows, weight[...]).astype(BF).astype(F32)
    d_wide, gm = norm_back(two[...].astype(F32), gain[...], d_norm)
    gm_o[...] = gm
    quarter = d_wide.shape[1] // 4
    d_two = jnp.concatenate([d_wide[:, k * quarter : (k + 1) * quarter] for k in range(4)], axis=0)
    d_two_o[...] = d_two
    put_edges(d_two, edges[...], (e0, e1, e2))


def merge_grads(norm, d_rows, order, send_o, keep_o):
    weight_grad(norm[...], order[...], d_rows[...], (send_o, keep_o), 0, halves=2)


def two_backward(
    d0, d1, d2, d3, mixed, packed, rolled, qkv, proj, gain, sel, bias, edges, order, gm, g3,
    wins_o, send_o, keep_o, e0, e1, e2, d_packed, d_mixed,
):
    above = pick(sel[...], joined((d0, d1, d2, d3)))
    width = above.shape[1]
    d_mixed[...] = mm_nt(above, proj[...]).astype(BF)

    def step(g, carry):
        rows = pl.ds(pl.multiple_of(g * PAIR, PAIR), PAIR)
        mask = tiled_bias(bias[g])
        for t in range(width // TILE):
            q, k, v = thirds(packed, rows, width, t)
            tall, share = soft(q, k, mask)
            given = stacked(d_mixed[rows, t * TILE : (t + 1) * TILE])
            put_thirds(d_packed, rows, width, t, head_grads(tall, share, given, k, v))
        return carry

    lax.fori_loop(0, packed.shape[0] // PAIR, step, 0)
    d_rolled = mm_nt(d_packed[...], qkv[...]).astype(BF)
    wins_o[...] = d_rolled
    put_edges(d_rolled, edges[...], (e0, e1, e2))
    outs = (send_o, keep_o)
    weight_grad(rolled[...], order[...], d_packed[...], outs, 0)
    weight_grad(mixed[...], order[...], above, outs, 3 * width)
    g2 = jnp.sum(d_rolled.astype(F32) * rolled[...].astype(F32), axis=0, keepdims=True) / gain[...]
    blank = jnp.zeros((1, width), F32)
    second = jnp.concatenate([g3[...], g2, blank], axis=1)
    line = lax.broadcasted_iota(jnp.int32, (16, 4 * width), 0)
    gains = jnp.where(line == 0, gm[...], jnp.where(line == 1, second, 0.0)).astype(BF)
    for out in outs:
        xs, rows = out.shape[:2]
        for x in range(xs):
            out[x, rows - 16 :, :] = gains


def tokens_backward(w0, w1, w2, w3, tokens, d_two, gain, sel_back, sel_out, out_o):
    d_normed = pick(sel_back[...], joined((w0, w1, w2, w3)))
    d_norm, _ = norm_back(tokens[...].astype(F32), gain[...], d_normed.astype(F32))
    total = (d_two[...].astype(F32) + d_norm.astype(F32)).astype(BF)
    laid = pick(sel_out[...], total)
    rows, cols = out_o.shape[:2]
    pad = laid.shape[0] // rows
    for r in range(rows):
        out_o[r] = laid[r * pad : r * pad + cols]


def pair_sum(keep, got, *outs):
    for x, out in enumerate(outs):
        out[...] = (keep[x].astype(F32) + got[x].astype(F32)).astype(BF)


def line_added(parts):
    parts = [p[...].astype(F32) for p in parts]
    while len(parts) > 1:
        half = len(parts) // 2
        parts = [parts[j] + parts[j + half] for j in range(half)]
    return parts[0]


def put_blocks(value, out, at):
    rows, sub = out.shape[:2]
    for r in range(rows):
        out[r, :, at : at + value.shape[1]] = value[r * sub : (r + 1) * sub].astype(BF)


def line_sum(*refs):
    *held, out = refs
    put_blocks(line_added(held), out, 0)


def line_sum_late(*refs):
    *held, out = refs
    count = len(held) // 2
    rows, sub = out.shape[:2]
    first = line_added(held[:count])
    second = line_added(held[count:]).astype(BF)
    share = second.shape[0] - 16
    part = share // rows
    p = lines(rows * sub)
    r, j = div(p, sub), mod(p, sub)
    wanted = jnp.where(j < part, r * part + j, share + j - part)
    put_blocks(first, out, 0)
    put_blocks(mm(one_hot(wanted, second.shape[0]), second), out, first.shape[1])


def call(body, outs, args, flops, scratch=(), scalars=0):
    smem, vmem = (pl.BlockSpec(memory_space=m) for m in (pltpu.SMEM, pltpu.VMEM))
    return pl.pallas_call(
        body,
        in_specs=[smem] * scalars + [vmem] * (len(args) - scalars),
        out_shape=[jax.ShapeDtypeStruct(shape, kind) for shape, kind in outs],
        scratch_shapes=[pltpu.VMEM(shape, kind) for shape, kind in scratch],
        cost_estimate=pl.CostEstimate(flops=flops, transcendentals=0, bytes_accessed=4 << 20),
        compiler_params=pltpu.CompilerParams(vmem_limit_bytes=8 << 20),
    )(*args)


def moved(value, axis, by):
    count = lax.axis_size(axis)
    return lax.ppermute(value, axis, [(i, (i + by) % count) for i in range(count)])


def moved_across(value, by):
    rows, cols = lax.axis_size("rows"), lax.axis_size(COLS)
    pairs = [
        (i * cols + j, ((i + by) % rows) * cols + (j + by) % cols)
        for i in range(rows)
        for j in range(cols)
    ]
    return lax.ppermute(value, ROWS_COLS, pairs)


def to_neighbours(pieces, by):
    rows, cols, corner = pieces
    return moved_across(corner, by), moved(rows, "rows", by), moved(cols, COLS, by)


def exchanged(pieces, by):
    corner, rows, cols = to_neighbours(pieces, by)
    return rows, cols, corner


def core_sum(send, keep):
    got = moved(send, "cols_1", 1)
    shape = (keep.shape[1:], BF)
    return call(pair_sum, [shape] * keep.shape[0], (keep, got), 1 << 26)


def line_parts(blocks):
    return [blocks[0]] + [moved(blocks[j], "cols_0", j) for j in range(1, len(blocks))]


def spread_sum(body, held, shape):
    (blocks,) = call(body, [(shape, BF)], held, 1 << 26)
    spread = lax.all_to_all(blocks, "rows", 0, 0)
    return jnp.sum(spread.astype(F32), axis=0)


def on_device(
    tokens,
    cotangent,
    shift_offsets,
    norm2_gain,
    qkv2,
    proj2,
    merge_gain,
    merge_weight,
    norm3_gain,
    qkv3,
    proj3,
):
    tile_rows, tile_cols, narrow = tokens.shape
    three_rows, three_cols, wide = cotangent.shape
    ranks = tuple(lax.axis_size(a) for a in ROWS_COLS)
    rows, xs, cores = ranks
    pad, pad3 = up16(tile_cols), up16(three_cols)
    size3 = three_rows * pad3
    n2 = (tile_rows // WIN) * (tile_cols // WIN) * SLOT
    n3 = (three_rows // WIN) * (three_cols // WIN) * SLOT
    n4 = 4 * size3
    er, ec, ex = up16(EDGE * tile_cols), up16(tile_rows * EDGE), up16(EDGE * EDGE)
    hr, tr, hc = EDGE * pad3, up16(EDGE * three_cols), up16(three_rows * EDGE)
    gain2, gain_m, gain3 = norm2_gain[None], merge_gain[None], norm3_gain[None]

    tokens_p, cot_p, *pieces = call(
        input_edges,
        [
            ((tile_rows * pad, narrow), BF),
            ((size3, wide), BF),
            ((EDGE * pad, narrow), BF),
            ((ec, narrow), BF),
            ((ex, narrow), BF),
            ((hr, wide), BF),
            ((hc, wide), BF),
            ((ex, wide), BF),
        ],
        (tokens, cotangent),
        1 << 28,
    )
    token_pieces = exchanged(pieces[:3], -1)
    cot_pieces = exchanged(pieces[3:], -1)
    where = jnp.stack([lax.axis_index(a) for a in ROWS_COLS]).astype(jnp.int32)
    tables, shapes = make_tables(
        (tile_rows, tile_cols), (three_rows, three_cols), ranks, (narrow, wide, 4 * narrow)
    )
    (
        sel_a, tail2, sel_tokens, sel_b, head3, sel3, tail3, sel3b, head2, sel_e, sel_out,
        order2, order3, order_m, bias2, bias3,
    ) = call(tables, shapes, (shift_offsets, where), 1 << 28, scalars=2)

    rolled, packed, mixed, wins, *edges = call(
        two_forward,
        [
            ((n2, narrow), BF),
            ((n2, 3 * narrow), BF),
            ((n2, narrow), BF),
            ((n2, narrow), BF),
            ((er, narrow), BF),
            ((ec, narrow), BF),
            ((ex, narrow), BF),
        ],
        (tokens_p, *token_pieces, gain2, qkv2, proj2, sel_a, bias2, tail2),
        1 << 30,
    )
    back = exchanged(edges, 1)
    two, tokens_q, merged_norm, merged, normed3, *edges = call(
        merge_forward,
        [
            ((size3, 4 * narrow), BF),
            ((n4, narrow), BF),
            ((size3, 4 * narrow), BF),
            ((size3, wide), BF),
            ((size3, wide), BF),
            ((hr, wide), BF),
            ((hc, wide), BF),
            ((ex, wide), BF),
        ],
        (tokens_p, wins, *back, sel_tokens, sel_b, gain_m, merge_weight, gain3, head3),
        1 << 30,
    )
    ahead = exchanged(edges, -1)
    both, rolled3, above3, mixed3, d_packed3, *edges = call(
        three_both,
        [
            ((n3, 2 * wide), BF),
            ((n3, wide), BF),
            ((n3, wide), BF),
            ((n3, wide), BF),
            ((n3, 3 * wide), BF),
            ((tr, 2 * wide), BF),
            ((hc, 2 * wide), BF),
            ((ex, 2 * wide), BF),
        ],
        (normed3, *ahead, cot_p, *cot_pieces, qkv3, proj3, sel3, bias3, tail3),
        1 << 30,
        scratch=[((n3, 3 * wide), BF)],
    )
    back = exchanged(edges, 1)
    share3 = wide // (xs * cores)
    send, keep = call(
        three_grads,
        [((xs, share3, 4 * wide), BF)] * 2,
        (rolled3, above3, mixed3, d_packed3, order3),
        1 << 30,
    )
    sum_a = core_sum(send, keep)
    merged_out, d_two, d_rows, grad_m, grad_3, *edges = call(
        merge_backward,
        [
            ((three_rows, three_cols, wide), BF),
            ((n4, narrow), BF),
            ((size3, wide), BF),
            ((1, 4 * narrow), F32),
            ((1, wide), F32),
            ((er, narrow), BF),
            ((ec, narrow), BF),
            ((ex, narrow), BF),
        ],
        (both, *back, merged, cot_p, two, sel3b, gain3, gain_m, merge_weight, head2),
        1 << 30,
    )
    ahead = exchanged(edges, -1)
    send, keep = call(
        merge_grads, [((xs, share3, 2 * wide), BF)] * 2, (merged_norm, d_rows, order_m), 1 << 30
    )
    sum_b = core_sum(send, keep)
    share2 = narrow // (xs * cores)
    wins, send, keep, *edges = call(
        two_backward,
        [
            ((n2, narrow), BF),
            ((xs, share2 + 16, 4 * narrow), BF),
            ((xs, share2 + 16, 4 * narrow), BF),
            ((er, narrow), BF),
            ((ec, narrow), BF),
            ((ex, narrow), BF),
        ],
        (
            d_two, *ahead, mixed, packed, rolled, qkv2, proj2, gain2, sel_e, bias2, tail2,
            order2, grad_m, grad_3,
        ),
        1 << 30,
        scratch=[((n2, 3 * narrow), BF), ((n2, narrow), BF)],
    )
    back = exchanged(edges, 1)
    sum_c = core_sum(send, keep)
    (tokens_grad,) = call(
        tokens_backward,
        [((tile_rows, tile_cols, narrow), BF)],
        (wins, *back, tokens_q, d_two, gain2, sel_b, sel_out),
        1 << 30,
    )

    sub = wide // (rows * xs * cores)
    early = spread_sum(line_sum, line_parts(sum_a), (rows, sub, 4 * wide))
    late = spread_sum(
        line_sum_late, line_parts(sum_b) + line_parts(sum_c), (rows, sub, 2 * wide + 4 * narrow)
    )
    chunk3 = early.astype(BF)
    merge_chunk = late[:, : 2 * wide].astype(BF)
    late = late[:, 2 * wide :]
    sub2 = narrow // (rows * xs * cores)
    gain_sums = jnp.concatenate(
        [late[sub2 + 1, wide : wide + narrow], late[sub2], late[sub2 + 1, :wide]]
    )
    chunk2 = late[:sub2].astype(BF)
    halves = [merge_chunk[:, h * wide : (h + 1) * wide] for h in range(2)]
    return (
        merged_out,
        tokens_grad,
        gain_sums,
        chunk2[:, : 3 * narrow].reshape(-1),
        chunk2[:, 3 * narrow :].reshape(-1),
        jnp.concatenate(halves, axis=0).reshape(-1),
        chunk3[:, : 3 * wide].reshape(-1),
        chunk3[:, 3 * wide :].reshape(-1),
    )


def solution(mesh):
    cores = 2
    split = Mesh(
        mesh.devices.reshape(
            mesh.shape["groups"], mesh.shape["rows"], mesh.shape["cols"] // cores, cores
        ),
        ("groups", "rows", "cols_0", "cols_1"),
    )
    tiles = P(("groups", "rows"), COLS, None)
    flat = P(GROUPS_ROWS_COLS)


    return jax.shard_map(
        on_device,
        mesh=split,
        in_specs=(tiles, tiles) + (P(),) * 9,
        out_specs=(tiles, tiles, P("groups"), flat, flat, flat, flat, flat),
        check_vma=False,
    )
```

profile of v0, /device:TPU:40, one launch (start us, length us, event | category | flops | bytes accessed | tf_op | source)
XLA Modules:
  0.0 151.3 jit_solution(4211485944548490431)
XLA Ops:
  0.7 1.0 copy-done.4
  1.6 0.9 copy-done.6
  2.5 0.3 shard_map.170
  2.8 24.6 %collective-permute-start.2 = (bf16[48,256]{1,0:T(8,128)(2,1)S(1)}, bf16[48,256]{1,0:T(8,128)(2,1)S(1)}, u32[]{:S(2)}, u32[]{:S(2)}) collective-permute-start(bf16[48,256]{1,0:T(8,128)(2,1)S(1)} %get-tuple-element.88), channel_id=1, source_target_pairs={{0,127},{1,120},{2,121},{3,122},{4,123},{5,124},{6,125},{7,126},{8... | collective-permute-start | bytes 73736 | tf_op jit(solution)/shard_map/ppermute | solution.py:622
  27.4 0.8 collective-permute-start.1
  28.2 0.1 collective-permute-start
  28.4 0.7 copy-done.10
  29.1 5.1 %shard_map.171 = (bf16[512,784]{1,0:T(8,128)(2,1)S(1)}, bf16[320,512]{1,0:T(8,128)(2,1)S(1)}, bf16[448,448]{1,0:T(8,128)(2,1)S(1)}, bf16[448,832]{1,0:T(8,128)(2...) custom-call(s32[4]{0:T(128)S(1)} %copy-done.10, ...), custom_call_target="tpu_custom_call" | custom-call | flops 268435456 | bytes 4194304 | tf_op jit(solution)/shard_map/pallas_call | solution.py:600
  34.1 0.8 copy-done.15
  35.0 2.6 %shard_map.172 = (bf16[512,256]{1,0:T(8,128)(2,1)S(1)}, bf16[512,768]{1,0:T(8,128)(2,1)S(1)}, bf16[512,256]{1,0:T(8,128)(2,1)S(1)}, bf16[512,256]{1,0:T(8,128)(2...) custom-call(bf16[448,256]{1,0:T(8,128)(2,1)S(1)} %get-tuple-element.85.t0.tokens, ...), custom_call_target="tpu_custom_call" | custom-call | flops 1073741824 | bytes 4194304 | tf_op jit(solution)/shard_map/pallas_call | solution.py:600
  37.6 2.0 %collective-permute-start.3 = (bf16[176,256]{1,0:T(8,128)(2,1)S(1)}, bf16[176,256]{1,0:T(8,128)(2,1)S(1)}, u32[]{:S(2)}, u32[]{:S(2)}) collective-permute-start(bf16[176,256]{1,0:T(8,128)(2,1)S(1)} %get-tuple-element.93), channel_id=1, source_target_pairs={{0,8},{8,16},{16,24},{24,32},{32,40},{40,48},{48,56},{56,64},{64,7... | collective-permute-start | bytes 270344 | tf_op jit(solution)/shard_map/ppermute | solution.py:612
  39.6 3.0 %collective-permute-start.10 = (bf16[48,512]{1,0:T(8,128)(2,1)S(1)}, bf16[48,512]{1,0:T(8,128)(2,1)S(1)}, u32[]{:S(2)}, u32[]{:S(2)}) collective-permute-start(bf16[48,512]{1,0:T(8,128)(2,1)S(1)} %get-tuple-element.105), channel_id=1, source_target_pairs={{0,7},{1,0},{2,1},{3,2},{4,3},{5,4},{6,5},{7,6},{8,15},{9,8},{10,9... | collective-permute-start | bytes 147464 | tf_op jit(solution)/shard_map/ppermute | solution.py:612
  42.5 2.7 %collective-permute-start.9 = (bf16[96,512]{1,0:T(8,128)(2,1)S(1)}, bf16[96,512]{1,0:T(8,128)(2,1)S(1)}, u32[]{:S(2)}, u32[]{:S(2)}) collective-permute-start(bf16[96,512]{1,0:T(8,128)(2,1)S(1)} %get-tuple-element.104), channel_id=1, source_target_pairs={{0,120},{8,0},{16,8},{24,16},{32,24},{40,32},{48,40},{56,48},{64,5... | collective-permute-start | bytes 294920 | tf_op jit(solution)/shard_map/ppermute | solution.py:612
  45.2 0.9 collective-permute-done.5.w3
  46.2 1.6 %shard_map.173 = (bf16[112,1024]{1,0:T(8,128)(2,1)S(1)}, bf16[448,256]{1,0:T(8,128)(2,1)S(1)}, bf16[112,1024]{1,0:T(8,128)(2,1)S(1)}, bf16[112,512]{1,0:T(8,128)...) custom-call(bf16[448,256]{1,0:T(8,128)(2,1)S(1)} %get-tuple-element., ...), custom_call_target="tpu_custom_call" | custom-call | flops 1073741824 | bytes 4194304 | tf_op jit(solution)/shard_map/pallas_call | solution.py:600
  47.8 0.7 copy-done.17
  48.6 0.3 collective-permute-start.11
  48.9 0.6 collective-permute-start.7
  49.5 2.7 %collective-permute-done.11.c3 = bf16[48,512]{1,0:T(8,128)(2,1)S(1)} collective-permute-done((bf16[48,512]{1,0:T(8,128)(2,1)S(1)}, bf16[48,512]{1,0:T(8,128)(2,1)S(1)}, u32[]{:S(2)}, u32[]{:S(2)}) %collective-permute-start.11) | collective-permute-done | bytes 49184 | tf_op jit(solution)/shard_map/ppermute | solution.py:622
  52.2 1.3 collective-permute-done.8.n3
  53.5 0.2 collective-permute-done.6.n1
  53.7 3.3 %shard_map.174 = (bf16[128,1024]{1,0:T(8,128)(2,1)S(1)}, bf16[128,512]{1,0:T(8,128)(2,1)S(1)}, bf16[128,512]{1,0:T(8,128)(2,1)S(1)}, bf16[128,512]{1,0:T(8,128)(...) custom-call(bf16[112,512]{1,0:T(8,128)(2,1)S(1)} %get-tuple-element., ...), custom_call_target="tpu_custom_call" | custom-call | flops 1073741824 | bytes 4194304 | tf_op jit(solution)/shard_map/pallas_call | solution.py:600
  57.1 1.8 %collective-permute-start.12 = (bf16[96,1024]{1,0:T(8,128)(2,1)S(1)}, bf16[96,1024]{1,0:T(8,128)(2,1)S(1)}, u32[]{:S(2)}, u32[]{:S(2)}) collective-permute-start(bf16[96,1024]{1,0:T(8,128)(2,1)S(1)} %get-tuple-element.111), channel_id=1, source_target_pairs={{0,8},{8,16},{16,24},{24,32},{32,40},{40,48},{48,56},{56,64},{64,7... | collective-permute-start | bytes 589832 | tf_op jit(solution)/shard_map/ppermute | solution.py:612
  58.9 2.2 %collective-permute-start.14 = (bf16[48,1024]{1,0:T(8,128)(2,1)S(1)}, bf16[48,1024]{1,0:T(8,128)(2,1)S(1)}, u32[]{:S(2)}, u32[]{:S(2)}) collective-permute-start(bf16[48,1024]{1,0:T(8,128)(2,1)S(1)} %get-tuple-element.113), channel_id=1, source_target_pairs={{0,9},{1,10},{2,11},{3,12},{4,13},{5,14},{6,15},{7,8},{8,17},{9,18... | collective-permute-start | bytes 294920 | tf_op jit(solution)/shard_map/ppermute | solution.py:622
  61.1 3.0 %collective-permute-done.13.b2 = bf16[48,1024]{1,0:T(8,128)(2,1)S(1)} collective-permute-done((bf16[48,1024]{1,0:T(8,128)(2,1)S(1)}, bf16[48,1024]{1,0:T(8,128)(2,1)S(1)}, u32[]{:S(2)}, u32[]{:S(2)}) %collective-permute-start.13) | collective-permute-done | bytes 98336 | tf_op jit(solution)/shard_map/ppermute | solution.py:612
  64.1 5.8 %collective-permute-done.14.b3 = bf16[48,1024]{1,0:T(8,128)(2,1)S(1)} collective-permute-done((bf16[48,1024]{1,0:T(8,128)(2,1)S(1)}, bf16[48,1024]{1,0:T(8,128)(2,1)S(1)}, u32[]{:S(2)}, u32[]{:S(2)}) %collective-permute-start.14) | collective-permute-done | bytes 98336 | tf_op jit(solution)/shard_map/ppermute | solution.py:622
  69.9 1.3 shard_map.175
  71.3 0.5 collective-permute-start.15
  71.8 1.2 shard_map.178
  73.0 0.2 collective-permute-start.21
  73.2 1.3 collective-permute-done.17.d3
  74.5 1.9 %collective-permute-done.15.d1 = bf16[176,256]{1,0:T(8,128)(2,1)S(1)} collective-permute-done((bf16[176,256]{1,0:T(8,128)(2,1)S(1)}, bf16[176,256]{1,0:T(8,128)(2,1)S(1)}, u32[]{:S(2)}, u32[]{:S(2)}) %collective-permute-start.15) | collective-permute-done | bytes 90144 | tf_op jit(solution)/shard_map/ppermute | solution.py:612
  76.4 6.4 %shard_map.176 = (bf16[512,256]{1,0:T(8,128)(2,1)S(1)}, bf16[4,48,1024]{2,1,0:T(8,128)(2,1)S(1)}, bf16[4,48,1024]{2,1,0:T(8,128)(2,1)S(1)}, bf16[176,256]{1,0:T(...) custom-call(bf16[448,256]{1,0:T(8,128)(2,1)S(1)} %get-tuple-element.119.d0.d_two, ...), custom_call_target="tpu_custom_call" | custom-call | flops 1073741824 | bytes 4194304 | tf_op jit(solution)/shard_map/pallas_call | solution.py:600
  82.9 1.5 shard_map.182
  84.5 0.8 collective-permute-start.29
  85.4 1.6 %collective-permute-start.26 = (bf16[48,1024]{1,0:T(8,128)(2,1)S(1)}, bf16[48,1024]{1,0:T(8,128)(2,1)S(1)}, u32[]{:S(2)}, u32[]{:S(2)}) collective-permute-start(bf16[48,1024]{1,0:T(8,128)(2,1)S(1)} %get-tuple-element.148), channel_id=1, source_target_pairs={{0,2},{2,4},{4,6},{6,0},{1,3},{3,5},{5,7},{7,1},{8,10},{10,12},{12... | collective-permute-start | bytes 294920 | tf_op jit(solution)/shard_map/ppermute | solution.py:612
  87.1 2.8 %collective-permute-start.22 = (bf16[64,1024]{1,0:T(8,128)(2,1)S(1)}, bf16[64,1024]{1,0:T(8,128)(2,1)S(1)}, u32[]{:S(2)}, u32[]{:S(2)}) collective-permute-start(bf16[64,1024]{1,0:T(8,128)(2,1)S(1)} %get-tuple-element.142), channel_id=1, source_target_pairs={{0,2},{2,4},{4,6},{6,0},{1,3},{3,5},{5,7},{7,1},{8,10},{10,12},{12... | collective-permute-start | bytes 393224 | tf_op jit(solution)/shard_map/ppermute | solution.py:612
  89.8 1.6 %collective-permute-start.23 = (bf16[64,1024]{1,0:T(8,128)(2,1)S(1)}, bf16[64,1024]{1,0:T(8,128)(2,1)S(1)}, u32[]{:S(2)}, u32[]{:S(2)}) collective-permute-start(bf16[64,1024]{1,0:T(8,128)(2,1)S(1)} %get-tuple-element.143), channel_id=1, source_target_pairs={{0,4},{2,6},{4,0},{6,2},{1,5},{3,7},{5,1},{7,3},{8,12},{10,14},{12... | collective-permute-start | bytes 393224 | tf_op jit(solution)/shard_map/ppermute | solution.py:612
  91.5 2.8 %collective-permute-done.26.refs_5_ = bf16[48,1024]{1,0:T(8,128)(2,1)S(1)} collective-permute-done((bf16[48,1024]{1,0:T(8,128)(2,1)S(1)}, bf16[48,1024]{1,0:T(8,128)(2,1)S(1)}, u32[]{:S(2)}, u32[]{:S(2)}) %collective-permute-start.26) | collective-permute-done | bytes 98336 | tf_op jit(solution)/shard_map/ppermute | solution.py:612
  94.3 1.5 collective-permute-start.28
  95.7 4.6 %collective-permute-done.28.refs_7_ = bf16[48,1024]{1,0:T(8,128)(2,1)S(1)} collective-permute-done((bf16[48,1024]{1,0:T(8,128)(2,1)S(1)}, bf16[48,1024]{1,0:T(8,128)(2,1)S(1)}, u32[]{:S(2)}, u32[]{:S(2)}) %collective-permute-start.28) | collective-permute-done | bytes 98336 | tf_op jit(solution)/shard_map/ppermute | solution.py:612
  100.3 1.0 shard_map.181
  101.3 4.6 %all-to-all-start = ((bf16[16,4,2048]{2,1,0:T(4,128)(2,1)}), bf16[16,4,2048]{2,1,0:T(4,128)(2,1)}, u32[]{:S(2)}, u32[]{:S(2)}) async-start(bf16[16,4,2048]{2,1,0:T(4,128)(2,1)} %shard_map.181), calls=%async_computation | async-start | bytes 524288 | tf_op jit(solution)/shard_map/all_to_all | solution.py:647
  105.9 0.2 shard_map.183
  106.2 1.0 collective-permute-start.30
  107.2 2.9 %collective-permute-start.31 = (bf16[64,2048]{1,0:T(8,128)(2,1)S(1)}, bf16[64,2048]{1,0:T(8,128)(2,1)S(1)}, u32[]{:S(2)}, u32[]{:S(2)}) collective-permute-start(bf16[64,2048]{1,0:T(8,128)(2,1)S(1)} %get-tuple-element.160), channel_id=1, source_target_pairs={{0,4},{2,6},{4,0},{6,2},{1,5},{3,7},{5,1},{7,3},{8,12},{10,14},{12... | collective-permute-start | bytes 786440 | tf_op jit(solution)/shard_map/ppermute | solution.py:612
  110.1 0.9 collective-permute-start.32
  111.0 1.4 collective-permute-start.18
  112.4 2.5 %collective-permute-done.30.refs_1_ = bf16[64,2048]{1,0:T(8,128)(2,1)S(1)} collective-permute-done((bf16[64,2048]{1,0:T(8,128)(2,1)S(1)}, bf16[64,2048]{1,0:T(8,128)(2,1)S(1)}, u32[]{:S(2)}, u32[]{:S(2)}) %collective-permute-start.30) | collective-permute-done | bytes 262176 | tf_op jit(solution)/shard_map/ppermute | solution.py:612
  115.0 5.7 %collective-permute-done.31.refs_2_ = bf16[64,2048]{1,0:T(8,128)(2,1)S(1)} collective-permute-done((bf16[64,2048]{1,0:T(8,128)(2,1)S(1)}, bf16[64,2048]{1,0:T(8,128)(2,1)S(1)}, u32[]{:S(2)}, u32[]{:S(2)}) %collective-permute-start.31) | collective-permute-done | bytes 262176 | tf_op jit(solution)/shard_map/ppermute | solution.py:612
  120.6 0.9 shard_map.184
  121.5 2.1 %all-to-all-done = bf16[16,4,2048]{2,1,0:T(4,128)(2,1)} async-done(((bf16[16,4,2048]{2,1,0:T(4,128)(2,1)}), bf16[16,4,2048]{2,1,0:T(4,128)(2,1)}, u32[]{:S(2)}, u32[]{:S(2)}) %all-to-all-start) | async-done | bytes 262176 | tf_op jit(solution)/shard_map/all_to_all | solution.py:647
  123.6 9.5 %all-to-all-start.1 = ((bf16[16,4,2048]{2,1,0:T(4,128)(2,1)}), bf16[16,4,2048]{2,1,0:T(4,128)(2,1)S(1)}, u32[]{:S(2)}, u32[]{:S(2)}) async-start(bf16[16,4,2048]{2,1,0:T(4,128)(2,1)} %shard_map.184), calls=%async_computation.1 | async-start | bytes 524288 | tf_op jit(solution)/shard_map/all_to_all | solution.py:647
  133.1 2.5 %collective-permute-start.20 = (bf16[48,256]{1,0:T(8,128)(2,1)S(1)}, bf16[48,256]{1,0:T(8,128)(2,1)S(1)}, u32[]{:S(2)}, u32[]{:S(2)}) collective-permute-start(bf16[48,256]{1,0:T(8,128)(2,1)S(1)} %get-tuple-element.133), channel_id=1, source_target_pairs={{0,9},{1,10},{2,11},{3,12},{4,13},{5,14},{6,15},{7,8},{8,17},{9,18... | collective-permute-start | bytes 73736 | tf_op jit(solution)/shard_map/ppermute | solution.py:622
  135.6 8.5 %collective-permute-done.20.w3 = bf16[48,256]{1,0:T(8,128)(2,1)S(1)} collective-permute-done((bf16[48,256]{1,0:T(8,128)(2,1)S(1)}, bf16[48,256]{1,0:T(8,128)(2,1)S(1)}, u32[]{:S(2)}, u32[]{:S(2)}) %collective-permute-start.20) | collective-permute-done | bytes 24608 | tf_op jit(solution)/shard_map/ppermute | solution.py:622
  144.2 1.7 %shard_map.177 = bf16[14,28,256]{2,1,0:T(8,128)(2,1)} custom-call(bf16[512,256]{1,0:T(8,128)(2,1)S(1)} %copy-done.12, bf16[176,256]{1,0:T(8,128)(2,1)S(1)} %collective-permute-done.18.w1, bf16[96,256]{1,0:T(8,128)(2,1)S(1)} %collective-permute-done.19.w2, bf16[48,256]{1,0:T(8,128)(2,1)S(1)} %collective-permute-done.20.w3, bf16[448,256]{1,0:T(8,128)(2,1)S(1)} %copy-done.18, ...), custom_call_target="tpu_custom_call" | custom-call | flops 1073741824 | bytes 4194304 | tf_op jit(solution)/shard_map/pallas_call | solution.py:600
  145.9 1.1 convert_reduce_fusion
  147.1 0.6 copy.19
  147.6 0.6 copy.20
  148.2 0.6 reshape.31
  148.9 0.6 pad_maximum_fusion
  149.5 0.5 all-to-all-done.1
  150.1 0.6 reshape.34
  150.7 0.6 copy.21
  (78 shorter events, 1.1 us)
Async XLA Ops:
  0.6 34.3 %copy-start.3 = (bf16[256,768]{1,0:T(8,128)(2,1)S(1)}, bf16[256,768]{1,0:T(8,128)(2,1)}, u32[]{:S(2)}) copy-start(bf16[256,768]{1,0:T(8,128)(2,1)} %qkv.5) | copy-start | bytes 1179652
  0.6 1.0 copy-start.4
  1.6 0.9 copy-start.6
  2.5 32.4 %copy-start.5 = (bf16[256,256]{1,0:T(8,128)(2,1)S(1)}, bf16[256,256]{1,0:T(8,128)(2,1)}, u32[]{:S(2)}) copy-start(bf16[256,256]{1,0:T(8,128)(2,1)} %proj.5) | copy-start | bytes 393220
  2.5 32.4 %copy-start.9 = (f32[256]{0:T(256)S(1)}, f32[256]{0:T(256)}, u32[]{:S(2)}) copy-start(f32[256]{0:T(256)} %param.14) | copy-start | bytes 3076
  2.8 32.1 %collective-permute-start.2 = (bf16[48,256]{1,0:T(8,128)(2,1)S(1)}, bf16[48,256]{1,0:T(8,128)(2,1)S(1)}, u32[]{:S(2)}, u32[]{:S(2)}) collective-permute-start(bf16[48,256]{1,0:T(8,128)(2,1)S(1)} %get-tuple-element.88), channel_id=1, source_target_pairs={{0,127},{1,120},{2,121},{3,122},{4,123},{5,124},{6,125},{7,126},{8... | collective-permute-start | bytes 73736 | tf_op jit(solution)/shard_map/ppermute | solution.py:622
  27.4 7.5 %collective-permute-start.1 = (bf16[96,256]{1,0:T(8,128)(2,1)S(1)}, bf16[96,256]{1,0:T(8,128)(2,1)S(1)}, u32[]{:S(2)}, u32[]{:S(2)}) collective-permute-start(bf16[96,256]{1,0:T(8,128)(2,1)S(1)} %get-tuple-element.87), channel_id=1, source_target_pairs={{0,7},{1,0},{2,1},{3,2},{4,3},{5,4},{6,5},{7,6},{8,15},{9,8},{10,9... | collective-permute-start | bytes 147464 | tf_op jit(solution)/shard_map/ppermute | solution.py:612
  28.2 6.7 %collective-permute-start = (bf16[192,256]{1,0:T(8,128)(2,1)S(1)}, bf16[192,256]{1,0:T(8,128)(2,1)S(1)}, u32[]{:S(2)}, u32[]{:S(2)}) collective-permute-start(bf16[192,256]{1,0:T(8,128)(2,1)S(1)} %get-tuple-element.86), channel_id=1, source_target_pairs={{0,120},{8,0},{16,8},{24,16},{32,24},{40,32},{48,40},{56,48},{64,5... | collective-permute-start | bytes 294920 | tf_op jit(solution)/shard_map/ppermute | solution.py:612
  28.4 0.7 copy-start.10
  34.1 0.8 copy-start.15
  34.9 11.3 %copy-start.13 = (bf16[448,832]{1,0:T(8,128)(2,1)}, bf16[448,832]{1,0:T(8,128)(2,1)S(1)}, u32[]{:S(2)}) copy-start(bf16[448,832]{1,0:T(8,128)(2,1)S(1)} %get-tuple-element.97.sel_back) | copy-start | bytes 2236420
  35.0 11.2 %copy-start.1 = (bf16[1024,512]{1,0:T(8,128)(2,1)S(1)}, bf16[1024,512]{1,0:T(8,128)(2,1)}, u32[]{:S(2)}) copy-start(bf16[1024,512]{1,0:T(8,128)(2,1)} %weight.3) | copy-start | bytes 3145732
  35.0 11.2 %copy-start.7 = (f32[1024]{0:T(1024)S(1)}, f32[1024]{0:T(1024)}, u32[]{:S(2)}) copy-start(f32[1024]{0:T(1024)} %param.17) | copy-start | bytes 12292
  35.0 11.2 %copy-start.8 = (f32[512]{0:T(512)S(1)}, f32[512]{0:T(512)}, u32[]{:S(2)}) copy-start(f32[512]{0:T(512)} %param.19) | copy-start | bytes 6148
  37.6 8.6 %collective-permute-start.3 = (bf16[176,256]{1,0:T(8,128)(2,1)S(1)}, bf16[176,256]{1,0:T(8,128)(2,1)S(1)}, u32[]{:S(2)}, u32[]{:S(2)}) collective-permute-start(bf16[176,256]{1,0:T(8,128)(2,1)S(1)} %get-tuple-element.93), channel_id=1, source_target_pairs={{0,8},{8,16},{16,24},{24,32},{32,40},{40,48},{48,56},{56,64},{64,7... | collective-permute-start | bytes 270344 | tf_op jit(solution)/shard_map/ppermute | solution.py:612
  39.6 6.6 %collective-permute-start.4 = (bf16[96,256]{1,0:T(8,128)(2,1)S(1)}, bf16[96,256]{1,0:T(8,128)(2,1)S(1)}, u32[]{:S(2)}, u32[]{:S(2)}) collective-permute-start(bf16[96,256]{1,0:T(8,128)(2,1)S(1)} %get-tuple-element.94), channel_id=1, source_target_pairs={{0,1},{1,2},{2,3},{3,4},{4,5},{5,6},{6,7},{7,0},{8,9},{9,10},{10,1... | collective-permute-start | bytes 147464 | tf_op jit(solution)/shard_map/ppermute | solution.py:612
  39.6 6.6 %collective-permute-start.5 = (bf16[48,256]{1,0:T(8,128)(2,1)S(1)}, bf16[48,256]{1,0:T(8,128)(2,1)S(1)}, u32[]{:S(2)}, u32[]{:S(2)}) collective-permute-start(bf16[48,256]{1,0:T(8,128)(2,1)S(1)} %get-tuple-element.95), channel_id=1, source_target_pairs={{0,9},{1,10},{2,11},{3,12},{4,13},{5,14},{6,15},{7,8},{8,17},{9,18... | collective-permute-start | bytes 73736 | tf_op jit(solution)/shard_map/ppermute | solution.py:622
  39.6 9.9 %collective-permute-start.10 = (bf16[48,512]{1,0:T(8,128)(2,1)S(1)}, bf16[48,512]{1,0:T(8,128)(2,1)S(1)}, u32[]{:S(2)}, u32[]{:S(2)}) collective-permute-start(bf16[48,512]{1,0:T(8,128)(2,1)S(1)} %get-tuple-element.105), channel_id=1, source_target_pairs={{0,7},{1,0},{2,1},{3,2},{4,3},{5,4},{6,5},{7,6},{8,15},{9,8},{10,9... | collective-permute-start | bytes 147464 | tf_op jit(solution)/shard_map/ppermute | solution.py:612
  42.5 9.7 %collective-permute-start.9 = (bf16[96,512]{1,0:T(8,128)(2,1)S(1)}, bf16[96,512]{1,0:T(8,128)(2,1)S(1)}, u32[]{:S(2)}, u32[]{:S(2)}) collective-permute-start(bf16[96,512]{1,0:T(8,128)(2,1)S(1)} %get-tuple-element.104), channel_id=1, source_target_pairs={{0,120},{8,0},{16,8},{24,16},{32,24},{40,32},{48,40},{56,48},{64,5... | collective-permute-start | bytes 294920 | tf_op jit(solution)/shard_map/ppermute | solution.py:612
  46.2 7.5 %copy-start = (bf16[512,1536]{1,0:T(8,128)(2,1)S(1)}, bf16[512,1536]{1,0:T(8,128)(2,1)}, u32[]{:S(2)}) copy-start(bf16[512,1536]{1,0:T(8,128)(2,1)} %qkv.4) | copy-start | bytes 4718596
  46.2 7.5 %copy-start.2 = (bf16[512,512]{1,0:T(8,128)(2,1)S(1)}, bf16[512,512]{1,0:T(8,128)(2,1)}, u32[]{:S(2)}) copy-start(bf16[512,512]{1,0:T(8,128)(2,1)} %proj.4) | copy-start | bytes 1572868
  47.8 0.7 copy-start.17
  48.5 5.2 %collective-permute-start.6 = (bf16[96,512]{1,0:T(8,128)(2,1)S(1)}, bf16[96,512]{1,0:T(8,128)(2,1)S(1)}, u32[]{:S(2)}, u32[]{:S(2)}) collective-permute-start(bf16[96,512]{1,0:T(8,128)(2,1)S(1)} %get-tuple-element.100), channel_id=1, source_target_pairs={{0,120},{8,0},{16,8},{24,16},{32,24},{40,32},{48,40},{56,48},{64,5... | collective-permute-start | bytes 294920 | tf_op jit(solution)/shard_map/ppermute | solution.py:612
  48.6 3.6 %collective-permute-start.11 = (bf16[48,512]{1,0:T(8,128)(2,1)S(1)}, bf16[48,512]{1,0:T(8,128)(2,1)S(1)}, u32[]{:S(2)}, u32[]{:S(2)}) collective-permute-start(bf16[48,512]{1,0:T(8,128)(2,1)S(1)} %get-tuple-element.106), channel_id=1, source_target_pairs={{0,127},{1,120},{2,121},{3,122},{4,123},{5,124},{6,125},{7,126},{8... | collective-permute-start | bytes 147464 | tf_op jit(solution)/shard_map/ppermute | solution.py:622
  48.9 3.3 %collective-permute-start.7 = (bf16[48,512]{1,0:T(8,128)(2,1)S(1)}, bf16[48,512]{1,0:T(8,128)(2,1)S(1)}, u32[]{:S(2)}, u32[]{:S(2)}) collective-permute-start(bf16[48,512]{1,0:T(8,128)(2,1)S(1)} %get-tuple-element.101), channel_id=1, source_target_pairs={{0,7},{1,0},{2,1},{3,2},{4,3},{5,4},{6,5},{7,6},{8,15},{9,8},{10,9... | collective-permute-start | bytes 147464 | tf_op jit(solution)/shard_map/ppermute | solution.py:612
  49.5 4.0 %collective-permute-start.8 = (bf16[48,512]{1,0:T(8,128)(2,1)S(1)}, bf16[48,512]{1,0:T(8,128)(2,1)S(1)}, u32[]{:S(2)}, u32[]{:S(2)}) collective-permute-start(bf16[48,512]{1,0:T(8,128)(2,1)S(1)} %get-tuple-element.102), channel_id=1, source_target_pairs={{0,127},{1,120},{2,121},{3,122},{4,123},{5,124},{6,125},{7,126},{8... | collective-permute-start | bytes 147464 | tf_op jit(solution)/shard_map/ppermute | solution.py:622
  57.1 12.8 %collective-permute-start.12 = (bf16[96,1024]{1,0:T(8,128)(2,1)S(1)}, bf16[96,1024]{1,0:T(8,128)(2,1)S(1)}, u32[]{:S(2)}, u32[]{:S(2)}) collective-permute-start(bf16[96,1024]{1,0:T(8,128)(2,1)S(1)} %get-tuple-element.111), channel_id=1, source_target_pairs={{0,8},{8,16},{16,24},{24,32},{32,40},{40,48},{48,56},{56,64},{64,7... | collective-permute-start | bytes 589832 | tf_op jit(solution)/shard_map/ppermute | solution.py:612
  58.9 5.3 %collective-permute-start.13 = (bf16[48,1024]{1,0:T(8,128)(2,1)S(1)}, bf16[48,1024]{1,0:T(8,128)(2,1)S(1)}, u32[]{:S(2)}, u32[]{:S(2)}) collective-permute-start(bf16[48,1024]{1,0:T(8,128)(2,1)S(1)} %get-tuple-element.112), channel_id=1, source_target_pairs={{0,1},{1,2},{2,3},{3,4},{4,5},{5,6},{6,7},{7,0},{8,9},{9,10},{10,1... | collective-permute-start | bytes 294920 | tf_op jit(solution)/shard_map/ppermute | solution.py:612
  58.9 11.0 %collective-permute-start.14 = (bf16[48,1024]{1,0:T(8,128)(2,1)S(1)}, bf16[48,1024]{1,0:T(8,128)(2,1)S(1)}, u32[]{:S(2)}, u32[]{:S(2)}) collective-permute-start(bf16[48,1024]{1,0:T(8,128)(2,1)S(1)} %get-tuple-element.113), channel_id=1, source_target_pairs={{0,9},{1,10},{2,11},{3,12},{4,13},{5,14},{6,15},{7,8},{8,17},{9,18... | collective-permute-start | bytes 294920 | tf_op jit(solution)/shard_map/ppermute | solution.py:622
  71.2 3.3 %collective-permute-start.17 = (bf16[48,256]{1,0:T(8,128)(2,1)S(1)}, bf16[48,256]{1,0:T(8,128)(2,1)S(1)}, u32[]{:S(2)}, u32[]{:S(2)}) collective-permute-start(bf16[48,256]{1,0:T(8,128)(2,1)S(1)} %get-tuple-element.122), channel_id=1, source_target_pairs={{0,127},{1,120},{2,121},{3,122},{4,123},{5,124},{6,125},{7,126},{8... | collective-permute-start | bytes 73736 | tf_op jit(solution)/shard_map/ppermute | solution.py:622
  71.3 3.2 %collective-permute-start.16 = (bf16[96,256]{1,0:T(8,128)(2,1)S(1)}, bf16[96,256]{1,0:T(8,128)(2,1)S(1)}, u32[]{:S(2)}, u32[]{:S(2)}) collective-permute-start(bf16[96,256]{1,0:T(8,128)(2,1)S(1)} %get-tuple-element.121), channel_id=1, source_target_pairs={{0,7},{1,0},{2,1},{3,2},{4,3},{5,4},{6,5},{7,6},{8,15},{9,8},{10,9... | collective-permute-start | bytes 147464 | tf_op jit(solution)/shard_map/ppermute | solution.py:612
  71.3 5.1 %collective-permute-start.15 = (bf16[176,256]{1,0:T(8,128)(2,1)S(1)}, bf16[176,256]{1,0:T(8,128)(2,1)S(1)}, u32[]{:S(2)}, u32[]{:S(2)}) collective-permute-start(bf16[176,256]{1,0:T(8,128)(2,1)S(1)} %get-tuple-element.120), channel_id=1, source_target_pairs={{0,120},{8,0},{16,8},{24,16},{32,24},{40,32},{48,40},{56,48},{64,5... | collective-permute-start | bytes 270344 | tf_op jit(solution)/shard_map/ppermute | solution.py:612
  73.0 13.9 %collective-permute-start.21 = (bf16[4,64,1024]{2,1,0:T(8,128)(2,1)S(1)}, bf16[4,64,1024]{2,1,0:T(8,128)(2,1)S(1)}, u32[]{:S(2)}, u32[]{:S(2)}) collective-permute-start(bf16[4,64,1024]{2,1,0:T(8,128)(2,1)S(1)} %get-tuple-element.140), channel_id=1, source_target_pairs={{0,1},{1,0},{2,3},{3,2},{4,5},{5,4},{6,7},{7,6},{8,9},{9,8},{10,11... | collective-permute-start | bytes 1572872 | tf_op jit(solution)/shard_map/ppermute | solution.py:612
  82.8 1.7 %copy-start.11 = (bf16[512,256]{1,0:T(8,128)(2,1)}, bf16[512,256]{1,0:T(8,128)(2,1)S(1)}, u32[]{:S(2)}) copy-start(bf16[512,256]{1,0:T(8,128)(2,1)S(1)} %get-tuple-element.130.w0) | copy-start | bytes 786436
  82.8 2.5 %collective-permute-start.25 = (bf16[4,48,1024]{2,1,0:T(8,128)(2,1)S(1)}, bf16[4,48,1024]{2,1,0:T(8,128)(2,1)S(1)}, u32[]{:S(2)}, u32[]{:S(2)}) collective-permute-start(bf16[4,48,1024]{2,1,0:T(8,128)(2,1)S(1)} %get-tuple-element.146), channel_id=1, source_target_pairs={{0,1},{1,0},{2,3},{3,2},{4,5},{5,4},{6,7},{7,6},{8,9},{9,8},{10,11... | collective-permute-start | bytes 1179656 | tf_op jit(solution)/shard_map/ppermute | solution.py:612
  84.5 21.4 %collective-permute-start.29 = (bf16[4,64,2048]{2,1,0:T(8,128)(2,1)S(1)}, bf16[4,64,2048]{2,1,0:T(8,128)(2,1)S(1)}, u32[]{:S(2)}, u32[]{:S(2)}) collective-permute-start(bf16[4,64,2048]{2,1,0:T(8,128)(2,1)S(1)} %get-tuple-element.157), channel_id=1, source_target_pairs={{0,1},{1,0},{2,3},{3,2},{4,5},{5,4},{6,7},{7,6},{8,9},{9,8},{10,11... | collective-permute-start | bytes 3145736 | tf_op jit(solution)/shard_map/ppermute | solution.py:612
  85.4 8.9 %collective-permute-start.26 = (bf16[48,1024]{1,0:T(8,128)(2,1)S(1)}, bf16[48,1024]{1,0:T(8,128)(2,1)S(1)}, u32[]{:S(2)}, u32[]{:S(2)}) collective-permute-start(bf16[48,1024]{1,0:T(8,128)(2,1)S(1)} %get-tuple-element.148), channel_id=1, source_target_pairs={{0,2},{2,4},{4,6},{6,0},{1,3},{3,5},{5,7},{7,1},{8,10},{10,12},{12... | collective-permute-start | bytes 294920 | tf_op jit(solution)/shard_map/ppermute | solution.py:612
  86.9 7.3 %collective-permute-start.27 = (bf16[48,1024]{1,0:T(8,128)(2,1)S(1)}, bf16[48,1024]{1,0:T(8,128)(2,1)S(1)}, u32[]{:S(2)}, u32[]{:S(2)}) collective-permute-start(bf16[48,1024]{1,0:T(8,128)(2,1)S(1)} %get-tuple-element.149), channel_id=1, source_target_pairs={{0,4},{2,6},{4,0},{6,2},{1,5},{3,7},{5,1},{7,3},{8,12},{10,14},{12... | collective-permute-start | bytes 294920 | tf_op jit(solution)/shard_map/ppermute | solution.py:612
  87.1 13.2 %collective-permute-start.22 = (bf16[64,1024]{1,0:T(8,128)(2,1)S(1)}, bf16[64,1024]{1,0:T(8,128)(2,1)S(1)}, u32[]{:S(2)}, u32[]{:S(2)}) collective-permute-start(bf16[64,1024]{1,0:T(8,128)(2,1)S(1)} %get-tuple-element.142), channel_id=1, source_target_pairs={{0,2},{2,4},{4,6},{6,0},{1,3},{3,5},{5,7},{7,1},{8,10},{10,12},{12... | collective-permute-start | bytes 393224 | tf_op jit(solution)/shard_map/ppermute | solution.py:612
  89.8 10.4 %collective-permute-start.23 = (bf16[64,1024]{1,0:T(8,128)(2,1)S(1)}, bf16[64,1024]{1,0:T(8,128)(2,1)S(1)}, u32[]{:S(2)}, u32[]{:S(2)}) collective-permute-start(bf16[64,1024]{1,0:T(8,128)(2,1)S(1)} %get-tuple-element.143), channel_id=1, source_target_pairs={{0,4},{2,6},{4,0},{6,2},{1,5},{3,7},{5,1},{7,3},{8,12},{10,14},{12... | collective-permute-start | bytes 393224 | tf_op jit(solution)/shard_map/ppermute | solution.py:612
  94.3 6.0 %collective-permute-start.24 = (bf16[64,1024]{1,0:T(8,128)(2,1)S(1)}, bf16[64,1024]{1,0:T(8,128)(2,1)S(1)}, u32[]{:S(2)}, u32[]{:S(2)}) collective-permute-start(bf16[64,1024]{1,0:T(8,128)(2,1)S(1)} %get-tuple-element.144), channel_id=1, source_target_pairs={{0,6},{2,0},{4,2},{6,4},{1,7},{3,1},{5,3},{7,5},{8,14},{10,8},{12,... | collective-permute-start | bytes 393224 | tf_op jit(solution)/shard_map/ppermute | solution.py:612
  94.3 6.0 %collective-permute-start.28 = (bf16[48,1024]{1,0:T(8,128)(2,1)S(1)}, bf16[48,1024]{1,0:T(8,128)(2,1)S(1)}, u32[]{:S(2)}, u32[]{:S(2)}) collective-permute-start(bf16[48,1024]{1,0:T(8,128)(2,1)S(1)} %get-tuple-element.150), channel_id=1, source_target_pairs={{0,6},{2,0},{4,2},{6,4},{1,7},{3,1},{5,3},{7,5},{8,14},{10,8},{12,... | collective-permute-start | bytes 294920 | tf_op jit(solution)/shard_map/ppermute | solution.py:612
  101.3 22.3 %all-to-all-start = ((bf16[16,4,2048]{2,1,0:T(4,128)(2,1)}), bf16[16,4,2048]{2,1,0:T(4,128)(2,1)}, u32[]{:S(2)}, u32[]{:S(2)}) async-start(bf16[16,4,2048]{2,1,0:T(4,128)(2,1)} %shard_map.181), calls=%async_computation | async-start | bytes 524288 | tf_op jit(solution)/shard_map/all_to_all | solution.py:647
  105.9 38.3 %copy-start.12 = (bf16[512,256]{1,0:T(8,128)(2,1)S(1)}, bf16[512,256]{1,0:T(8,128)(2,1)}, u32[]{:S(2)}) copy-start(bf16[512,256]{1,0:T(8,128)(2,1)} %copy-done.11) | copy-start | bytes 786436
  105.9 38.2 %copy-start.16 = (bf16[448,448]{1,0:T(8,128)(2,1)S(1)}, bf16[448,448]{1,0:T(8,128)(2,1)}, u32[]{:S(2)}) copy-start(bf16[448,448]{1,0:T(8,128)(2,1)} %copy-done.15) | copy-start | bytes 1204228
  105.9 38.2 %copy-start.18 = (bf16[448,256]{1,0:T(8,128)(2,1)S(1)}, bf16[448,256]{1,0:T(8,128)(2,1)}, u32[]{:S(2)}) copy-start(bf16[448,256]{1,0:T(8,128)(2,1)} %copy-done.17) | copy-start | bytes 688132
  106.2 38.0 %copy-start.14 = (bf16[448,832]{1,0:T(8,128)(2,1)S(1)}, bf16[448,832]{1,0:T(8,128)(2,1)}, u32[]{:S(2)}) copy-start(bf16[448,832]{1,0:T(8,128)(2,1)} %copy-done.13) | copy-start | bytes 2236420
  106.2 8.8 %collective-permute-start.30 = (bf16[64,2048]{1,0:T(8,128)(2,1)S(1)}, bf16[64,2048]{1,0:T(8,128)(2,1)S(1)}, u32[]{:S(2)}, u32[]{:S(2)}) collective-permute-start(bf16[64,2048]{1,0:T(8,128)(2,1)S(1)} %get-tuple-element.159), channel_id=1, source_target_pairs={{0,2},{2,4},{4,6},{6,0},{1,3},{3,5},{5,7},{7,1},{8,10},{10,12},{12... | collective-permute-start | bytes 786440 | tf_op jit(solution)/shard_map/ppermute | solution.py:612
  107.2 13.4 %collective-permute-start.31 = (bf16[64,2048]{1,0:T(8,128)(2,1)S(1)}, bf16[64,2048]{1,0:T(8,128)(2,1)S(1)}, u32[]{:S(2)}, u32[]{:S(2)}) collective-permute-start(bf16[64,2048]{1,0:T(8,128)(2,1)S(1)} %get-tuple-element.160), channel_id=1, source_target_pairs={{0,4},{2,6},{4,0},{6,2},{1,5},{3,7},{5,1},{7,3},{8,12},{10,14},{12... | collective-permute-start | bytes 786440 | tf_op jit(solution)/shard_map/ppermute | solution.py:612
  110.1 10.6 %collective-permute-start.32 = (bf16[64,2048]{1,0:T(8,128)(2,1)S(1)}, bf16[64,2048]{1,0:T(8,128)(2,1)S(1)}, u32[]{:S(2)}, u32[]{:S(2)}) collective-permute-start(bf16[64,2048]{1,0:T(8,128)(2,1)S(1)} %get-tuple-element.161), channel_id=1, source_target_pairs={{0,6},{2,0},{4,2},{6,4},{1,7},{3,1},{5,3},{7,5},{8,14},{10,8},{12,... | collective-permute-start | bytes 786440 | tf_op jit(solution)/shard_map/ppermute | solution.py:612
  111.0 33.1 %collective-permute-start.18 = (bf16[176,256]{1,0:T(8,128)(2,1)S(1)}, bf16[176,256]{1,0:T(8,128)(2,1)S(1)}, u32[]{:S(2)}, u32[]{:S(2)}) collective-permute-start(bf16[176,256]{1,0:T(8,128)(2,1)S(1)} %get-tuple-element.131), channel_id=1, source_target_pairs={{0,8},{8,16},{16,24},{24,32},{32,40},{40,48},{48,56},{56,64},{64,7... | collective-permute-start | bytes 270344 | tf_op jit(solution)/shard_map/ppermute | solution.py:612
  123.6 26.4 %all-to-all-start.1 = ((bf16[16,4,2048]{2,1,0:T(4,128)(2,1)}), bf16[16,4,2048]{2,1,0:T(4,128)(2,1)S(1)}, u32[]{:S(2)}, u32[]{:S(2)}) async-start(bf16[16,4,2048]{2,1,0:T(4,128)(2,1)} %shard_map.184), calls=%async_computation.1 | async-start | bytes 524288 | tf_op jit(solution)/shard_map/all_to_all | solution.py:647
  133.1 11.1 %collective-permute-start.19 = (bf16[96,256]{1,0:T(8,128)(2,1)S(1)}, bf16[96,256]{1,0:T(8,128)(2,1)S(1)}, u32[]{:S(2)}, u32[]{:S(2)}) collective-permute-start(bf16[96,256]{1,0:T(8,128)(2,1)S(1)} %get-tuple-element.132), channel_id=1, source_target_pairs={{0,1},{1,2},{2,3},{3,4},{4,5},{5,6},{6,7},{7,0},{8,9},{9,10},{10,1... | collective-permute-start | bytes 147464 | tf_op jit(solution)/shard_map/ppermute | solution.py:612
  133.1 11.0 %collective-permute-start.20 = (bf16[48,256]{1,0:T(8,128)(2,1)S(1)}, bf16[48,256]{1,0:T(8,128)(2,1)S(1)}, u32[]{:S(2)}, u32[]{:S(2)}) collective-permute-start(bf16[48,256]{1,0:T(8,128)(2,1)S(1)} %get-tuple-element.133), channel_id=1, source_target_pairs={{0,9},{1,10},{2,11},{3,12},{4,13},{5,14},{6,15},{7,8},{8,17},{9,18... | collective-permute-start | bytes 73736 | tf_op jit(solution)/shard_map/ppermute | solution.py:622
where the time goes:
time: 153 us; the launch traced here: 151 us
  starting transfers between devices  70.1 us (46%)
  waiting for transfers between devices  43.9 us (29%)
  Pallas kernels  27.2 us (18%)
  local copies, waits for them, and re-layouts  7.1 us (5%)
  other arithmetic  1.89 us (1%)
    ppermute x7, starting transfers between devices, moved_across(): return lax.ppermute(value, ROWS_COLS, pairs)  29.6 us
    pallas_call x15, Pallas kernels, call(): pl.pallas_call(body, in_specs=[smem] * scalars + [vmem] * (len(args) - sc...  27.2 us
    ppermute x26, starting transfers between devices, moved(): lax.ppermute(value, axis, [(i, (i + by) % count) for i in range(count)])  26.5 us
    ppermute x26, waiting for transfers between devices, moved(): lax.ppermute(value, axis, [(i, (i + by) % count) for i in range(count)])  20.8 us
    ppermute x7, waiting for transfers between devices, moved_across(): return lax.ppermute(value, ROWS_COLS, pairs)  20.5 us
    all_to_all x2, starting transfers between devices, spread_sum(): spread = lax.all_to_all(blocks, 'rows', 0, 0)  14 us
    unnamed x43, local copies, waits for them, and re-layouts  5.85 us
  transfers between devices with their start and end apart: 35, of which 15 were waited for; matrix products, arithmetic and copies ran while one was open for 2% of the time, Pallas kernels for 13%

commit v1 on v0

--- a/solution.py
+++ b/solution.py
@@ -14,6 +14,7 @@
 TILE = 128
 HEAD = 32
 EDGE = WIN - 1
+NEAR = 4
 COLS = ("cols_0", "cols_1")
 ROWS_COLS = ("rows", "cols_0", "cols_1")
 GROUPS_ROWS_COLS = ("groups", "rows", "cols_0", "cols_1")
@@ -92,8 +93,12 @@
     return jnp.concatenate([bias] * (TILE // HEAD), axis=0)
 
 
+def tile_at(start):
+    return pl.ds(pl.multiple_of(start, TILE), TILE)
+
+
 def thirds(packed, rows, width, t):
-    return (packed[rows, p * width + t * TILE : p * width + (t + 1) * TILE] for p in range(3))
+    return (packed[rows, tile_at(p * width + t * TILE)] for p in range(3))
 
 
 def head_grads(tall, share, above, k, v):
@@ -109,29 +114,32 @@
 
 def put_thirds(out, rows, width, t, grads):
     for p, grad in enumerate(grads):
-        at = p * width + t * TILE
-        out[rows, at : at + TILE] = grad.astype(BF)
+        out[rows, tile_at(p * width + t * TILE)] = grad.astype(BF)
 
 
 def put_pieces(grad, outs, block, lanes, halves=1):
     cores, xs = len(outs), outs[0].shape[0]
     size = grad.shape[0] // (cores * xs * halves)
     width = grad.shape[1]
+    rows = pl.ds(pl.multiple_of(block * size, size), size)
     for h in range(halves):
         for c in range(cores):
             for x in range(xs):
                 at = ((h * cores + c) * xs + x) * size
                 lo = lanes + h * width
-                outs[c][x, block * size : (block + 1) * size, lo : lo + width] = grad[
-                    at : at + size
-                ].astype(BF)
-
-
-def weight_grad(acts, order, upstream, out, lanes, halves=1):
+                outs[c][x, rows, lo : lo + width] = grad[at : at + size].astype(BF)
+
+
+def weight_grad(acts, order, upstream, outs, lanes, halves=1):
     side = order.shape[0]
-    for block in range(acts.shape[1] // side):
-        moved = pick_cols(acts[:, block * side : (block + 1) * side], order)
-        put_pieces(mm_tn(moved, upstream), out, block, lanes, halves)
+
+    def step(block, carry):
+        cols = pl.ds(pl.multiple_of(block * side, side), side)
+        moved_cols = pick_cols(acts[:, cols], order)
+        put_pieces(mm_tn(moved_cols, upstream), outs, block, lanes, halves)
+        return carry
+
+    lax.fori_loop(0, acts.shape[1] // side, step, 0)
 
 
 def pick_cols(acts, order):
@@ -171,27 +179,23 @@
     return jnp.where(p < height * breadth, place(r + row0, c + col0), -1)
 
 
-def input_edges(tokens, cot, tokens_o, cot_o, t0, t1, t2, c0, c1, c2):
-    for source, laid, rows_o, cols_o, corner_o in (
-        (tokens, tokens_o, t0, t1, t2),
-        (cot, cot_o, c0, c1, c2),
-    ):
-        rows, cols, width = source.shape
-        pad = laid.shape[0] // rows
-        blank = jnp.zeros((pad - cols, width), BF)
-        parts = []
-        for r in range(rows):
-            parts += [source[r].astype(F32), blank.astype(F32)]
-        whole = jnp.concatenate(parts, axis=0).astype(BF)
-        laid[...] = whole
-        rows_o[...] = whole[: EDGE * pad]
-
-        def place(r, c, pad=pad):
-            return r * pad + c
-
-        for out, height in ((cols_o, rows), (corner_o, EDGE)):
-            wanted = strip(lines(out.shape[0]), height, EDGE, place)
-            out[...] = pick(one_hot(wanted, whole.shape[0]), whole)
+def input_edges(source, laid, rows_o, cols_o, corner_o):
+    rows, cols, width = source.shape
+    pad = laid.shape[0] // rows
+    blank = jnp.zeros((pad - cols, width), F32)
+    parts = []
+    for r in range(rows):
+        parts += [source[r].astype(F32), blank]
+    whole = jnp.concatenate(parts, axis=0).astype(BF)
+    laid[...] = whole
+    rows_o[...] = whole[: EDGE * pad]
+
+    def place(r, c):
+        return r * pad + c
+
+    for out, height in ((cols_o, rows), (corner_o, EDGE)):
+        wanted = strip(lines(out.shape[0]), height, EDGE, place)
+        out[...] = pick(one_hot(wanted, whole.shape[0]), whole)
 
 
 def make_tables(tile, tile3, ranks, depths):
@@ -267,50 +271,63 @@
         a, b = div(m, pad3), mod(m, pad3)
         return b < three_cols, 2 * a + mod(k, 2), 2 * b + div(k, 2)
 
-    def body(
-        offsets, where, sel_a, tail2, sel_tokens, sel_b, head3, sel3, tail3, sel3b, head2, sel_e,
-        sel_out, order2, order3, order_m, bias2, bias3,
-    ):
-        s0, s1, s2, s3 = (offsets[i] for i in range(4))
+    def fill(out, wanted_of, block):
+        def step(i, carry):
+            at = pl.multiple_of(i * block, block)
+            out[pl.ds(at, block), :] = one_hot(wanted_of(lines(block, at)), out.shape[1])
+            return carry
+
+        lax.fori_loop(0, out.shape[0] // block, step, 0)
+
+    def in_pad(r, c):
+        return r * pad + c
+
+    def in_pad3(r, c):
+        return r * pad3 + c
+
+    def label(at, extent, shift):
+        return jnp.where(at < extent - WIN, 0, jnp.where(at < extent - shift, 1, 2))
+
+    def bias(where, first, line, extent, shifts):
         row_rank, x_rank, c_rank = (where[i] for i in range(3))
         col_rank = x_rank * cores + c_rank
 
-        def fill(out, wanted_of, block):
-            def step(i, carry):
-                at = pl.multiple_of(i * block, block)
-                out[pl.ds(at, block), :] = one_hot(wanted_of(lines(block, at)), out.shape[1])
-                return carry
-
-            lax.fori_loop(0, out.shape[0] // block, step, 0)
-
-        def in_pad(r, c):
-            return r * pad + c
-
-        def in_pad3(r, c):
-            return r * pad3 + c
-
+        def marks(p):
+            valid, row, col = window_line(p, line)
+            r = label(row + row_rank * extent[0], extent[0] * rows, shifts[0])
+            c = label(col + col_rank * extent[1], extent[1] * xs * cores, shifts[1])
+            near = div(p, SLOT) * 2 + jnp.where(valid, 1, 0)
+            return near, jnp.where(valid, r * 3 + c, -1)
+
+        near_p, mark_p = marks(lines(PAIR, first))
+        near_q, mark_q = marks(lax.broadcasted_iota(jnp.int32, (1, PAIR), 1) + first)
+        same = jnp.where(mark_p == mark_q, 0.0, MASKED)
+        return jnp.where(near_p == near_q, same, APART).astype(F32)
+
+    def early(offsets, where, sel_a, tail2, sel_tokens, sel_b, head3, bias2):
+        s0, s1 = offsets[0], offsets[1]
         fill(
             sel_a,
             lambda p: ahead(p, line2, tile, (s0, s1), in_pad, main_n, pad, rows_n, ec),
-            64,
+            32,
         )
         fill(
             tail2,
             lambda p: edges(p, in_windows2, tile, (tile_rows - EDGE, tile_cols - EDGE), (er, ec)),
-            64,
+            32,
         )
 
         def from_grid(q):
             real, r, c = grid_of(q)
             return jnp.where(real, in_pad(r, c), -1)
 
-        fill(sel_tokens, from_grid, 64)
+        fill(sel_tokens, from_grid, 32)
 
         def back2(q):
             real, r, c = grid_of(q)
             return behind(real, r - s0, c - s1, in_windows2, n2, tile, er, ec)
 
-        fill(sel_b, back2, 64)
+        fill(sel_b, back2, 32)
 
         def head_of_three(p):
             v = strip(p - hr, three_rows, EDGE, in_pad3)
@@ -318,10 +335,18 @@
             return jnp.where(p < hr, p, jnp.where(p < hr + hc, v, x))
 
         fill(head3, head_of_three, 16)
+        for g in range(bias2.shape[0]):
+            bias2[g] = bias(where, g * PAIR, line2, tile, (s0, s1))
+
+    def late(
+        offsets, where, sel3, tail3, sel3b, head2, sel_e, sel_out, order2, order3, order_m, bias3
+    ):
+        s0, s1, s2, s3 = (offsets[i] for i in range(4))
+        x_rank, c_rank = where[1], where[2]
         fill(
             sel3,
             lambda p: ahead(p, line3, tile3, (s2, s3), in_pad3, size3, pad3, hr, hc),
-            64,
+            32,
         )
         fill(
             tail3,
@@ -336,17 +361,17 @@
             return behind(b < three_cols, a - s2, b - s3, in_windows3, n3, tile3, tr, hc)
 
         fill(sel3b, back3, 16)
-        fill(head2, lambda p: edges(p, in_planes, tile, (0, 0), (er, ec)), 64)
+        fill(head2, lambda p: edges(p, in_planes, tile, (0, 0), (er, ec)), 32)
         fill(
             sel_e,
             lambda p: ahead(p, line2, tile, (s0, s1), in_planes, n4, tile_cols, er, ec),
-            64,
+            32,
         )
 
         def to_grid(g):
             return jnp.where(mod(g, pad) < tile_cols, in_planes(div(g, pad), mod(g, pad)), -1)
 
-        fill(sel_out, to_grid, 64)
+        fill(sel_out, to_grid, 32)
 
         for out, depth, halves in ((order2, depths[0], 1), (order3, depths[1], 1), (order_m, depths[2], 2)):
             side = out.shape[0]
@@ -363,33 +388,17 @@
             lanes = lax.broadcasted_iota(jnp.int32, (side, side), 0)
             out[...] = (lanes == source).astype(F32).astype(BF)
 
-        def label(at, extent, shift):
-            return jnp.where(at < extent - WIN, 0, jnp.where(at < extent - shift, 1, 2))
-
-        def marks(p, line, extent, shifts):
-            valid, row, col = window_line(p, line)
-            r = label(row + row_rank * extent[0], extent[0] * rows, shifts[0])
-            c = label(col + col_rank * extent[1], extent[1] * xs * cores, shifts[1])
-            near = div(p, SLOT) * 2 + jnp.where(valid, 1, 0)
-            return near, jnp.where(valid, r * 3 + c, -1)
-
-        def bias(first, line, extent, shifts):
-            near_p, mark_p = marks(lines(PAIR, first), line, extent, shifts)
-            across = lax.broadcasted_iota(jnp.int32, (1, PAIR), 1) + first
-            near_q, mark_q = marks(across, line, extent, shifts)
-            same = jnp.where(mark_p == mark_q, 0.0, MASKED)
-            return jnp.where(near_p == near_q, same, APART).astype(F32)
-
-        for g in range(bias2.shape[0]):
-            bias2[g] = bias(g * PAIR, line2, tile, (s0, s1))
-        bias3[...] = bias(0, line3, tile3, (s2, s3))
-
-    shapes = [
+        bias3[...] = bias(where, 0, line3, tile3, (s2, s3))
+
+    early_shapes = [
         ((n2, main_n + rows_n + ec + ex), BF),
         ((er + ec + ex, n2), BF),
         ((n4, main_n), BF),
         ((n4, n2 + er + ec + ex), BF),
         ((hr + hc + ex, size3), BF),
+        ((n2 // PAIR, PAIR, PAIR), F32),
+    ]
+    late_shapes = [
         ((n3, size3 + hr + hc + ex), BF),
         ((tr + hc + ex, n3), BF),
         ((size3, n3 + tr + hc + ex), BF),
@@ -399,10 +408,9 @@
         ((256, 256), BF),
         ((256, 256), BF),
         ((256, 256), BF),
-        ((n2 // PAIR, PAIR, PAIR), F32),
         ((PAIR, PAIR), F32),
     ]
-    return body, shapes
+    return early, early_shapes, late, late_shapes
 
 
 def two_forward(
@@ -413,13 +421,17 @@
     rolled_o[...] = rolled
     packed_o[...] = mm(rolled, qkv[...]).astype(BF)
     width = rolled.shape[1]
-    for g in range(packed_o.shape[0] // PAIR):
-        rows = slice(g * PAIR, (g + 1) * PAIR)
+
+    def step(g, carry):
+        rows = pl.ds(pl.multiple_of(g * PAIR, PAIR), PAIR)
         mask = tiled_bias(bias[g])
         for t in range(width // TILE):
             q, k, v = thirds(packed_o, rows, width, t)
             share = soft(q, k, mask)[1].astype(BF)
-            mixed_o[rows, t * TILE : (t + 1) * TILE] = unstacked(mm(share, v)).astype(BF)
+            mixed_o[rows, tile_at(t * TILE)] = unstacked(mm(share, v)).astype(BF)
+        return carry
+
+    lax.fori_loop(0, packed_o.shape[0] // PAIR, step, 0)
     projected = mm(mixed_o[...], proj[...]).astype(BF)
     wins_o[...] = projected
     put_edges(projected, edges[...], (e0, e1, e2))
@@ -447,7 +459,7 @@
 
 def three_both(
     n0, n1, n2, n3, c0, c1, c2, c3, qkv, proj, sel, bias, edges,
-    both_o, rolled_o, above_o, mixed, d_packed, e0, e1, e2, packed,
+    both_o, rolled_o, above_o, mixed, d_packed, e0, e1, e2, packed, d_mixed,
 ):
     rolled = pick(sel[...], joined((n0, n1, n2, n3)))
     above = pick(sel[...], joined((c0, c1, c2, c3)))
@@ -455,17 +467,21 @@
     above_o[...] = above
     width = rolled.shape[1]
     packed[...] = mm(rolled, qkv[...]).astype(BF)
-    d_mixed = mm_nt(above, proj[...]).astype(BF)
+    d_mixed[...] = mm_nt(above, proj[...]).astype(BF)
     mask = tiled_bias(bias[...])
     rows = slice(0, PAIR)
-    for t in range(width // TILE):
-        lanes = slice(t * TILE, (t + 1) * TILE)
-        q, k, v = thirds(packed, rows, width, t)
-        tall, share = soft(q, k, mask)
-        mixed[:, lanes] = unstacked(mm(share.astype(BF), v)).astype(BF)
-        put_thirds(
-            d_packed, rows, width, t, head_grads(tall, share, stacked(d_mixed[:, lanes]), k, v)
-        )
+
+    def step(i, carry):
+        for t in (2 * i, 2 * i + 1):
+            lanes = tile_at(t * TILE)
+            q, k, v = thirds(packed, rows, width, t)
+            tall, share = soft(q, k, mask)
+            mixed[rows, lanes] = unstacked(mm(share.astype(BF), v)).astype(BF)
+            given = stacked(d_mixed[rows, lanes])
+            put_thirds(d_packed, rows, width, t, head_grads(tall, share, given, k, v))
+        return carry
+
+    lax.fori_loop(0, width // (2 * TILE), step, 0)
     projected = mm(mixed[...], proj[...]).astype(BF)
     d_rolled = mm_nt(d_packed[...], qkv[...]).astype(BF)
     both = jnp.concatenate([projected, d_rolled], axis=1)
@@ -475,8 +491,8 @@
 
 def three_grads(rolled, above, mixed, d_packed, order, send_o, keep_o):
     outs = (send_o, keep_o)
-    weight_grad(rolled[...], order[...], d_packed[...], outs, 0)
-    weight_grad(mixed[...], order[...], above[...], outs, 3 * rolled.shape[1])
+    weight_grad(rolled, order[...], d_packed[...], outs, 0)
+    weight_grad(mixed, order[...], above[...], outs, 3 * rolled.shape[1])
 
 
 def merge_backward(
@@ -506,7 +522,7 @@
 
 
 def merge_grads(norm, d_rows, order, send_o, keep_o):
-    weight_grad(norm[...], order[...], d_rows[...], (send_o, keep_o), 0, halves=2)
+    weight_grad(norm, order[...], d_rows[...], (send_o, keep_o), 0, halves=2)
 
 
 def two_backward(
@@ -532,8 +548,8 @@
     wins_o[...] = d_rolled
     put_edges(d_rolled, edges[...], (e0, e1, e2))
     outs = (send_o, keep_o)
-    weight_grad(rolled[...], order[...], d_packed[...], outs, 0)
-    weight_grad(mixed[...], order[...], above, outs, 3 * width)
+    weight_grad(rolled, order[...], d_packed[...], outs, 0)
+    weight_grad(mixed, order[...], above, outs, 3 * width)
     g2 = jnp.sum(d_rolled.astype(F32) * rolled[...].astype(F32), axis=0, keepdims=True) / gain[...]
     blank = jnp.zeros((1, width), F32)
     second = jnp.concatenate([g3[...], g2, blank], axis=1)
@@ -561,7 +577,7 @@
         out[...] = (keep[x].astype(F32) + got[x].astype(F32)).astype(BF)
 
 
-def line_added(parts):
+def added(parts):
     parts = [p[...].astype(F32) for p in parts]
     while len(parts) > 1:
         half = len(parts) // 2
@@ -569,30 +585,74 @@
     return parts[0]
 
 
-def put_blocks(value, out, at):
-    rows, sub = out.shape[:2]
-    for r in range(rows):
-        out[r, :, at : at + value.shape[1]] = value[r * sub : (r + 1) * sub].astype(BF)
-
-
-def line_sum(*refs):
-    *held, out = refs
-    put_blocks(line_added(held), out, 0)
-
-
-def line_sum_late(*refs):
-    *held, out = refs
-    count = len(held) // 2
-    rows, sub = out.shape[:2]
-    first = line_added(held[:count])
-    second = line_added(held[count:]).astype(BF)
-    share = second.shape[0] - 16
-    part = share // rows
-    p = lines(rows * sub)
-    r, j = div(p, sub), mod(p, sub)
-    wanted = jnp.where(j < part, r * part + j, share + j - part)
-    put_blocks(first, out, 0)
-    put_blocks(mm(one_hot(wanted, second.shape[0]), second), out, first.shape[1])
+def make_line_sum(rows, near, sub):
+    far = rows // near
+    size = far * sub
+
+    def line_sum(where, *refs):
+        held, outs = refs[: len(refs) - near], refs[len(refs) - near :]
+        count = len(held) // 3
+        p = lines(rows * sub)
+        j, a, k = div(p, size), div(mod(p, size), sub), mod(p, sub)
+        row = a * near + mod(mod(where[0], near) + j, near)
+        at = 0
+        for b in range(3):
+            total = added(held[b * count : (b + 1) * count]).astype(BF)
+            wanted = row * sub + k
+            if b == 2:
+                share = total.shape[0] - 16
+                part = share // rows
+                wanted = jnp.where(k < part, row * part + k, share + k - part)
+            laid = pick(one_hot(wanted, total.shape[0]), total)
+            for j, out in enumerate(outs):
+                out[:, at : at + laid.shape[1]] = laid[j * size : (j + 1) * size]
+            at += laid.shape[1]
+
+    def near_sum(where, *refs):
+        held, outs = refs[:near], refs[near:]
+        total = added(held).astype(BF)
+        p = lines(size)
+        own = div(where[0], near)
+        wanted = mod(own + div(p, sub), far) * sub + mod(p, sub)
+        laid = mm(one_hot(wanted, size), total)
+        for j, out in enumerate(outs):
+            out[...] = laid[j * sub : (j + 1) * sub].astype(BF)
+
+    return line_sum, near_sum
+
+
+def flat_lines(value, lo, width):
+    parts = []
+    for r in range(value.shape[0]):
+        for at in range(lo, lo + width, TILE):
+            parts.append(value[r : r + 1, at : at + TILE])
+    return parts
+
+
+def make_finish(wide, narrow, sub2, far):
+    def finish(*refs):
+        held, (gains_o, qkv2_o, proj2_o, merge_o, qkv3_o, proj3_o) = refs[:far], refs[far:]
+        total = added(held)
+        at = 6 * wide
+        late = total[:sub2]
+        extra = total[sub2 : sub2 + 2]
+        first, second = extra[:1], extra[1:]
+        gains = (
+            flat_lines(second, at + wide, narrow)
+            + flat_lines(first, at, 4 * narrow)
+            + flat_lines(second, at, wide)
+        )
+        for out, parts in (
+            (gains_o, gains),
+            (qkv2_o, flat_lines(late, at, 3 * narrow)),
+            (proj2_o, flat_lines(late, at + 3 * narrow, narrow)),
+            (merge_o, flat_lines(total, 4 * wide, wide) + flat_lines(total, 5 * wide, wide)),
+            (qkv3_o, flat_lines(total, 0, 3 * wide)),
+            (proj3_o, flat_lines(total, 3 * wide, wide)),
+        ):
+            out[...] = jnp.concatenate(parts, axis=0).astype(out.dtype)
+
+    return finish
 
 
 def call(body, outs, args, flops, scratch=(), scalars=0):
@@ -642,10 +702,10 @@
     return [blocks[0]] + [moved(blocks[j], "cols_0", j) for j in range(1, len(blocks))]
 
 
-def spread_sum(body, held, shape):
-    (blocks,) = call(body, [(shape, BF)], held, 1 << 26)
-    spread = lax.all_to_all(blocks, "rows", 0, 0)
-    return jnp.sum(spread.astype(F32), axis=0)
+def moved_near(value, by, near):
+    count = lax.axis_size("rows")
+    pairs = [(i, i - i % near + (i % near + by) % near) for i in range(count)]
+    return lax.ppermute(value, "rows", pairs)
 
 
 def on_device(
@@ -674,31 +734,36 @@
     hr, tr, hc = EDGE * pad3, up16(EDGE * three_cols), up16(three_rows * EDGE)
     gain2, gain_m, gain3 = norm2_gain[None], merge_gain[None], norm3_gain[None]
 
-    tokens_p, cot_p, *pieces = call(
+    tokens_p, *pieces = call(
         input_edges,
         [
             ((tile_rows * pad, narrow), BF),
-            ((size3, wide), BF),
             ((EDGE * pad, narrow), BF),
             ((ec, narrow), BF),
             ((ex, narrow), BF),
-            ((hr, wide), BF),
-            ((hc, wide), BF),
-            ((ex, wide), BF),
         ],
-        (tokens, cotangent),
+        (tokens,),
         1 << 28,
     )
-    token_pieces = exchanged(pieces[:3], -1)
-    cot_pieces = exchanged(pieces[3:], -1)
+    token_pieces = exchanged(pieces, -1)
+    cot_p, *pieces = call(
+        input_edges,
+        [((size3, wide), BF), ((hr, wide), BF), ((hc, wide), BF), ((ex, wide), BF)],
+        (cotangent,),
+        1 << 28,
+    )
+    cot_pieces = exchanged(pieces, -1)
     where = jnp.stack([lax.axis_index(a) for a in ROWS_COLS]).astype(jnp.int32)
-    tables, shapes = make_tables(
+    early, early_shapes, late, late_shapes = make_tables(
         (tile_rows, tile_cols), (three_rows, three_cols), ranks, (narrow, wide, 4 * narrow)
     )
-    (
-        sel_a, tail2, sel_tokens, sel_b, head3, sel3, tail3, sel3b, head2, sel_e, sel_out,
-        order2, order3, order_m, bias2, bias3,
-    ) = call(tables, shapes, (shift_offsets, where), 1 << 28, scalars=2)
+    scalars = (shift_offsets, where)
+    sel_a, tail2, sel_tokens, sel_b, head3, bias2 = call(
+        early, early_shapes, scalars, 1 << 28, scalars=2
+    )
+    sel3, tail3, sel3b, head2, sel_e, sel_out, order2, order3, order_m, bias3 = call(
+        late, late_shapes, scalars, 1 << 28, scalars=2
+    )
 
     rolled, packed, mixed, wins, *edges = call(
         two_forward,
@@ -745,7 +810,7 @@
         ],
         (normed3, *ahead, cot_p, *cot_pieces, qkv3, proj3, sel3, bias3, tail3),
         1 << 30,
-        scratch=[((n3, 3 * wide), BF)],
+        scratch=[((n3, 3 * wide), BF), ((n3, wide), BF)],
     )
     back = exchanged(edges, 1)
     share3 = wide // (xs * cores)
@@ -804,29 +869,30 @@
     )
 
     sub = wide // (rows * xs * cores)
-    early = spread_sum(line_sum, line_parts(sum_a), (rows, sub, 4 * wide))
-    late = spread_sum(
-        line_sum_late, line_parts(sum_b) + line_parts(sum_c), (rows, sub, 2 * wide + 4 * narrow)
-    )
-    chunk3 = early.astype(BF)
-    merge_chunk = late[:, : 2 * wide].astype(BF)
-    late = late[:, 2 * wide :]
     sub2 = narrow // (rows * xs * cores)
-    gain_sums = jnp.concatenate(
-        [late[sub2 + 1, wide : wide + narrow], late[sub2], late[sub2 + 1, :wide]]
-    )
-    chunk2 = late[:sub2].astype(BF)
-    halves = [merge_chunk[:, h * wide : (h + 1) * wide] for h in range(2)]
-    return (
-        merged_out,
-        tokens_grad,
-        gain_sums,
-        chunk2[:, : 3 * narrow].reshape(-1),
-        chunk2[:, 3 * narrow :].reshape(-1),
-        jnp.concatenate(halves, axis=0).reshape(-1),
-        chunk3[:, : 3 * wide].reshape(-1),
-        chunk3[:, 3 * wide :].reshape(-1),
-    )
+    far = rows // NEAR
+    lanes = 6 * wide + 4 * narrow
+    sum_lines, sum_near = make_line_sum(rows, NEAR, sub)
+    held = line_parts(sum_a) + line_parts(sum_b) + line_parts(sum_c)
+    parts = call(sum_lines, [((far * sub, lanes), BF)] * NEAR, (where, *held), 1 << 26, scalars=1)
+    held = [parts[0]] + [moved_near(parts[j], j, NEAR) for j in range(1, NEAR)]
+    parts = call(sum_near, [((sub, lanes), BF)] * far, (where, *held), 1 << 26, scalars=1)
+    held = [parts[0]] + [moved(parts[j], "rows", j * NEAR) for j in range(1, far)]
+    sizes = (
+        (narrow + 4 * narrow + wide, F32),
+        (sub2 * 3 * narrow, BF),
+        (sub2 * narrow, BF),
+        (2 * sub * wide, BF),
+        (sub * 3 * wide, BF),
+        (sub * wide, BF),
+    )
+    grads = call(
+        make_finish(wide, narrow, sub2, far),
+        [((size // TILE, TILE), kind) for size, kind in sizes],
+        held,
+        1 << 26,
+    )
+    return (merged_out, tokens_grad, *(g.reshape(-1) for g in grads))
 
 
 def solution(mesh):

time: 153 us -> 151 us (0.987)
  waiting for transfers between devices: 43.9 us -> 52.5 us
  starting transfers between devices: 70.1 us -> 62.1 us
  Pallas kernels: 27.2 us -> 33 us
  local copies, waits for them, and re-layouts: 7.1 us -> 1.69 us
  other arithmetic: 1.89 us -> 0.08 us
    ppermute x26 -> x29, waiting for transfers between devices: 20.8 us -> 37.8 us  [moved(): lax.ppermute(value, axis, [(i, (i + by) % count) for i in range(count)])]
    all_to_all x2 -> x0, starting transfers between devices: 14 us -> none  [spread_sum(): spread = lax.all_to_all(blocks, 'rows', 0, 0)]
    ppermute x7, waiting for transfers between devices: 20.5 us -> 7.02 us  [moved_across(): return lax.ppermute(value, ROWS_COLS, pairs)]
    ppermute x0 -> x3, waiting for transfers between devices: none -> 7.67 us  [moved_near(): return lax.ppermute(value, 'rows', pairs)]
    pallas_call x15 -> x18, Pallas kernels: 27.2 us -> 33 us  [call(): pl.pallas_call(body, in_specs=[smem] * scalars + [vmem] * (len(args) - sc...]
    unnamed x43 -> x24, local copies, waits for them, and re-layouts: 5.85 us -> 1.69 us
    ppermute x26 -> x29, starting transfers between devices: 26.5 us -> 30.6 us  [moved(): lax.ppermute(value, axis, [(i, (i + by) % count) for i in range(count)])]
    ppermute x0 -> x3, starting transfers between devices: none -> 3.97 us  [moved_near(): return lax.ppermute(value, 'rows', pairs)]
  transfers between devices with their start and end apart: 35 -> 39, of which waited for: 15 -> 15; matrix products, arithmetic and copies ran while one was open for 2% -> 0% of each run, Pallas kernels for 13% -> 13%
where the time goes in v1:
time: 151 us; the launch traced here: 150 us
  starting transfers between devices  62.1 us (41%)
  waiting for transfers between devices  52.5 us (35%)
  Pallas kernels  33 us (22%)
  local copies, waits for them, and re-layouts  1.69 us (1%)
    ppermute x29, waiting for transfers between devices, moved(): lax.ppermute(value, axis, [(i, (i + by) % count) for i in range(count)])  37.8 us
    pallas_call x18, Pallas kernels, call(): pl.pallas_call(body, in_specs=[smem] * scalars + [vmem] * (len(args) - sc...  33 us
    ppermute x29, starting transfers between devices, moved(): lax.ppermute(value, axis, [(i, (i + by) % count) for i in range(count)])  30.6 us
    ppermute x7, starting transfers between devices, moved_across(): return lax.ppermute(value, ROWS_COLS, pairs)  27.5 us
    ppermute x3, waiting for transfers between devices, moved_near(): return lax.ppermute(value, 'rows', pairs)  7.67 us
    ppermute x7, waiting for transfers between devices, moved_across(): return lax.ppermute(value, ROWS_COLS, pairs)  7.02 us
    ppermute x3, starting transfers between devices, moved_near(): return lax.ppermute(value, 'rows', pairs)  3.97 us
  transfers between devices with their start and end apart: 39, of which 15 were waited for; matrix products, arithmetic and copies ran while one was open for 0% of the time, Pallas kernels for 13%

profile of v1, /device:TPU:40, one launch (start us, length us, event | category | flops | bytes accessed | tf_op | source)
XLA Modules:
  0.0 150.3 jit_solution(17907174991844524337)
XLA Ops:
  0.7 1.0 copy-done.4
  1.6 0.2 shard_map.170
  1.9 24.6 %collective-permute-start.2 = (bf16[48,256]{1,0:T(8,128)(2,1)S(1)}, bf16[48,256]{1,0:T(8,128)(2,1)S(1)}, u32[]{:S(2)}, u32[]{:S(2)}) collective-permute-start(bf16[48,256]{1,0:T(8,128)(2,1)S(1)} %get-tuple-element.102), channel_id=1, source_target_pairs={{0,127},{1,120},{2,121},{3,122},{4,123},{5,124},{6,125},{7,126},{8... | collective-permute-start | bytes 73736 | tf_op jit(solution)/shard_map/ppermute | solution.py:682
  26.5 0.8 collective-permute-start.1
  27.2 0.1 collective-permute-start
  27.5 0.7 copy-done.10
  28.1 3.2 %shard_map.171 = (bf16[512,784]{1,0:T(8,128)(2,1)S(1)}, bf16[320,512]{1,0:T(8,128)(2,1)S(1)}, bf16[448,448]{1,0:T(8,128)(2,1)S(1)}, bf16[448,832]{1,0:T(8,128)(2...) custom-call(s32[4]{0:T(128)S(1)} %copy-done.10, s32[3]{0:T(128)S(1)} %pad_add_fusion.where), custom_call_target="tpu_custom_call" | custom-call | flops 268435456 | bytes 4194304 | tf_op jit(solution)/shard_map/pallas_call | solution.py:660
  31.4 0.5 collective-permute-done.t1
  31.9 4.7 %shard_map.172 = (bf16[512,256]{1,0:T(8,128)(2,1)S(1)}, bf16[512,768]{1,0:T(8,128)(2,1)S(1)}, bf16[512,256]{1,0:T(8,128)(2,1)S(1)}, bf16[512,256]{1,0:T(8,128)(2...) custom-call(bf16[448,256]{1,0:T(8,128)(2,1)S(1)} %get-tuple-element.99.t0.tokens, ...), custom_call_target="tpu_custom_call" | custom-call | flops 1073741824 | bytes 4194304 | tf_op jit(solution)/shard_map/pallas_call | solution.py:660
  36.6 1.5 %collective-permute-start.3 = (bf16[176,256]{1,0:T(8,128)(2,1)S(1)}, bf16[176,256]{1,0:T(8,128)(2,1)S(1)}, u32[]{:S(2)}, u32[]{:S(2)}) collective-permute-start(bf16[176,256]{1,0:T(8,128)(2,1)S(1)} %get-tuple-element.107), channel_id=1, source_target_pairs={{0,8},{8,16},{16,24},{24,32},{32,40},{40,48},{48,56},{56,64},{64,7... | collective-permute-start | bytes 270344 | tf_op jit(solution)/shard_map/ppermute | solution.py:672
  38.1 0.2 shard_map.174
  38.3 3.0 %collective-permute-start.10 = (bf16[48,512]{1,0:T(8,128)(2,1)S(1)}, bf16[48,512]{1,0:T(8,128)(2,1)S(1)}, u32[]{:S(2)}, u32[]{:S(2)}) collective-permute-start(bf16[48,512]{1,0:T(8,128)(2,1)S(1)} %get-tuple-element.119), channel_id=1, source_target_pairs={{0,7},{1,0},{2,1},{3,2},{4,3},{5,4},{6,5},{7,6},{8,15},{9,8},{10,9... | collective-permute-start | bytes 147464 | tf_op jit(solution)/shard_map/ppermute | solution.py:672
  41.3 2.7 %collective-permute-start.9 = (bf16[96,512]{1,0:T(8,128)(2,1)S(1)}, bf16[96,512]{1,0:T(8,128)(2,1)S(1)}, u32[]{:S(2)}, u32[]{:S(2)}) collective-permute-start(bf16[96,512]{1,0:T(8,128)(2,1)S(1)} %get-tuple-element.118), channel_id=1, source_target_pairs={{0,120},{8,0},{16,8},{24,16},{32,24},{40,32},{48,40},{56,48},{64,5... | collective-permute-start | bytes 294920 | tf_op jit(solution)/shard_map/ppermute | solution.py:672
  44.0 0.7 collective-permute-done.5.w3
  44.7 1.6 %shard_map.173 = (bf16[112,1024]{1,0:T(8,128)(2,1)S(1)}, bf16[448,256]{1,0:T(8,128)(2,1)S(1)}, bf16[112,1024]{1,0:T(8,128)(2,1)S(1)}, bf16[112,512]{1,0:T(8,128)...) custom-call(bf16[448,256]{1,0:T(8,128)(2,1)S(1)} %get-tuple-element., ...), custom_call_target="tpu_custom_call" | custom-call | flops 1073741824 | bytes 4194304 | tf_op jit(solution)/shard_map/pallas_call | solution.py:660
  46.3 0.7 collective-permute-start.6
  47.0 0.4 collective-permute-start.11
  47.5 0.4 collective-permute-start.7
  47.9 0.2 collective-permute-start.8
  48.1 2.9 %shard_map.175 = (bf16[128,304]{1,0:T(8,128)(2,1)S(1)}, bf16[192,128]{1,0:T(8,128)(2,1)S(1)}, bf16[112,320]{1,0:T(8,128)(2,1)S(1)}, bf16[320,448]{1,0:T(8,128)(2...) custom-call(s32[4]{0:T(128)S(1)} %copy-done.11, ...), custom_call_target="tpu_custom_call" | custom-call | flops 268435456 | bytes 4194304 | tf_op jit(solution)/shard_map/pallas_call | solution.py:660
  51.1 1.0 collective-permute-done.8.n3
  52.1 4.1 %shard_map.176 = (bf16[128,1024]{1,0:T(8,128)(2,1)S(1)}, bf16[128,512]{1,0:T(8,128)(2,1)S(1)}, bf16[128,512]{1,0:T(8,128)(2,1)S(1)}, bf16[128,512]{1,0:T(8,128)(...) custom-call(bf16[112,512]{1,0:T(8,128)(2,1)S(1)} %get-tuple-element., ...), custom_call_target="tpu_custom_call" | custom-call | flops 1073741824 | bytes 4194304 | tf_op jit(solution)/shard_map/pallas_call | solution.py:660
  56.2 2.1 %shard_map.180 = (bf16[4,64,2048]{2,1,0:T(8,128)(2,1)S(1)}, bf16[4,64,2048]{2,1,0:T(8,128)(2,1)S(1)}) custom-call(bf16[128,512]{1,0:T(8,128)(2,1)S(1)} %get-tuple-element.150.rolled, bf16[128,512]{1,0:T(8,128)(2,1)S(1)} %get-tuple-element.151.above, bf16[128,512]{1,0:T(8,128)(2,1)S(1)} %get-tuple-element.152.mixed, ...), custom_call_target="tpu_custom_call" | custom-call | flops 1073741824 | bytes 4194304 | tf_op jit(solution)/shard_map/pallas_call | solution.py:660
  58.4 0.4 collective-permute-start.21
  58.8 1.7 %collective-permute-start.12 = (bf16[96,1024]{1,0:T(8,128)(2,1)S(1)}, bf16[96,1024]{1,0:T(8,128)(2,1)S(1)}, u32[]{:S(2)}, u32[]{:S(2)}) collective-permute-start(bf16[96,1024]{1,0:T(8,128)(2,1)S(1)} %get-tuple-element.125), channel_id=1, source_target_pairs={{0,8},{8,16},{16,24},{24,32},{32,40},{40,48},{48,56},{56,64},{64,7... | collective-permute-start | bytes 589832 | tf_op jit(solution)/shard_map/ppermute | solution.py:672
  60.5 1.6 %collective-permute-start.14 = (bf16[48,1024]{1,0:T(8,128)(2,1)S(1)}, bf16[48,1024]{1,0:T(8,128)(2,1)S(1)}, u32[]{:S(2)}, u32[]{:S(2)}) collective-permute-start(bf16[48,1024]{1,0:T(8,128)(2,1)S(1)} %get-tuple-element.127), channel_id=1, source_target_pairs={{0,9},{1,10},{2,11},{3,12},{4,13},{5,14},{6,15},{7,8},{8,17},{9,18... | collective-permute-start | bytes 294920 | tf_op jit(solution)/shard_map/ppermute | solution.py:682
  62.1 3.7 %collective-permute-done.13.b2 = bf16[48,1024]{1,0:T(8,128)(2,1)S(1)} collective-permute-done((bf16[48,1024]{1,0:T(8,128)(2,1)S(1)}, bf16[48,1024]{1,0:T(8,128)(2,1)S(1)}, u32[]{:S(2)}, u32[]{:S(2)}) %collective-permute-start.13) | collective-permute-done | bytes 98336 | tf_op jit(solution)/shard_map/ppermute | solution.py:672
  65.7 5.2 %collective-permute-done.14.b3 = bf16[48,1024]{1,0:T(8,128)(2,1)S(1)} collective-permute-done((bf16[48,1024]{1,0:T(8,128)(2,1)S(1)}, bf16[48,1024]{1,0:T(8,128)(2,1)S(1)}, u32[]{:S(2)}, u32[]{:S(2)}) %collective-permute-start.14) | collective-permute-done | bytes 98336 | tf_op jit(solution)/shard_map/ppermute | solution.py:682
  70.9 1.3 shard_map.177
  72.2 0.7 collective-permute-start.17
  72.9 0.2 collective-permute-start.16
  73.1 0.4 collective-permute-start.15
  73.5 1.8 %shard_map.182 = (bf16[4,64,1024]{2,1,0:T(8,128)(2,1)S(1)}, bf16[4,64,1024]{2,1,0:T(8,128)(2,1)S(1)}) custom-call(bf16[112,1024]{1,0:T(8,128)(2,1)S(1)} %get-tuple-element.161.norm, bf16[112,512]{1,0:T(8,128)(2,1)S(1)} %get-tuple-element.162.d_rows, bf16[256,256]{1,0:T(8,128)(2,1)S(1)} %get-tuple-element.163.order), custom_call_target="tpu_custom_call" | custom-call | flops 1073741824 | bytes 4194304 | tf_op jit(solution)/shard_map/pallas_call | solution.py:660
  75.3 0.1 collective-permute-start.25
  75.5 2.7 %collective-permute-done.15.d1 = bf16[176,256]{1,0:T(8,128)(2,1)S(1)} collective-permute-done((bf16[176,256]{1,0:T(8,128)(2,1)S(1)}, bf16[176,256]{1,0:T(8,128)(2,1)S(1)}, u32[]{:S(2)}, u32[]{:S(2)}) %collective-permute-start.15) | collective-permute-done | bytes 90144 | tf_op jit(solution)/shard_map/ppermute | solution.py:672
  78.2 6.4 %shard_map.178 = (bf16[512,256]{1,0:T(8,128)(2,1)S(1)}, bf16[4,48,1024]{2,1,0:T(8,128)(2,1)S(1)}, bf16[4,48,1024]{2,1,0:T(8,128)(2,1)S(1)}, bf16[176,256]{1,0:T(...) custom-call(bf16[448,256]{1,0:T(8,128)(2,1)S(1)} %get-tuple-element.133.d0.d_two, ...), custom_call_target="tpu_custom_call" | custom-call | flops 1073741824 | bytes 4194304 | tf_op jit(solution)/shard_map/pallas_call | solution.py:660
  84.7 1.7 %collective-permute-done.29.got = bf16[4,48,1024]{2,1,0:T(8,128)(2,1)S(1)} collective-permute-done((bf16[4,48,1024]{2,1,0:T(8,128)(2,1)S(1)}, bf16[4,48,1024]{2,1,0:T(8,128)(2,1)S(1)}, u32[]{:S(2)}, u32[]{:S(2)}) %collective-permute-start.29) | collective-permute-done | bytes 393248 | tf_op jit(solution)/shard_map/ppermute | solution.py:672
  86.5 1.0 collective-permute-start.30
  87.6 1.3 collective-permute-start.31
  89.0 2.2 %collective-permute-start.26 = (bf16[64,1024]{1,0:T(8,128)(2,1)S(1)}, bf16[64,1024]{1,0:T(8,128)(2,1)S(1)}, u32[]{:S(2)}, u32[]{:S(2)}) collective-permute-start(bf16[64,1024]{1,0:T(8,128)(2,1)S(1)} %get-tuple-element.167), channel_id=1, source_target_pairs={{0,2},{2,4},{4,6},{6,0},{1,3},{3,5},{5,7},{7,1},{8,10},{10,12},{12... | collective-permute-start | bytes 393224 | tf_op jit(solution)/shard_map/ppermute | solution.py:672
  91.2 0.2 shard_map.181
  91.4 0.2 collective-permute-start.22
  91.7 2.5 %collective-permute-start.23 = (bf16[64,2048]{1,0:T(8,128)(2,1)S(1)}, bf16[64,2048]{1,0:T(8,128)(2,1)S(1)}, u32[]{:S(2)}, u32[]{:S(2)}) collective-permute-start(bf16[64,2048]{1,0:T(8,128)(2,1)S(1)} %get-tuple-element.159), channel_id=1, source_target_pairs={{0,4},{2,6},{4,0},{6,2},{1,5},{3,7},{5,1},{7,3},{8,12},{10,14},{12... | collective-permute-start | bytes 786440 | tf_op jit(solution)/shard_map/ppermute | solution.py:672
  94.1 1.6 %collective-permute-done.30.refs_9_ = bf16[48,1024]{1,0:T(8,128)(2,1)S(1)} collective-permute-done((bf16[48,1024]{1,0:T(8,128)(2,1)S(1)}, bf16[48,1024]{1,0:T(8,128)(2,1)S(1)}, u32[]{:S(2)}, u32[]{:S(2)}) %collective-permute-start.30) | collective-permute-done | bytes 98336 | tf_op jit(solution)/shard_map/ppermute | solution.py:672
  95.8 0.4 collective-permute-start.32
  96.2 12.4 %collective-permute-done.32.refs_11_ = bf16[48,1024]{1,0:T(8,128)(2,1)S(1)} collective-permute-done((bf16[48,1024]{1,0:T(8,128)(2,1)S(1)}, bf16[48,1024]{1,0:T(8,128)(2,1)S(1)}, u32[]{:S(2)}, u32[]{:S(2)}) %collective-permute-start.32) | collective-permute-done | bytes 98336 | tf_op jit(solution)/shard_map/ppermute | solution.py:672
  108.6 1.2 collective-permute-start.27
  109.8 2.0 %collective-permute-start.28 = (bf16[64,1024]{1,0:T(8,128)(2,1)S(1)}, bf16[64,1024]{1,0:T(8,128)(2,1)S(1)}, u32[]{:S(2)}, u32[]{:S(2)}) collective-permute-start(bf16[64,1024]{1,0:T(8,128)(2,1)S(1)} %get-tuple-element.169), channel_id=1, source_target_pairs={{0,6},{2,0},{4,2},{6,4},{1,7},{3,1},{5,3},{7,5},{8,14},{10,8},{12,... | collective-permute-start | bytes 393224 | tf_op jit(solution)/shard_map/ppermute | solution.py:672
  111.8 3.3 %collective-permute-done.27.refs_6_ = bf16[64,1024]{1,0:T(8,128)(2,1)S(1)} collective-permute-done((bf16[64,1024]{1,0:T(8,128)(2,1)S(1)}, bf16[64,1024]{1,0:T(8,128)(2,1)S(1)}, u32[]{:S(2)}, u32[]{:S(2)}) %collective-permute-start.27) | collective-permute-done | bytes 131104 | tf_op jit(solution)/shard_map/ppermute | solution.py:672
  115.1 3.3 %collective-permute-done.28.refs_7_ = bf16[64,1024]{1,0:T(8,128)(2,1)S(1)} collective-permute-done((bf16[64,1024]{1,0:T(8,128)(2,1)S(1)}, bf16[64,1024]{1,0:T(8,128)(2,1)S(1)}, u32[]{:S(2)}, u32[]{:S(2)}) %collective-permute-start.28) | collective-permute-done | bytes 131104 | tf_op jit(solution)/shard_map/ppermute | solution.py:672
  118.3 1.0 shard_map.185
  119.4 1.5 collective-permute-start.33
  120.8 0.2 collective-permute-start.34
  121.1 2.3 %collective-permute-start.35 = (bf16[16,4096]{1,0:T(8,128)(2,1)S(1)}, bf16[16,4096]{1,0:T(8,128)(2,1)S(1)}, u32[]{:S(2)}, u32[]{:S(2)}) collective-permute-start(bf16[16,4096]{1,0:T(8,128)(2,1)S(1)} %get-tuple-element.179), channel_id=1, source_target_pairs={{0,24},{8,0},{16,8},{24,16},{32,56},{40,32},{48,40},{56,48},{64,88... | collective-permute-start | bytes 393224 | tf_op jit(solution)/shard_map/ppermute | solution.py:708
  123.4 0.5 collective-permute-start.18
  123.9 3.8 %collective-permute-done.33.refs_1_ = bf16[16,4096]{1,0:T(8,128)(2,1)S(1)} collective-permute-done((bf16[16,4096]{1,0:T(8,128)(2,1)S(1)}, bf16[16,4096]{1,0:T(8,128)(2,1)S(1)}, u32[]{:S(2)}, u32[]{:S(2)}) %collective-permute-start.33) | collective-permute-done | bytes 131104 | tf_op jit(solution)/shard_map/ppermute | solution.py:708
  127.7 3.9 %collective-permute-done.34.refs_2_ = bf16[16,4096]{1,0:T(8,128)(2,1)S(1)} collective-permute-done((bf16[16,4096]{1,0:T(8,128)(2,1)S(1)}, bf16[16,4096]{1,0:T(8,128)(2,1)S(1)}, u32[]{:S(2)}, u32[]{:S(2)}) %collective-permute-start.34) | collective-permute-done | bytes 131104 | tf_op jit(solution)/shard_map/ppermute | solution.py:708
  131.6 0.7 shard_map.186
  132.3 1.0 collective-permute-start.36
  133.3 5.8 %collective-permute-start.37 = (bf16[4,4096]{1,0:T(4,128)(2,1)S(1)}, bf16[4,4096]{1,0:T(4,128)(2,1)S(1)}, u32[]{:S(2)}, u32[]{:S(2)}) collective-permute-start(bf16[4,4096]{1,0:T(4,128)(2,1)S(1)} %get-tuple-element.182), channel_id=1, source_target_pairs={{0,64},{8,72},{16,80},{24,88},{32,96},{40,104},{48,112},{56,120},{... | collective-permute-start | bytes 98312 | tf_op jit(solution)/shard_map/ppermute | solution.py:672
  139.2 1.7 %shard_map.179 = bf16[14,28,256]{2,1,0:T(8,128)(2,1)} custom-call(bf16[512,256]{1,0:T(8,128)(2,1)S(1)} %get-tuple-element.144.w0, bf16[176,256]{1,0:T(8,128)(2,1)S(1)} %collective-permute-done.18.w1, bf16[96,256]{1,0:T(8,128)(2,1)S(1)} %collective-permute-done.19.w2, bf16[48,256]{1,0:T(8,128)(2,1)S(1)} %collective-permute-done.20.w3, ...), custom_call_target="tpu_custom_call" | custom-call | flops 1073741824 | bytes 4194304 | tf_op jit(solution)/shard_map/pallas_call | solution.py:660
  141.0 5.0 %collective-permute-done.37.refs_2_ = bf16[4,4096]{1,0:T(4,128)(2,1)S(1)} collective-permute-done((bf16[4,4096]{1,0:T(4,128)(2,1)S(1)}, bf16[4,4096]{1,0:T(4,128)(2,1)S(1)}, u32[]{:S(2)}, u32[]{:S(2)}) %collective-permute-start.37) | collective-permute-done | bytes 32800 | tf_op jit(solution)/shard_map/ppermute | solution.py:672
  145.9 3.7 %collective-permute-done.38.refs_3_ = bf16[4,4096]{1,0:T(4,128)(2,1)S(1)} collective-permute-done((bf16[4,4096]{1,0:T(4,128)(2,1)S(1)}, bf16[4,4096]{1,0:T(4,128)(2,1)S(1)}, u32[]{:S(2)}, u32[]{:S(2)}) %collective-permute-start.38) | collective-permute-done | bytes 32800 | tf_op jit(solution)/shard_map/ppermute | solution.py:672
  149.6 0.6 shard_map.187
  (57 shorter events, 0.8 us)
Async XLA Ops:
  0.6 31.2 %copy-start.3 = (bf16[256,768]{1,0:T(8,128)(2,1)S(1)}, bf16[256,768]{1,0:T(8,128)(2,1)}, u32[]{:S(2)}) copy-start(bf16[256,768]{1,0:T(8,128)(2,1)} %qkv.5) | copy-start | bytes 1179652
  0.6 1.0 copy-start.4
  1.6 30.2 %copy-start.5 = (bf16[256,256]{1,0:T(8,128)(2,1)S(1)}, bf16[256,256]{1,0:T(8,128)(2,1)}, u32[]{:S(2)}) copy-start(bf16[256,256]{1,0:T(8,128)(2,1)} %proj.5) | copy-start | bytes 393220
  1.6 30.2 %copy-start.9 = (f32[256]{0:T(256)S(1)}, f32[256]{0:T(256)}, u32[]{:S(2)}) copy-start(f32[256]{0:T(256)} %param.14) | copy-start | bytes 3076
  1.9 29.5 %collective-permute-start.2 = (bf16[48,256]{1,0:T(8,128)(2,1)S(1)}, bf16[48,256]{1,0:T(8,128)(2,1)S(1)}, u32[]{:S(2)}, u32[]{:S(2)}) collective-permute-start(bf16[48,256]{1,0:T(8,128)(2,1)S(1)} %get-tuple-element.102), channel_id=1, source_target_pairs={{0,127},{1,120},{2,121},{3,122},{4,123},{5,124},{6,125},{7,126},{8... | collective-permute-start | bytes 73736 | tf_op jit(solution)/shard_map/ppermute | solution.py:682
  26.5 4.9 %collective-permute-start.1 = (bf16[96,256]{1,0:T(8,128)(2,1)S(1)}, bf16[96,256]{1,0:T(8,128)(2,1)S(1)}, u32[]{:S(2)}, u32[]{:S(2)}) collective-permute-start(bf16[96,256]{1,0:T(8,128)(2,1)S(1)} %get-tuple-element.101), channel_id=1, source_target_pairs={{0,7},{1,0},{2,1},{3,2},{4,3},{5,4},{6,5},{7,6},{8,15},{9,8},{10,9... | collective-permute-start | bytes 147464 | tf_op jit(solution)/shard_map/ppermute | solution.py:672
  27.2 4.6 %collective-permute-start = (bf16[192,256]{1,0:T(8,128)(2,1)S(1)}, bf16[192,256]{1,0:T(8,128)(2,1)S(1)}, u32[]{:S(2)}, u32[]{:S(2)}) collective-permute-start(bf16[192,256]{1,0:T(8,128)(2,1)S(1)} %get-tuple-element.100), channel_id=1, source_target_pairs={{0,120},{8,0},{16,8},{24,16},{32,24},{40,32},{48,40},{56,48},{64,5... | collective-permute-start | bytes 294920 | tf_op jit(solution)/shard_map/ppermute | solution.py:672
  27.5 0.7 copy-start.10
  31.9 6.3 %copy-start.6 = (bf16[7,14,512]{2,1,0:T(8,128)(2,1)S(1)}, bf16[7,14,512]{2,1,0:T(8,128)(2,1)}, u32[]{:S(2)}) copy-start(bf16[7,14,512]{2,1,0:T(8,128)(2,1)} %source.3) | copy-start | bytes 301060
  31.9 12.8 %copy-start.1 = (bf16[1024,512]{1,0:T(8,128)(2,1)S(1)}, bf16[1024,512]{1,0:T(8,128)(2,1)}, u32[]{:S(2)}) copy-start(bf16[1024,512]{1,0:T(8,128)(2,1)} %weight.3) | copy-start | bytes 3145732
  31.9 12.8 %copy-start.7 = (f32[1024]{0:T(1024)S(1)}, f32[1024]{0:T(1024)}, u32[]{:S(2)}) copy-start(f32[1024]{0:T(1024)} %param.17) | copy-start | bytes 12292
  31.9 12.8 %copy-start.8 = (f32[512]{0:T(512)S(1)}, f32[512]{0:T(512)}, u32[]{:S(2)}) copy-start(f32[512]{0:T(512)} %param.19) | copy-start | bytes 6148
  36.6 8.1 %collective-permute-start.3 = (bf16[176,256]{1,0:T(8,128)(2,1)S(1)}, bf16[176,256]{1,0:T(8,128)(2,1)S(1)}, u32[]{:S(2)}, u32[]{:S(2)}) collective-permute-start(bf16[176,256]{1,0:T(8,128)(2,1)S(1)} %get-tuple-element.107), channel_id=1, source_target_pairs={{0,8},{8,16},{16,24},{24,32},{32,40},{40,48},{48,56},{56,64},{64,7... | collective-permute-start | bytes 270344 | tf_op jit(solution)/shard_map/ppermute | solution.py:672
  38.1 6.6 %collective-permute-start.4 = (bf16[96,256]{1,0:T(8,128)(2,1)S(1)}, bf16[96,256]{1,0:T(8,128)(2,1)S(1)}, u32[]{:S(2)}, u32[]{:S(2)}) collective-permute-start(bf16[96,256]{1,0:T(8,128)(2,1)S(1)} %get-tuple-element.108), channel_id=1, source_target_pairs={{0,1},{1,2},{2,3},{3,4},{4,5},{5,6},{6,7},{7,0},{8,9},{9,10},{10,1... | collective-permute-start | bytes 147464 | tf_op jit(solution)/shard_map/ppermute | solution.py:672
  38.1 6.6 %collective-permute-start.5 = (bf16[48,256]{1,0:T(8,128)(2,1)S(1)}, bf16[48,256]{1,0:T(8,128)(2,1)S(1)}, u32[]{:S(2)}, u32[]{:S(2)}) collective-permute-start(bf16[48,256]{1,0:T(8,128)(2,1)S(1)} %get-tuple-element.109), channel_id=1, source_target_pairs={{0,9},{1,10},{2,11},{3,12},{4,13},{5,14},{6,15},{7,8},{8,17},{9,18... | collective-permute-start | bytes 73736 | tf_op jit(solution)/shard_map/ppermute | solution.py:682
  38.3 9.6 %collective-permute-start.10 = (bf16[48,512]{1,0:T(8,128)(2,1)S(1)}, bf16[48,512]{1,0:T(8,128)(2,1)S(1)}, u32[]{:S(2)}, u32[]{:S(2)}) collective-permute-start(bf16[48,512]{1,0:T(8,128)(2,1)S(1)} %get-tuple-element.119), channel_id=1, source_target_pairs={{0,7},{1,0},{2,1},{3,2},{4,3},{5,4},{6,5},{7,6},{8,15},{9,8},{10,9... | collective-permute-start | bytes 147464 | tf_op jit(solution)/shard_map/ppermute | solution.py:672
  41.3 9.8 %collective-permute-start.9 = (bf16[96,512]{1,0:T(8,128)(2,1)S(1)}, bf16[96,512]{1,0:T(8,128)(2,1)S(1)}, u32[]{:S(2)}, u32[]{:S(2)}) collective-permute-start(bf16[96,512]{1,0:T(8,128)(2,1)S(1)} %get-tuple-element.118), channel_id=1, source_target_pairs={{0,120},{8,0},{16,8},{24,16},{32,24},{40,32},{48,40},{56,48},{64,5... | collective-permute-start | bytes 294920 | tf_op jit(solution)/shard_map/ppermute | solution.py:672
  44.7 3.4 %copy-start.11 = (s32[4]{0:T(128)S(1)}, s32[4]{0:T(128)}, u32[]{:S(2)}) copy-start(s32[4]{0:T(128)} %offsets.3) | copy-start | bytes 52
  44.7 7.4 %copy-start = (bf16[512,1536]{1,0:T(8,128)(2,1)S(1)}, bf16[512,1536]{1,0:T(8,128)(2,1)}, u32[]{:S(2)}) copy-start(bf16[512,1536]{1,0:T(8,128)(2,1)} %qkv.4) | copy-start | bytes 4718596
  44.7 7.4 %copy-start.2 = (bf16[512,512]{1,0:T(8,128)(2,1)S(1)}, bf16[512,512]{1,0:T(8,128)(2,1)}, u32[]{:S(2)}) copy-start(bf16[512,512]{1,0:T(8,128)(2,1)} %proj.4) | copy-start | bytes 1572868
  46.3 5.8 %collective-permute-start.6 = (bf16[96,512]{1,0:T(8,128)(2,1)S(1)}, bf16[96,512]{1,0:T(8,128)(2,1)S(1)}, u32[]{:S(2)}, u32[]{:S(2)}) collective-permute-start(bf16[96,512]{1,0:T(8,128)(2,1)S(1)} %get-tuple-element.114), channel_id=1, source_target_pairs={{0,120},{8,0},{16,8},{24,16},{32,24},{40,32},{48,40},{56,48},{64,5... | collective-permute-start | bytes 294920 | tf_op jit(solution)/shard_map/ppermute | solution.py:672
  47.0 4.0 %collective-permute-start.11 = (bf16[48,512]{1,0:T(8,128)(2,1)S(1)}, bf16[48,512]{1,0:T(8,128)(2,1)S(1)}, u32[]{:S(2)}, u32[]{:S(2)}) collective-permute-start(bf16[48,512]{1,0:T(8,128)(2,1)S(1)} %get-tuple-element.120), channel_id=1, source_target_pairs={{0,127},{1,120},{2,121},{3,122},{4,123},{5,124},{6,125},{7,126},{8... | collective-permute-start | bytes 147464 | tf_op jit(solution)/shard_map/ppermute | solution.py:682
  47.5 3.6 %collective-permute-start.7 = (bf16[48,512]{1,0:T(8,128)(2,1)S(1)}, bf16[48,512]{1,0:T(8,128)(2,1)S(1)}, u32[]{:S(2)}, u32[]{:S(2)}) collective-permute-start(bf16[48,512]{1,0:T(8,128)(2,1)S(1)} %get-tuple-element.115), channel_id=1, source_target_pairs={{0,7},{1,0},{2,1},{3,2},{4,3},{5,4},{6,5},{7,6},{8,15},{9,8},{10,9... | collective-permute-start | bytes 147464 | tf_op jit(solution)/shard_map/ppermute | solution.py:672
  47.9 4.2 %collective-permute-start.8 = (bf16[48,512]{1,0:T(8,128)(2,1)S(1)}, bf16[48,512]{1,0:T(8,128)(2,1)S(1)}, u32[]{:S(2)}, u32[]{:S(2)}) collective-permute-start(bf16[48,512]{1,0:T(8,128)(2,1)S(1)} %get-tuple-element.116), channel_id=1, source_target_pairs={{0,127},{1,120},{2,121},{3,122},{4,123},{5,124},{6,125},{7,126},{8... | collective-permute-start | bytes 147464 | tf_op jit(solution)/shard_map/ppermute | solution.py:682
  58.4 32.8 %collective-permute-start.21 = (bf16[4,64,2048]{2,1,0:T(8,128)(2,1)S(1)}, bf16[4,64,2048]{2,1,0:T(8,128)(2,1)S(1)}, u32[]{:S(2)}, u32[]{:S(2)}) collective-permute-start(bf16[4,64,2048]{2,1,0:T(8,128)(2,1)S(1)} %get-tuple-element.156), channel_id=1, source_target_pairs={{0,1},{1,0},{2,3},{3,2},{4,5},{5,4},{6,7},{7,6},{8,9},{9,8},{10,11... | collective-permute-start | bytes 3145736 | tf_op jit(solution)/shard_map/ppermute | solution.py:672
  58.8 12.1 %collective-permute-start.12 = (bf16[96,1024]{1,0:T(8,128)(2,1)S(1)}, bf16[96,1024]{1,0:T(8,128)(2,1)S(1)}, u32[]{:S(2)}, u32[]{:S(2)}) collective-permute-start(bf16[96,1024]{1,0:T(8,128)(2,1)S(1)} %get-tuple-element.125), channel_id=1, source_target_pairs={{0,8},{8,16},{16,24},{24,32},{32,40},{40,48},{48,56},{56,64},{64,7... | collective-permute-start | bytes 589832 | tf_op jit(solution)/shard_map/ppermute | solution.py:672
  60.5 5.3 %collective-permute-start.13 = (bf16[48,1024]{1,0:T(8,128)(2,1)S(1)}, bf16[48,1024]{1,0:T(8,128)(2,1)S(1)}, u32[]{:S(2)}, u32[]{:S(2)}) collective-permute-start(bf16[48,1024]{1,0:T(8,128)(2,1)S(1)} %get-tuple-element.126), channel_id=1, source_target_pairs={{0,1},{1,2},{2,3},{3,4},{4,5},{5,6},{6,7},{7,0},{8,9},{9,10},{10,1... | collective-permute-start | bytes 294920 | tf_op jit(solution)/shard_map/ppermute | solution.py:672
  60.5 10.4 %collective-permute-start.14 = (bf16[48,1024]{1,0:T(8,128)(2,1)S(1)}, bf16[48,1024]{1,0:T(8,128)(2,1)S(1)}, u32[]{:S(2)}, u32[]{:S(2)}) collective-permute-start(bf16[48,1024]{1,0:T(8,128)(2,1)S(1)} %get-tuple-element.127), channel_id=1, source_target_pairs={{0,9},{1,10},{2,11},{3,12},{4,13},{5,14},{6,15},{7,8},{8,17},{9,18... | collective-permute-start | bytes 294920 | tf_op jit(solution)/shard_map/ppermute | solution.py:682
  72.2 3.3 %collective-permute-start.17 = (bf16[48,256]{1,0:T(8,128)(2,1)S(1)}, bf16[48,256]{1,0:T(8,128)(2,1)S(1)}, u32[]{:S(2)}, u32[]{:S(2)}) collective-permute-start(bf16[48,256]{1,0:T(8,128)(2,1)S(1)} %get-tuple-element.136), channel_id=1, source_target_pairs={{0,127},{1,120},{2,121},{3,122},{4,123},{5,124},{6,125},{7,126},{8... | collective-permute-start | bytes 73736 | tf_op jit(solution)/shard_map/ppermute | solution.py:682
  72.9 2.6 %collective-permute-start.16 = (bf16[96,256]{1,0:T(8,128)(2,1)S(1)}, bf16[96,256]{1,0:T(8,128)(2,1)S(1)}, u32[]{:S(2)}, u32[]{:S(2)}) collective-permute-start(bf16[96,256]{1,0:T(8,128)(2,1)S(1)} %get-tuple-element.135), channel_id=1, source_target_pairs={{0,7},{1,0},{2,1},{3,2},{4,3},{5,4},{6,5},{7,6},{8,15},{9,8},{10,9... | collective-permute-start | bytes 147464 | tf_op jit(solution)/shard_map/ppermute | solution.py:672
  73.1 5.1 %collective-permute-start.15 = (bf16[176,256]{1,0:T(8,128)(2,1)S(1)}, bf16[176,256]{1,0:T(8,128)(2,1)S(1)}, u32[]{:S(2)}, u32[]{:S(2)}) collective-permute-start(bf16[176,256]{1,0:T(8,128)(2,1)S(1)} %get-tuple-element.134), channel_id=1, source_target_pairs={{0,120},{8,0},{16,8},{24,16},{32,24},{40,32},{48,40},{56,48},{64,5... | collective-permute-start | bytes 270344 | tf_op jit(solution)/shard_map/ppermute | solution.py:672
  75.3 13.5 %collective-permute-start.25 = (bf16[4,64,1024]{2,1,0:T(8,128)(2,1)S(1)}, bf16[4,64,1024]{2,1,0:T(8,128)(2,1)S(1)}, u32[]{:S(2)}, u32[]{:S(2)}) collective-permute-start(bf16[4,64,1024]{2,1,0:T(8,128)(2,1)S(1)} %get-tuple-element.165), channel_id=1, source_target_pairs={{0,1},{1,0},{2,3},{3,2},{4,5},{5,4},{6,7},{7,6},{8,9},{9,8},{10,11... | collective-permute-start | bytes 1572872 | tf_op jit(solution)/shard_map/ppermute | solution.py:672
  84.6 1.8 %collective-permute-start.29 = (bf16[4,48,1024]{2,1,0:T(8,128)(2,1)S(1)}, bf16[4,48,1024]{2,1,0:T(8,128)(2,1)S(1)}, u32[]{:S(2)}, u32[]{:S(2)}) collective-permute-start(bf16[4,48,1024]{2,1,0:T(8,128)(2,1)S(1)} %get-tuple-element.171), channel_id=1, source_target_pairs={{0,1},{1,0},{2,3},{3,2},{4,5},{5,4},{6,7},{7,6},{8,9},{9,8},{10,11... | collective-permute-start | bytes 1179656 | tf_op jit(solution)/shard_map/ppermute | solution.py:672
  86.5 9.3 %collective-permute-start.30 = (bf16[48,1024]{1,0:T(8,128)(2,1)S(1)}, bf16[48,1024]{1,0:T(8,128)(2,1)S(1)}, u32[]{:S(2)}, u32[]{:S(2)}) collective-permute-start(bf16[48,1024]{1,0:T(8,128)(2,1)S(1)} %get-tuple-element.173), channel_id=1, source_target_pairs={{0,2},{2,4},{4,6},{6,0},{1,3},{3,5},{5,7},{7,1},{8,10},{10,12},{12... | collective-permute-start | bytes 294920 | tf_op jit(solution)/shard_map/ppermute | solution.py:672
  87.6 8.2 %collective-permute-start.31 = (bf16[48,1024]{1,0:T(8,128)(2,1)S(1)}, bf16[48,1024]{1,0:T(8,128)(2,1)S(1)}, u32[]{:S(2)}, u32[]{:S(2)}) collective-permute-start(bf16[48,1024]{1,0:T(8,128)(2,1)S(1)} %get-tuple-element.174), channel_id=1, source_target_pairs={{0,4},{2,6},{4,0},{6,2},{1,5},{3,7},{5,1},{7,3},{8,12},{10,14},{12... | collective-permute-start | bytes 294920 | tf_op jit(solution)/shard_map/ppermute | solution.py:672
  89.0 20.8 %collective-permute-start.26 = (bf16[64,1024]{1,0:T(8,128)(2,1)S(1)}, bf16[64,1024]{1,0:T(8,128)(2,1)S(1)}, u32[]{:S(2)}, u32[]{:S(2)}) collective-permute-start(bf16[64,1024]{1,0:T(8,128)(2,1)S(1)} %get-tuple-element.167), channel_id=1, source_target_pairs={{0,2},{2,4},{4,6},{6,0},{1,3},{3,5},{5,7},{7,1},{8,10},{10,12},{12... | collective-permute-start | bytes 393224 | tf_op jit(solution)/shard_map/ppermute | solution.py:672
  91.4 26.9 %collective-permute-start.22 = (bf16[64,2048]{1,0:T(8,128)(2,1)S(1)}, bf16[64,2048]{1,0:T(8,128)(2,1)S(1)}, u32[]{:S(2)}, u32[]{:S(2)}) collective-permute-start(bf16[64,2048]{1,0:T(8,128)(2,1)S(1)} %get-tuple-element.158), channel_id=1, source_target_pairs={{0,2},{2,4},{4,6},{6,0},{1,3},{3,5},{5,7},{7,1},{8,10},{10,12},{12... | collective-permute-start | bytes 786440 | tf_op jit(solution)/shard_map/ppermute | solution.py:672
  91.7 26.7 %collective-permute-start.23 = (bf16[64,2048]{1,0:T(8,128)(2,1)S(1)}, bf16[64,2048]{1,0:T(8,128)(2,1)S(1)}, u32[]{:S(2)}, u32[]{:S(2)}) collective-permute-start(bf16[64,2048]{1,0:T(8,128)(2,1)S(1)} %get-tuple-element.159), channel_id=1, source_target_pairs={{0,4},{2,6},{4,0},{6,2},{1,5},{3,7},{5,1},{7,3},{8,12},{10,14},{12... | collective-permute-start | bytes 786440 | tf_op jit(solution)/shard_map/ppermute | solution.py:672
  95.8 22.6 %collective-permute-start.24 = (bf16[64,2048]{1,0:T(8,128)(2,1)S(1)}, bf16[64,2048]{1,0:T(8,128)(2,1)S(1)}, u32[]{:S(2)}, u32[]{:S(2)}) collective-permute-start(bf16[64,2048]{1,0:T(8,128)(2,1)S(1)} %get-tuple-element.160), channel_id=1, source_target_pairs={{0,6},{2,0},{4,2},{6,4},{1,7},{3,1},{5,3},{7,5},{8,14},{10,8},{12,... | collective-permute-start | bytes 786440 | tf_op jit(solution)/shard_map/ppermute | solution.py:672
  95.8 12.8 %collective-permute-start.32 = (bf16[48,1024]{1,0:T(8,128)(2,1)S(1)}, bf16[48,1024]{1,0:T(8,128)(2,1)S(1)}, u32[]{:S(2)}, u32[]{:S(2)}) collective-permute-start(bf16[48,1024]{1,0:T(8,128)(2,1)S(1)} %get-tuple-element.175), channel_id=1, source_target_pairs={{0,6},{2,0},{4,2},{6,4},{1,7},{3,1},{5,3},{7,5},{8,14},{10,8},{12,... | collective-permute-start | bytes 294920 | tf_op jit(solution)/shard_map/ppermute | solution.py:672
  108.6 6.5 %collective-permute-start.27 = (bf16[64,1024]{1,0:T(8,128)(2,1)S(1)}, bf16[64,1024]{1,0:T(8,128)(2,1)S(1)}, u32[]{:S(2)}, u32[]{:S(2)}) collective-permute-start(bf16[64,1024]{1,0:T(8,128)(2,1)S(1)} %get-tuple-element.168), channel_id=1, source_target_pairs={{0,4},{2,6},{4,0},{6,2},{1,5},{3,7},{5,1},{7,3},{8,12},{10,14},{12... | collective-permute-start | bytes 393224 | tf_op jit(solution)/shard_map/ppermute | solution.py:672
  109.8 8.5 %collective-permute-start.28 = (bf16[64,1024]{1,0:T(8,128)(2,1)S(1)}, bf16[64,1024]{1,0:T(8,128)(2,1)S(1)}, u32[]{:S(2)}, u32[]{:S(2)}) collective-permute-start(bf16[64,1024]{1,0:T(8,128)(2,1)S(1)} %get-tuple-element.169), channel_id=1, source_target_pairs={{0,6},{2,0},{4,2},{6,4},{1,7},{3,1},{5,3},{7,5},{8,14},{10,8},{12,... | collective-permute-start | bytes 393224 | tf_op jit(solution)/shard_map/ppermute | solution.py:672
  119.4 8.3 %collective-permute-start.33 = (bf16[16,4096]{1,0:T(8,128)(2,1)S(1)}, bf16[16,4096]{1,0:T(8,128)(2,1)S(1)}, u32[]{:S(2)}, u32[]{:S(2)}) collective-permute-start(bf16[16,4096]{1,0:T(8,128)(2,1)S(1)} %get-tuple-element.177), channel_id=1, source_target_pairs={{0,8},{8,16},{16,24},{24,0},{32,40},{40,48},{48,56},{56,32},{64,72... | collective-permute-start | bytes 393224 | tf_op jit(solution)/shard_map/ppermute | solution.py:708
  120.8 10.7 %collective-permute-start.34 = (bf16[16,4096]{1,0:T(8,128)(2,1)S(1)}, bf16[16,4096]{1,0:T(8,128)(2,1)S(1)}, u32[]{:S(2)}, u32[]{:S(2)}) collective-permute-start(bf16[16,4096]{1,0:T(8,128)(2,1)S(1)} %get-tuple-element.178), channel_id=1, source_target_pairs={{0,16},{8,24},{16,0},{24,8},{32,48},{40,56},{48,32},{56,40},{64,80... | collective-permute-start | bytes 393224 | tf_op jit(solution)/shard_map/ppermute | solution.py:708
  121.1 10.5 %collective-permute-start.35 = (bf16[16,4096]{1,0:T(8,128)(2,1)S(1)}, bf16[16,4096]{1,0:T(8,128)(2,1)S(1)}, u32[]{:S(2)}, u32[]{:S(2)}) collective-permute-start(bf16[16,4096]{1,0:T(8,128)(2,1)S(1)} %get-tuple-element.179), channel_id=1, source_target_pairs={{0,24},{8,0},{16,8},{24,16},{32,56},{40,32},{48,40},{56,48},{64,88... | collective-permute-start | bytes 393224 | tf_op jit(solution)/shard_map/ppermute | solution.py:708
  123.4 15.9 %collective-permute-start.18 = (bf16[176,256]{1,0:T(8,128)(2,1)S(1)}, bf16[176,256]{1,0:T(8,128)(2,1)S(1)}, u32[]{:S(2)}, u32[]{:S(2)}) collective-permute-start(bf16[176,256]{1,0:T(8,128)(2,1)S(1)} %get-tuple-element.145), channel_id=1, source_target_pairs={{0,8},{8,16},{16,24},{24,32},{32,40},{40,48},{48,56},{56,64},{64,7... | collective-permute-start | bytes 270344 | tf_op jit(solution)/shard_map/ppermute | solution.py:672
  123.9 15.3 %collective-permute-start.19 = (bf16[96,256]{1,0:T(8,128)(2,1)S(1)}, bf16[96,256]{1,0:T(8,128)(2,1)S(1)}, u32[]{:S(2)}, u32[]{:S(2)}) collective-permute-start(bf16[96,256]{1,0:T(8,128)(2,1)S(1)} %get-tuple-element.146), channel_id=1, source_target_pairs={{0,1},{1,2},{2,3},{3,4},{4,5},{5,6},{6,7},{7,0},{8,9},{9,10},{10,1... | collective-permute-start | bytes 147464 | tf_op jit(solution)/shard_map/ppermute | solution.py:672
  127.7 11.4 %collective-permute-start.20 = (bf16[48,256]{1,0:T(8,128)(2,1)S(1)}, bf16[48,256]{1,0:T(8,128)(2,1)S(1)}, u32[]{:S(2)}, u32[]{:S(2)}) collective-permute-start(bf16[48,256]{1,0:T(8,128)(2,1)S(1)} %get-tuple-element.147), channel_id=1, source_target_pairs={{0,9},{1,10},{2,11},{3,12},{4,13},{5,14},{6,15},{7,8},{8,17},{9,18... | collective-permute-start | bytes 73736 | tf_op jit(solution)/shard_map/ppermute | solution.py:682
  132.3 8.6 %collective-permute-start.36 = (bf16[4,4096]{1,0:T(4,128)(2,1)S(1)}, bf16[4,4096]{1,0:T(4,128)(2,1)S(1)}, u32[]{:S(2)}, u32[]{:S(2)}) collective-permute-start(bf16[4,4096]{1,0:T(4,128)(2,1)S(1)} %get-tuple-element.181), channel_id=1, source_target_pairs={{0,32},{8,40},{16,48},{24,56},{32,64},{40,72},{48,80},{56,88},{64,... | collective-permute-start | bytes 98312 | tf_op jit(solution)/shard_map/ppermute | solution.py:672
  133.3 12.6 %collective-permute-start.37 = (bf16[4,4096]{1,0:T(4,128)(2,1)S(1)}, bf16[4,4096]{1,0:T(4,128)(2,1)S(1)}, u32[]{:S(2)}, u32[]{:S(2)}) collective-permute-start(bf16[4,4096]{1,0:T(4,128)(2,1)S(1)} %get-tuple-element.182), channel_id=1, source_target_pairs={{0,64},{8,72},{16,80},{24,88},{32,96},{40,104},{48,112},{56,120},{... | collective-permute-start | bytes 98312 | tf_op jit(solution)/shard_map/ppermute | solution.py:672
  139.1 10.5 %collective-permute-start.38 = (bf16[4,4096]{1,0:T(4,128)(2,1)S(1)}, bf16[4,4096]{1,0:T(4,128)(2,1)S(1)}, u32[]{:S(2)}, u32[]{:S(2)}) collective-permute-start(bf16[4,4096]{1,0:T(4,128)(2,1)S(1)} %get-tuple-element.183), channel_id=1, source_target_pairs={{0,96},{8,104},{16,112},{24,120},{32,0},{40,8},{48,16},{56,24},{64... | collective-permute-start | bytes 98312 | tf_op jit(solution)/shard_map/ppermute | solution.py:672

commit v2 on v1

--- a/solution.py
+++ b/solution.py
@@ -1,3 +1,5 @@
+import functools
+
 import jax
 import jax.numpy as jnp
 from jax import lax
@@ -94,6 +96,8 @@
 
 
 def tile_at(start):
+    if isinstance(start, int):
+        return slice(start, start + TILE)
     return pl.ds(pl.multiple_of(start, TILE), TILE)
 
 
@@ -179,23 +183,39 @@
     return jnp.where(p < height * breadth, place(r + row0, c + col0), -1)
 
 
-def input_edges(source, laid, rows_o, cols_o, corner_o):
-    rows, cols, width = source.shape
-    pad = laid.shape[0] // rows
-    blank = jnp.zeros((pad - cols, width), F32)
-    parts = []
-    for r in range(rows):
-        parts += [source[r].astype(F32), blank]
-    whole = jnp.concatenate(parts, axis=0).astype(BF)
-    laid[...] = whole
-    rows_o[...] = whole[: EDGE * pad]
-
-    def place(r, c):
-        return r * pad + c
-
-    for out, height in ((cols_o, rows), (corner_o, EDGE)):
-        wanted = strip(lines(out.shape[0]), height, EDGE, place)
-        out[...] = pick(one_hot(wanted, whole.shape[0]), whole)
+def input_edges(tokens, cot, tokens_o, cot_o, rows_o, cols_o, corner_o):
+    narrow = tokens.shape[2]
+    at = [0, 0, 0]
+    for source, laid in ((tokens, tokens_o), (cot, cot_o)):
+        rows, cols, width = source.shape
+        pad = laid.shape[0] // rows
+        blank = jnp.zeros((pad - cols, width), F32)
+        parts = []
+        for r in range(rows):
+            parts += [source[r].astype(F32), blank]
+        whole = jnp.concatenate(parts, axis=0).astype(BF)
+        laid[...] = whole
+
+        def place(r, c, pad=pad):
+            return r * pad + c
+
+        def edge(height, whole=whole, place=place):
+            wanted = strip(lines(up16(height * EDGE)), height, EDGE, place)
+            return pick(one_hot(wanted, whole.shape[0]), whole)
+
+        edges = (whole[: EDGE * pad], edge(rows), edge(EDGE))
+        for k, (out, value) in enumerate(zip((rows_o, cols_o, corner_o), edges)):
+            for lo in range(0, width, narrow):
+                out[at[k] : at[k] + value.shape[0], :] = value[:, lo : lo + narrow]
+                at[k] += value.shape[0]
+
+
+def cotangent_part(piece, first, wide):
+    narrow = piece.shape[1]
+    size = (piece.shape[0] - first) // (wide // narrow)
+    return jnp.concatenate(
+        [piece[first + k * size : first + (k + 1) * size] for k in range(wide // narrow)], axis=1
+    )
 
 
 def make_tables(tile, tile3, ranks, depths):
@@ -414,24 +434,27 @@
 
 
 def two_forward(
-    t0, t1, t2, t3, gain, qkv, proj, sel, bias, edges, rolled_o, packed_o, mixed_o, wins_o, e0, e1, e2
+    sizes, t0, t1, t2, t3, gain, qkv, proj, sel, bias, edges, rolled_o, packed_o, mixed_o, wins_o, e0, e1, e2
 ):
-    tokens = pick(sel[...], joined((t0, t1, t2, t3)))
+    held = [t0[...]] + [t[:size] for t, size in zip((t1, t2, t3), sizes)]
+    tokens = pick(sel[...], jnp.concatenate(held, axis=0))
     rolled = normed(tokens.astype(F32), gain[...])
     rolled_o[...] = rolled
     packed_o[...] = mm(rolled, qkv[...]).astype(BF)
     width = rolled.shape[1]
 
     def step(g, carry):
-        rows = pl.ds(pl.multiple_of(g * PAIR, PAIR), PAIR)
-        mask = tiled_bias(bias[g])
-        for t in range(width // TILE):
-            q, k, v = thirds(packed_o, rows, width, t)
-            share = soft(q, k, mask)[1].astype(BF)
-            mixed_o[rows, tile_at(t * TILE)] = unstacked(mm(share, v)).astype(BF)
+        for pair in (2 * g, 2 * g + 1):
+            rows = slice(pair * PAIR, (pair + 1) * PAIR)
+            mask = tiled_bias(bias[pair])
+            for t in range(width // TILE):
+                q, k, v = thirds(packed_o, rows, width, t)
+                share = soft(q, k, mask)[1].astype(BF)
+                mixed_o[rows, tile_at(t * TILE)] = unstacked(mm(share, v)).astype(BF)
         return carry
 
-    lax.fori_loop(0, packed_o.shape[0] // PAIR, step, 0)
+    for g in range(packed_o.shape[0] // (2 * PAIR)):
+        step(g, 0)
     projected = mm(mixed_o[...], proj[...]).astype(BF)
     wins_o[...] = projected
     put_edges(projected, edges[...], (e0, e1, e2))
@@ -458,11 +481,14 @@
 
 
 def three_both(
-    n0, n1, n2, n3, c0, c1, c2, c3, qkv, proj, sel, bias, edges,
+    sizes, n0, n1, n2, n3, c0, c1, c2, c3, qkv, proj, sel, bias, edges,
     both_o, rolled_o, above_o, mixed, d_packed, e0, e1, e2, packed, d_mixed,
 ):
     rolled = pick(sel[...], joined((n0, n1, n2, n3)))
-    above = pick(sel[...], joined((c0, c1, c2, c3)))
+    cots = [c0[...]] + [
+        cotangent_part(c[...], size, c0.shape[1]) for c, size in zip((c1, c2, c3), sizes)
+    ]
+    above = pick(sel[...], jnp.concatenate(cots, axis=0))
     rolled_o[...] = rolled
     above_o[...] = above
     width = rolled.shape[1]
@@ -481,7 +507,8 @@
             put_thirds(d_packed, rows, width, t, head_grads(tall, share, given, k, v))
         return carry
 
-    lax.fori_loop(0, width // (2 * TILE), step, 0)
+    for i in range(width // (2 * TILE)):
+        step(i, 0)
     projected = mm(mixed[...], proj[...]).astype(BF)
     d_rolled = mm_nt(d_packed[...], qkv[...]).astype(BF)
     both = jnp.concatenate([projected, d_rolled], axis=1)
@@ -734,25 +761,21 @@
     hr, tr, hc = EDGE * pad3, up16(EDGE * three_cols), up16(three_rows * EDGE)
     gain2, gain_m, gain3 = norm2_gain[None], merge_gain[None], norm3_gain[None]
 
-    tokens_p, *pieces = call(
+    edge_sizes = (EDGE * pad, ec, ex)
+    parts = wide // narrow
+    tokens_p, cot_p, *pieces = call(
         input_edges,
         [
             ((tile_rows * pad, narrow), BF),
-            ((EDGE * pad, narrow), BF),
-            ((ec, narrow), BF),
-            ((ex, narrow), BF),
+            ((size3, wide), BF),
+            ((edge_sizes[0] + parts * hr, narrow), BF),
+            ((edge_sizes[1] + parts * hc, narrow), BF),
+            ((edge_sizes[2] + parts * ex, narrow), BF),
         ],
-        (tokens,),
+        (tokens, cotangent),
         1 << 28,
     )
-    token_pieces = exchanged(pieces, -1)
-    cot_p, *pieces = call(
-        input_edges,
-        [((size3, wide), BF), ((hr, wide), BF), ((hc, wide), BF), ((ex, wide), BF)],
-        (cotangent,),
-        1 << 28,
-    )
-    cot_pieces = exchanged(pieces, -1)
+    input_pieces = exchanged(pieces, -1)
     where = jnp.stack([lax.axis_index(a) for a in ROWS_COLS]).astype(jnp.int32)
     early, early_shapes, late, late_shapes = make_tables(
         (tile_rows, tile_cols), (three_rows, three_cols), ranks, (narrow, wide, 4 * narrow)
@@ -766,7 +789,7 @@
     )
 
     rolled, packed, mixed, wins, *edges = call(
-        two_forward,
+        functools.partial(two_forward, edge_sizes),
         [
             ((n2, narrow), BF),
             ((n2, 3 * narrow), BF),
@@ -776,7 +799,7 @@
             ((ec, narrow), BF),
             ((ex, narrow), BF),
         ],
-        (tokens_p, *token_pieces, gain2, qkv2, proj2, sel_a, bias2, tail2),
+        (tokens_p, *input_pieces, gain2, qkv2, proj2, sel_a, bias2, tail2),
         1 << 30,
     )
     back = exchanged(edges, 1)
@@ -797,7 +820,7 @@
     )
     ahead = exchanged(edges, -1)
     both, rolled3, above3, mixed3, d_packed3, *edges = call(
-        three_both,
+        functools.partial(three_both, edge_sizes),
         [
             ((n3, 2 * wide), BF),
             ((n3, wide), BF),
@@ -808,7 +831,7 @@
             ((hc, 2 * wide), BF),
             ((ex, 2 * wide), BF),
         ],
-        (normed3, *ahead, cot_p, *cot_pieces, qkv3, proj3, sel3, bias3, tail3),
+        (normed3, *ahead, cot_p, *input_pieces, qkv3, proj3, sel3, bias3, tail3),
         1 << 30,
         scratch=[((n3, 3 * wide), BF), ((n3, wide), BF)],
     )

time: 151 us -> 148 us (0.980)
  starting transfers between devices: 62.1 us -> 56.8 us
  waiting for transfers between devices: 52.5 us -> 57.1 us
  Pallas kernels: 33 us -> 30 us
    ppermute x7 -> x6, starting transfers between devices: 27.5 us -> 5 us  [moved_across(): return lax.ppermute(value, ROWS_COLS, pairs)]
    ppermute x29 -> x27, starting transfers between devices: 30.6 us -> 47.8 us  [moved(): lax.ppermute(value, axis, [(i, (i + by) % count) for i in range(count)])]
    ppermute x7 -> x6, waiting for transfers between devices: 7.02 us -> 12 us  [moved_across(): return lax.ppermute(value, ROWS_COLS, pairs)]
    pallas_call x18 -> x17, Pallas kernels: 33 us -> 30 us  [call(): pl.pallas_call(body, in_specs=[smem] * scalars + [vmem] * (len(args) - sc...]
    ppermute x29 -> x27, waiting for transfers between devices: 37.8 us -> 37.4 us  [moved(): lax.ppermute(value, axis, [(i, (i + by) % count) for i in range(count)])]
  transfers between devices with their start and end apart: 39 -> 36, of which waited for: 15 -> 15; matrix products, arithmetic and copies ran while one was open for 0% -> 0% of each run, Pallas kernels for 13% -> 13%
where the time goes in v2:
time: 148 us
  waiting for transfers between devices  57.1 us (39%)
  starting transfers between devices  56.8 us (38%)
  Pallas kernels  30 us (20%)
  local copies, waits for them, and re-layouts  2.58 us (2%)
    ppermute x27, starting transfers between devices, moved(): lax.ppermute(value, axis, [(i, (i + by) % count) for i in range(count)])  47.8 us
    ppermute x27, waiting for transfers between devices, moved(): lax.ppermute(value, axis, [(i, (i + by) % count) for i in range(count)])  37.4 us
    pallas_call x17, Pallas kernels, call(): pl.pallas_call(body, in_specs=[smem] * scalars + [vmem] * (len(args) - sc...  30 us
    ppermute x6, waiting for transfers between devices, moved_across(): return lax.ppermute(value, ROWS_COLS, pairs)  12 us
    ppermute x3, waiting for transfers between devices, moved_near(): return lax.ppermute(value, 'rows', pairs)  7.67 us
    ppermute x6, starting transfers between devices, moved_across(): return lax.ppermute(value, ROWS_COLS, pairs)  5 us
    ppermute x3, starting transfers between devices, moved_near(): return lax.ppermute(value, 'rows', pairs)  4.08 us
  transfers between devices with their start and end apart: 36, of which 15 were waited for; matrix products, arithmetic and copies ran while one was open for 0% of the time, Pallas kernels for 13%

profile of v2, /device:TPU:40, one launch (start us, length us, event | category | flops | bytes accessed | tf_op | source)
XLA Modules:
  0.0 147.5 jit_solution(8187027144164990676)
XLA Ops:
  0.7 1.0 copy-done.4
  1.6 0.9 copy-done.6
  2.5 0.2 shard_map.170
  2.8 22.5 %collective-permute-start = (bf16[384,256]{1,0:T(8,128)(2,1)S(1)}, bf16[384,256]{1,0:T(8,128)(2,1)S(1)}, u32[]{:S(2)}, u32[]{:S(2)}) collective-permute-start(bf16[384,256]{1,0:T(8,128)(2,1)S(1)} %get-tuple-element.97), channel_id=1, source_target_pairs={{0,120},{8,0},{16,8},{24,16},{32,24},{40,32},{48,40},{56,48},{64,5... | collective-permute-start | bytes 589832 | tf_op jit(solution)/shard_map/ppermute | solution.py:699
  25.3 2.2 %collective-permute-start.2 = (bf16[144,256]{1,0:T(8,128)(2,1)S(1)}, bf16[144,256]{1,0:T(8,128)(2,1)S(1)}, u32[]{:S(2)}, u32[]{:S(2)}) collective-permute-start(bf16[144,256]{1,0:T(8,128)(2,1)S(1)} %get-tuple-element.99), channel_id=1, source_target_pairs={{0,127},{1,120},{2,121},{3,122},{4,123},{5,124},{6,125},{7,126},{8... | collective-permute-start | bytes 221192 | tf_op jit(solution)/shard_map/ppermute | solution.py:709
  27.5 0.8 collective-permute-start.1
  28.4 0.7 copy-done.10
  29.1 3.2 %shard_map.171 = (bf16[512,784]{1,0:T(8,128)(2,1)S(1)}, bf16[320,512]{1,0:T(8,128)(2,1)S(1)}, bf16[448,448]{1,0:T(8,128)(2,1)S(1)}, bf16[448,832]{1,0:T(8,128)(2...) custom-call(s32[4]{0:T(128)S(1)} %copy-done.10, s32[3]{0:T(128)S(1)} %pad_add_fusion.where), custom_call_target="tpu_custom_call" | custom-call | flops 268435456 | bytes 4194304 | tf_op jit(solution)/shard_map/pallas_call | solution.py:687
  32.4 2.6 %shard_map.172 = (bf16[512,256]{1,0:T(8,128)(2,1)S(1)}, bf16[512,768]{1,0:T(8,128)(2,1)S(1)}, bf16[512,256]{1,0:T(8,128)(2,1)S(1)}, bf16[512,256]{1,0:T(8,128)(2...) custom-call(bf16[448,256]{1,0:T(8,128)(2,1)S(1)} %get-tuple-element.96.t0.tokens, ...), custom_call_target="tpu_custom_call" | custom-call | flops 1073741824 | bytes 4194304 | tf_op jit(solution)/shard_map/pallas_call | solution.py:687
  35.0 2.0 %collective-permute-start.3 = (bf16[176,256]{1,0:T(8,128)(2,1)S(1)}, bf16[176,256]{1,0:T(8,128)(2,1)S(1)}, u32[]{:S(2)}, u32[]{:S(2)}) collective-permute-start(bf16[176,256]{1,0:T(8,128)(2,1)S(1)} %get-tuple-element.104), channel_id=1, source_target_pairs={{0,8},{8,16},{16,24},{24,32},{32,40},{40,48},{48,56},{56,64},{64,7... | collective-permute-start | bytes 270344 | tf_op jit(solution)/shard_map/ppermute | solution.py:699
  37.0 6.6 %collective-permute-done.5.w3 = bf16[48,256]{1,0:T(8,128)(2,1)S(1)} collective-permute-done((bf16[48,256]{1,0:T(8,128)(2,1)S(1)}, bf16[48,256]{1,0:T(8,128)(2,1)S(1)}, u32[]{:S(2)}, u32[]{:S(2)}) %collective-permute-start.5) | collective-permute-done | bytes 24608 | tf_op jit(solution)/shard_map/ppermute | solution.py:709
  43.6 1.6 %shard_map.173 = (bf16[112,1024]{1,0:T(8,128)(2,1)S(1)}, bf16[448,256]{1,0:T(8,128)(2,1)S(1)}, bf16[112,1024]{1,0:T(8,128)(2,1)S(1)}, bf16[112,512]{1,0:T(8,128)...) custom-call(bf16[448,256]{1,0:T(8,128)(2,1)S(1)} %get-tuple-element., ...), custom_call_target="tpu_custom_call" | custom-call | flops 1073741824 | bytes 4194304 | tf_op jit(solution)/shard_map/pallas_call | solution.py:687
  45.2 0.7 collective-permute-start.6
  45.9 0.3 collective-permute-start.7
  46.2 1.2 collective-permute-start.8
  47.4 2.9 %shard_map.174 = (bf16[128,304]{1,0:T(8,128)(2,1)S(1)}, bf16[192,128]{1,0:T(8,128)(2,1)S(1)}, bf16[112,320]{1,0:T(8,128)(2,1)S(1)}, bf16[320,448]{1,0:T(8,128)(2...) custom-call(s32[4]{0:T(128)S(1)} %copy-done.11, ...), custom_call_target="tpu_custom_call" | custom-call | flops 268435456 | bytes 4194304 | tf_op jit(solution)/shard_map/pallas_call | solution.py:687
  50.4 3.3 %shard_map.175 = (bf16[128,1024]{1,0:T(8,128)(2,1)S(1)}, bf16[128,512]{1,0:T(8,128)(2,1)S(1)}, bf16[128,512]{1,0:T(8,128)(2,1)S(1)}, bf16[128,512]{1,0:T(8,128)(...) custom-call(bf16[112,512]{1,0:T(8,128)(2,1)S(1)} %get-tuple-element., ...), custom_call_target="tpu_custom_call" | custom-call | flops 1073741824 | bytes 4194304 | tf_op jit(solution)/shard_map/pallas_call | solution.py:687
  53.8 2.1 %shard_map.179 = (bf16[4,64,2048]{2,1,0:T(8,128)(2,1)S(1)}, bf16[4,64,2048]{2,1,0:T(8,128)(2,1)S(1)}) custom-call(bf16[128,512]{1,0:T(8,128)(2,1)S(1)} %get-tuple-element.144.rolled, bf16[128,512]{1,0:T(8,128)(2,1)S(1)} %get-tuple-element.145.above, bf16[128,512]{1,0:T(8,128)(2,1)S(1)} %get-tuple-element.146.mixed, ...), custom_call_target="tpu_custom_call" | custom-call | flops 1073741824 | bytes 4194304 | tf_op jit(solution)/shard_map/pallas_call | solution.py:687
  55.9 0.5 collective-permute-start.18
  56.4 1.7 %collective-permute-start.9 = (bf16[96,1024]{1,0:T(8,128)(2,1)S(1)}, bf16[96,1024]{1,0:T(8,128)(2,1)S(1)}, u32[]{:S(2)}, u32[]{:S(2)}) collective-permute-start(bf16[96,1024]{1,0:T(8,128)(2,1)S(1)} %get-tuple-element.119), channel_id=1, source_target_pairs={{0,8},{8,16},{16,24},{24,32},{32,40},{40,48},{48,56},{56,64},{64,7... | collective-permute-start | bytes 589832 | tf_op jit(solution)/shard_map/ppermute | solution.py:699
  58.1 0.1 collective-permute-start.10
  58.2 1.2 collective-permute-start.11
  59.3 4.0 %collective-permute-done.10.b2 = bf16[48,1024]{1,0:T(8,128)(2,1)S(1)} collective-permute-done((bf16[48,1024]{1,0:T(8,128)(2,1)S(1)}, bf16[48,1024]{1,0:T(8,128)(2,1)S(1)}, u32[]{:S(2)}, u32[]{:S(2)}) %collective-permute-start.10) | collective-permute-done | bytes 98336 | tf_op jit(solution)/shard_map/ppermute | solution.py:699
  63.3 5.1 %collective-permute-done.11.b3 = bf16[48,1024]{1,0:T(8,128)(2,1)S(1)} collective-permute-done((bf16[48,1024]{1,0:T(8,128)(2,1)S(1)}, bf16[48,1024]{1,0:T(8,128)(2,1)S(1)}, u32[]{:S(2)}, u32[]{:S(2)}) %collective-permute-start.11) | collective-permute-done | bytes 98336 | tf_op jit(solution)/shard_map/ppermute | solution.py:709
  68.4 1.3 shard_map.176
  69.8 0.3 collective-permute-start.14
  70.1 0.6 collective-permute-start.13
  70.8 1.8 %shard_map.181 = (bf16[4,64,1024]{2,1,0:T(8,128)(2,1)S(1)}, bf16[4,64,1024]{2,1,0:T(8,128)(2,1)S(1)}) custom-call(bf16[112,1024]{1,0:T(8,128)(2,1)S(1)} %get-tuple-element.155.norm, bf16[112,512]{1,0:T(8,128)(2,1)S(1)} %get-tuple-element.156.d_rows, bf16[256,256]{1,0:T(8,128)(2,1)S(1)} %get-tuple-element.157.order), custom_call_target="tpu_custom_call" | custom-call | flops 1073741824 | bytes 4194304 | tf_op jit(solution)/shard_map/pallas_call | solution.py:687
  72.5 0.1 collective-permute-start.22
  72.7 0.4 collective-permute-done.14.d3
  73.0 2.6 %collective-permute-done.12.d1 = bf16[176,256]{1,0:T(8,128)(2,1)S(1)} collective-permute-done((bf16[176,256]{1,0:T(8,128)(2,1)S(1)}, bf16[176,256]{1,0:T(8,128)(2,1)S(1)}, u32[]{:S(2)}, u32[]{:S(2)}) %collective-permute-start.12) | collective-permute-done | bytes 90144 | tf_op jit(solution)/shard_map/ppermute | solution.py:699
  75.6 6.4 %shard_map.177 = (bf16[512,256]{1,0:T(8,128)(2,1)S(1)}, bf16[4,48,1024]{2,1,0:T(8,128)(2,1)S(1)}, bf16[4,48,1024]{2,1,0:T(8,128)(2,1)S(1)}, bf16[176,256]{1,0:T(...) custom-call(bf16[448,256]{1,0:T(8,128)(2,1)S(1)} %get-tuple-element.127.d0.d_two, ...), custom_call_target="tpu_custom_call" | custom-call | flops 1073741824 | bytes 4194304 | tf_op jit(solution)/shard_map/pallas_call | solution.py:687
  82.0 0.4 collective-permute-start.26
  82.4 1.7 %collective-permute-done.26.got = bf16[4,48,1024]{2,1,0:T(8,128)(2,1)S(1)} collective-permute-done((bf16[4,48,1024]{2,1,0:T(8,128)(2,1)S(1)}, bf16[4,48,1024]{2,1,0:T(8,128)(2,1)S(1)}, u32[]{:S(2)}, u32[]{:S(2)}) %collective-permute-start.26) | collective-permute-done | bytes 393248 | tf_op jit(solution)/shard_map/ppermute | solution.py:699
  84.1 0.1 shard_map.183
  84.2 0.6 collective-permute-start.27
  84.8 1.6 %collective-permute-start.28 = (bf16[48,1024]{1,0:T(8,128)(2,1)S(1)}, bf16[48,1024]{1,0:T(8,128)(2,1)S(1)}, u32[]{:S(2)}, u32[]{:S(2)}) collective-permute-start(bf16[48,1024]{1,0:T(8,128)(2,1)S(1)} %get-tuple-element.168), channel_id=1, source_target_pairs={{0,4},{2,6},{4,0},{6,2},{1,5},{3,7},{5,1},{7,3},{8,12},{10,14},{12... | collective-permute-start | bytes 294920 | tf_op jit(solution)/shard_map/ppermute | solution.py:699
  86.4 0.1 shard_map.182
  86.5 2.1 %collective-permute-start.23 = (bf16[64,1024]{1,0:T(8,128)(2,1)S(1)}, bf16[64,1024]{1,0:T(8,128)(2,1)S(1)}, u32[]{:S(2)}, u32[]{:S(2)}) collective-permute-start(bf16[64,1024]{1,0:T(8,128)(2,1)S(1)} %get-tuple-element.161), channel_id=1, source_target_pairs={{0,2},{2,4},{4,6},{6,0},{1,3},{3,5},{5,7},{7,1},{8,10},{10,12},{12... | collective-permute-start | bytes 393224 | tf_op jit(solution)/shard_map/ppermute | solution.py:699
  88.6 0.2 shard_map.180
  88.9 0.2 collective-permute-start.19
  89.0 2.7 %collective-permute-start.20 = (bf16[64,2048]{1,0:T(8,128)(2,1)S(1)}, bf16[64,2048]{1,0:T(8,128)(2,1)S(1)}, u32[]{:S(2)}, u32[]{:S(2)}) collective-permute-start(bf16[64,2048]{1,0:T(8,128)(2,1)S(1)} %get-tuple-element.153), channel_id=1, source_target_pairs={{0,4},{2,6},{4,0},{6,2},{1,5},{3,7},{5,1},{7,3},{8,12},{10,14},{12... | collective-permute-start | bytes 786440 | tf_op jit(solution)/shard_map/ppermute | solution.py:699
  91.7 1.5 collective-permute-done.27.refs_9_
  93.2 0.5 collective-permute-start.29
  93.6 12.4 %collective-permute-done.29.refs_11_ = bf16[48,1024]{1,0:T(8,128)(2,1)S(1)} collective-permute-done((bf16[48,1024]{1,0:T(8,128)(2,1)S(1)}, bf16[48,1024]{1,0:T(8,128)(2,1)S(1)}, u32[]{:S(2)}, u32[]{:S(2)}) %collective-permute-start.29) | collective-permute-done | bytes 98336 | tf_op jit(solution)/shard_map/ppermute | solution.py:699
  106.0 1.0 collective-permute-start.24
  107.0 2.0 %collective-permute-start.25 = (bf16[64,1024]{1,0:T(8,128)(2,1)S(1)}, bf16[64,1024]{1,0:T(8,128)(2,1)S(1)}, u32[]{:S(2)}, u32[]{:S(2)}) collective-permute-start(bf16[64,1024]{1,0:T(8,128)(2,1)S(1)} %get-tuple-element.163), channel_id=1, source_target_pairs={{0,6},{2,0},{4,2},{6,4},{1,7},{3,1},{5,3},{7,5},{8,14},{10,8},{12,... | collective-permute-start | bytes 393224 | tf_op jit(solution)/shard_map/ppermute | solution.py:699
  109.0 3.5 %collective-permute-done.24.refs_6_ = bf16[64,1024]{1,0:T(8,128)(2,1)S(1)} collective-permute-done((bf16[64,1024]{1,0:T(8,128)(2,1)S(1)}, bf16[64,1024]{1,0:T(8,128)(2,1)S(1)}, u32[]{:S(2)}, u32[]{:S(2)}) %collective-permute-start.24) | collective-permute-done | bytes 131104 | tf_op jit(solution)/shard_map/ppermute | solution.py:699
  112.5 3.3 %collective-permute-done.25.refs_7_ = bf16[64,1024]{1,0:T(8,128)(2,1)S(1)} collective-permute-done((bf16[64,1024]{1,0:T(8,128)(2,1)S(1)}, bf16[64,1024]{1,0:T(8,128)(2,1)S(1)}, u32[]{:S(2)}, u32[]{:S(2)}) %collective-permute-start.25) | collective-permute-done | bytes 131104 | tf_op jit(solution)/shard_map/ppermute | solution.py:699
  115.8 1.0 shard_map.184
  116.8 1.6 %collective-permute-start.30 = (bf16[16,4096]{1,0:T(8,128)(2,1)S(1)}, bf16[16,4096]{1,0:T(8,128)(2,1)S(1)}, u32[]{:S(2)}, u32[]{:S(2)}) collective-permute-start(bf16[16,4096]{1,0:T(8,128)(2,1)S(1)} %get-tuple-element.171), channel_id=1, source_target_pairs={{0,8},{8,16},{16,24},{24,0},{32,40},{40,48},{48,56},{56,32},{64,72... | collective-permute-start | bytes 393224 | tf_op jit(solution)/shard_map/ppermute | solution.py:735
  118.4 0.2 collective-permute-start.31
  118.6 2.3 %collective-permute-start.32 = (bf16[16,4096]{1,0:T(8,128)(2,1)S(1)}, bf16[16,4096]{1,0:T(8,128)(2,1)S(1)}, u32[]{:S(2)}, u32[]{:S(2)}) collective-permute-start(bf16[16,4096]{1,0:T(8,128)(2,1)S(1)} %get-tuple-element.173), channel_id=1, source_target_pairs={{0,24},{8,0},{16,8},{24,16},{32,56},{40,32},{48,40},{56,48},{64,88... | collective-permute-start | bytes 393224 | tf_op jit(solution)/shard_map/ppermute | solution.py:735
  120.9 0.4 collective-permute-start.15
  121.3 3.8 %collective-permute-done.30.refs_1_ = bf16[16,4096]{1,0:T(8,128)(2,1)S(1)} collective-permute-done((bf16[16,4096]{1,0:T(8,128)(2,1)S(1)}, bf16[16,4096]{1,0:T(8,128)(2,1)S(1)}, u32[]{:S(2)}, u32[]{:S(2)}) %collective-permute-start.30) | collective-permute-done | bytes 131104 | tf_op jit(solution)/shard_map/ppermute | solution.py:735
  125.1 3.9 %collective-permute-done.31.refs_2_ = bf16[16,4096]{1,0:T(8,128)(2,1)S(1)} collective-permute-done((bf16[16,4096]{1,0:T(8,128)(2,1)S(1)}, bf16[16,4096]{1,0:T(8,128)(2,1)S(1)}, u32[]{:S(2)}, u32[]{:S(2)}) %collective-permute-start.31) | collective-permute-done | bytes 131104 | tf_op jit(solution)/shard_map/ppermute | solution.py:735
  129.0 0.7 shard_map.185
  129.7 0.3 collective-permute-start.33
  130.0 6.3 %collective-permute-start.34 = (bf16[4,4096]{1,0:T(4,128)(2,1)S(1)}, bf16[4,4096]{1,0:T(4,128)(2,1)S(1)}, u32[]{:S(2)}, u32[]{:S(2)}) collective-permute-start(bf16[4,4096]{1,0:T(4,128)(2,1)S(1)} %get-tuple-element.176), channel_id=1, source_target_pairs={{0,64},{8,72},{16,80},{24,88},{32,96},{40,104},{48,112},{56,120},{... | collective-permute-start | bytes 98312 | tf_op jit(solution)/shard_map/ppermute | solution.py:699
  136.3 0.4 collective-permute-start.35
  136.7 1.7 %shard_map.178 = bf16[14,28,256]{2,1,0:T(8,128)(2,1)} custom-call(bf16[512,256]{1,0:T(8,128)(2,1)S(1)} %get-tuple-element.138.w0, bf16[176,256]{1,0:T(8,128)(2,1)S(1)} %collective-permute-done.15.w1, bf16[96,256]{1,0:T(8,128)(2,1)S(1)} %collective-permute-done.16.w2, bf16[48,256]{1,0:T(8,128)(2,1)S(1)} %collective-permute-done.17.w3, ...), custom_call_target="tpu_custom_call" | custom-call | flops 1073741824 | bytes 4194304 | tf_op jit(solution)/shard_map/pallas_call | solution.py:687
  138.5 4.3 %collective-permute-done.34.refs_2_ = bf16[4,4096]{1,0:T(4,128)(2,1)S(1)} collective-permute-done((bf16[4,4096]{1,0:T(4,128)(2,1)S(1)}, bf16[4,4096]{1,0:T(4,128)(2,1)S(1)}, u32[]{:S(2)}, u32[]{:S(2)}) %collective-permute-start.34) | collective-permute-done | bytes 32800 | tf_op jit(solution)/shard_map/ppermute | solution.py:699
  142.8 4.1 %collective-permute-done.35.refs_3_ = bf16[4,4096]{1,0:T(4,128)(2,1)S(1)} collective-permute-done((bf16[4,4096]{1,0:T(4,128)(2,1)S(1)}, bf16[4,4096]{1,0:T(4,128)(2,1)S(1)}, u32[]{:S(2)}, u32[]{:S(2)}) %collective-permute-start.35) | collective-permute-done | bytes 32800 | tf_op jit(solution)/shard_map/ppermute | solution.py:699
  146.9 0.6 shard_map.186
  (50 shorter events, 0.3 us)
Async XLA Ops:
  0.6 31.7 %copy-start.3 = (bf16[256,768]{1,0:T(8,128)(2,1)S(1)}, bf16[256,768]{1,0:T(8,128)(2,1)}, u32[]{:S(2)}) copy-start(bf16[256,768]{1,0:T(8,128)(2,1)} %qkv.5) | copy-start | bytes 1179652
  0.6 1.0 copy-start.4
  1.6 0.9 copy-start.6
  2.5 29.8 %copy-start.5 = (bf16[256,256]{1,0:T(8,128)(2,1)S(1)}, bf16[256,256]{1,0:T(8,128)(2,1)}, u32[]{:S(2)}) copy-start(bf16[256,256]{1,0:T(8,128)(2,1)} %proj.5) | copy-start | bytes 393220
  2.5 29.8 %copy-start.9 = (f32[256]{0:T(256)S(1)}, f32[256]{0:T(256)}, u32[]{:S(2)}) copy-start(f32[256]{0:T(256)} %param.14) | copy-start | bytes 3076
  2.8 29.5 %collective-permute-start = (bf16[384,256]{1,0:T(8,128)(2,1)S(1)}, bf16[384,256]{1,0:T(8,128)(2,1)S(1)}, u32[]{:S(2)}, u32[]{:S(2)}) collective-permute-start(bf16[384,256]{1,0:T(8,128)(2,1)S(1)} %get-tuple-element.97), channel_id=1, source_target_pairs={{0,120},{8,0},{16,8},{24,16},{32,24},{40,32},{48,40},{56,48},{64,5... | collective-permute-start | bytes 589832 | tf_op jit(solution)/shard_map/ppermute | solution.py:699
  25.3 7.0 %collective-permute-start.2 = (bf16[144,256]{1,0:T(8,128)(2,1)S(1)}, bf16[144,256]{1,0:T(8,128)(2,1)S(1)}, u32[]{:S(2)}, u32[]{:S(2)}) collective-permute-start(bf16[144,256]{1,0:T(8,128)(2,1)S(1)} %get-tuple-element.99), channel_id=1, source_target_pairs={{0,127},{1,120},{2,121},{3,122},{4,123},{5,124},{6,125},{7,126},{8... | collective-permute-start | bytes 221192 | tf_op jit(solution)/shard_map/ppermute | solution.py:709
  27.5 4.8 %collective-permute-start.1 = (bf16[192,256]{1,0:T(8,128)(2,1)S(1)}, bf16[192,256]{1,0:T(8,128)(2,1)S(1)}, u32[]{:S(2)}, u32[]{:S(2)}) collective-permute-start(bf16[192,256]{1,0:T(8,128)(2,1)S(1)} %get-tuple-element.98), channel_id=1, source_target_pairs={{0,7},{1,0},{2,1},{3,2},{4,3},{5,4},{6,5},{7,6},{8,15},{9,8},{10,9... | collective-permute-start | bytes 294920 | tf_op jit(solution)/shard_map/ppermute | solution.py:699
  28.4 0.7 copy-start.10
  32.3 11.2 %copy-start.1 = (bf16[1024,512]{1,0:T(8,128)(2,1)S(1)}, bf16[1024,512]{1,0:T(8,128)(2,1)}, u32[]{:S(2)}) copy-start(bf16[1024,512]{1,0:T(8,128)(2,1)} %weight.3) | copy-start | bytes 3145732
  32.3 11.2 %copy-start.7 = (f32[1024]{0:T(1024)S(1)}, f32[1024]{0:T(1024)}, u32[]{:S(2)}) copy-start(f32[1024]{0:T(1024)} %param.17) | copy-start | bytes 12292
  32.4 11.2 %copy-start.8 = (f32[512]{0:T(512)S(1)}, f32[512]{0:T(512)}, u32[]{:S(2)}) copy-start(f32[512]{0:T(512)} %param.19) | copy-start | bytes 6148
  35.0 8.6 %collective-permute-start.3 = (bf16[176,256]{1,0:T(8,128)(2,1)S(1)}, bf16[176,256]{1,0:T(8,128)(2,1)S(1)}, u32[]{:S(2)}, u32[]{:S(2)}) collective-permute-start(bf16[176,256]{1,0:T(8,128)(2,1)S(1)} %get-tuple-element.104), channel_id=1, source_target_pairs={{0,8},{8,16},{16,24},{24,32},{32,40},{40,48},{48,56},{56,64},{64,7... | collective-permute-start | bytes 270344 | tf_op jit(solution)/shard_map/ppermute | solution.py:699
  37.0 6.6 %collective-permute-start.4 = (bf16[96,256]{1,0:T(8,128)(2,1)S(1)}, bf16[96,256]{1,0:T(8,128)(2,1)S(1)}, u32[]{:S(2)}, u32[]{:S(2)}) collective-permute-start(bf16[96,256]{1,0:T(8,128)(2,1)S(1)} %get-tuple-element.105), channel_id=1, source_target_pairs={{0,1},{1,2},{2,3},{3,4},{4,5},{5,6},{6,7},{7,0},{8,9},{9,10},{10,1... | collective-permute-start | bytes 147464 | tf_op jit(solution)/shard_map/ppermute | solution.py:699
  37.0 6.6 %collective-permute-start.5 = (bf16[48,256]{1,0:T(8,128)(2,1)S(1)}, bf16[48,256]{1,0:T(8,128)(2,1)S(1)}, u32[]{:S(2)}, u32[]{:S(2)}) collective-permute-start(bf16[48,256]{1,0:T(8,128)(2,1)S(1)} %get-tuple-element.106), channel_id=1, source_target_pairs={{0,9},{1,10},{2,11},{3,12},{4,13},{5,14},{6,15},{7,8},{8,17},{9,18... | collective-permute-start | bytes 73736 | tf_op jit(solution)/shard_map/ppermute | solution.py:709
  43.6 3.9 %copy-start.11 = (s32[4]{0:T(128)S(1)}, s32[4]{0:T(128)}, u32[]{:S(2)}) copy-start(s32[4]{0:T(128)} %offsets.3) | copy-start | bytes 52
  43.6 6.9 %copy-start = (bf16[512,1536]{1,0:T(8,128)(2,1)S(1)}, bf16[512,1536]{1,0:T(8,128)(2,1)}, u32[]{:S(2)}) copy-start(bf16[512,1536]{1,0:T(8,128)(2,1)} %qkv.4) | copy-start | bytes 4718596
  43.6 6.8 %copy-start.2 = (bf16[512,512]{1,0:T(8,128)(2,1)S(1)}, bf16[512,512]{1,0:T(8,128)(2,1)}, u32[]{:S(2)}) copy-start(bf16[512,512]{1,0:T(8,128)(2,1)} %proj.4) | copy-start | bytes 1572868
  45.2 5.3 %collective-permute-start.6 = (bf16[96,512]{1,0:T(8,128)(2,1)S(1)}, bf16[96,512]{1,0:T(8,128)(2,1)S(1)}, u32[]{:S(2)}, u32[]{:S(2)}) collective-permute-start(bf16[96,512]{1,0:T(8,128)(2,1)S(1)} %get-tuple-element.111), channel_id=1, source_target_pairs={{0,120},{8,0},{16,8},{24,16},{32,24},{40,32},{48,40},{56,48},{64,5... | collective-permute-start | bytes 294920 | tf_op jit(solution)/shard_map/ppermute | solution.py:699
  45.9 4.5 %collective-permute-start.7 = (bf16[48,512]{1,0:T(8,128)(2,1)S(1)}, bf16[48,512]{1,0:T(8,128)(2,1)S(1)}, u32[]{:S(2)}, u32[]{:S(2)}) collective-permute-start(bf16[48,512]{1,0:T(8,128)(2,1)S(1)} %get-tuple-element.112), channel_id=1, source_target_pairs={{0,7},{1,0},{2,1},{3,2},{4,3},{5,4},{6,5},{7,6},{8,15},{9,8},{10,9... | collective-permute-start | bytes 147464 | tf_op jit(solution)/shard_map/ppermute | solution.py:699
  46.2 4.2 %collective-permute-start.8 = (bf16[48,512]{1,0:T(8,128)(2,1)S(1)}, bf16[48,512]{1,0:T(8,128)(2,1)S(1)}, u32[]{:S(2)}, u32[]{:S(2)}) collective-permute-start(bf16[48,512]{1,0:T(8,128)(2,1)S(1)} %get-tuple-element.113), channel_id=1, source_target_pairs={{0,127},{1,120},{2,121},{3,122},{4,123},{5,124},{6,125},{7,126},{8... | collective-permute-start | bytes 147464 | tf_op jit(solution)/shard_map/ppermute | solution.py:709
  55.9 32.7 %collective-permute-start.18 = (bf16[4,64,2048]{2,1,0:T(8,128)(2,1)S(1)}, bf16[4,64,2048]{2,1,0:T(8,128)(2,1)S(1)}, u32[]{:S(2)}, u32[]{:S(2)}) collective-permute-start(bf16[4,64,2048]{2,1,0:T(8,128)(2,1)S(1)} %get-tuple-element.150), channel_id=1, source_target_pairs={{0,1},{1,0},{2,3},{3,2},{4,5},{5,4},{6,7},{7,6},{8,9},{9,8},{10,11... | collective-permute-start | bytes 3145736 | tf_op jit(solution)/shard_map/ppermute | solution.py:699
  56.4 12.0 %collective-permute-start.9 = (bf16[96,1024]{1,0:T(8,128)(2,1)S(1)}, bf16[96,1024]{1,0:T(8,128)(2,1)S(1)}, u32[]{:S(2)}, u32[]{:S(2)}) collective-permute-start(bf16[96,1024]{1,0:T(8,128)(2,1)S(1)} %get-tuple-element.119), channel_id=1, source_target_pairs={{0,8},{8,16},{16,24},{24,32},{32,40},{40,48},{48,56},{56,64},{64,7... | collective-permute-start | bytes 589832 | tf_op jit(solution)/shard_map/ppermute | solution.py:699
  58.1 5.3 %collective-permute-start.10 = (bf16[48,1024]{1,0:T(8,128)(2,1)S(1)}, bf16[48,1024]{1,0:T(8,128)(2,1)S(1)}, u32[]{:S(2)}, u32[]{:S(2)}) collective-permute-start(bf16[48,1024]{1,0:T(8,128)(2,1)S(1)} %get-tuple-element.120), channel_id=1, source_target_pairs={{0,1},{1,2},{2,3},{3,4},{4,5},{5,6},{6,7},{7,0},{8,9},{9,10},{10,1... | collective-permute-start | bytes 294920 | tf_op jit(solution)/shard_map/ppermute | solution.py:699
  58.2 10.3 %collective-permute-start.11 = (bf16[48,1024]{1,0:T(8,128)(2,1)S(1)}, bf16[48,1024]{1,0:T(8,128)(2,1)S(1)}, u32[]{:S(2)}, u32[]{:S(2)}) collective-permute-start(bf16[48,1024]{1,0:T(8,128)(2,1)S(1)} %get-tuple-element.121), channel_id=1, source_target_pairs={{0,9},{1,10},{2,11},{3,12},{4,13},{5,14},{6,15},{7,8},{8,17},{9,18... | collective-permute-start | bytes 294920 | tf_op jit(solution)/shard_map/ppermute | solution.py:709
  69.8 3.3 %collective-permute-start.14 = (bf16[48,256]{1,0:T(8,128)(2,1)S(1)}, bf16[48,256]{1,0:T(8,128)(2,1)S(1)}, u32[]{:S(2)}, u32[]{:S(2)}) collective-permute-start(bf16[48,256]{1,0:T(8,128)(2,1)S(1)} %get-tuple-element.130), channel_id=1, source_target_pairs={{0,127},{1,120},{2,121},{3,122},{4,123},{5,124},{6,125},{7,126},{8... | collective-permute-start | bytes 73736 | tf_op jit(solution)/shard_map/ppermute | solution.py:709
  70.1 2.9 %collective-permute-start.13 = (bf16[96,256]{1,0:T(8,128)(2,1)S(1)}, bf16[96,256]{1,0:T(8,128)(2,1)S(1)}, u32[]{:S(2)}, u32[]{:S(2)}) collective-permute-start(bf16[96,256]{1,0:T(8,128)(2,1)S(1)} %get-tuple-element.129), channel_id=1, source_target_pairs={{0,7},{1,0},{2,1},{3,2},{4,3},{5,4},{6,5},{7,6},{8,15},{9,8},{10,9... | collective-permute-start | bytes 147464 | tf_op jit(solution)/shard_map/ppermute | solution.py:699
  70.7 4.9 %collective-permute-start.12 = (bf16[176,256]{1,0:T(8,128)(2,1)S(1)}, bf16[176,256]{1,0:T(8,128)(2,1)S(1)}, u32[]{:S(2)}, u32[]{:S(2)}) collective-permute-start(bf16[176,256]{1,0:T(8,128)(2,1)S(1)} %get-tuple-element.128), channel_id=1, source_target_pairs={{0,120},{8,0},{16,8},{24,16},{32,24},{40,32},{48,40},{56,48},{64,5... | collective-permute-start | bytes 270344 | tf_op jit(solution)/shard_map/ppermute | solution.py:699
  72.5 13.9 %collective-permute-start.22 = (bf16[4,64,1024]{2,1,0:T(8,128)(2,1)S(1)}, bf16[4,64,1024]{2,1,0:T(8,128)(2,1)S(1)}, u32[]{:S(2)}, u32[]{:S(2)}) collective-permute-start(bf16[4,64,1024]{2,1,0:T(8,128)(2,1)S(1)} %get-tuple-element.159), channel_id=1, source_target_pairs={{0,1},{1,0},{2,3},{3,2},{4,5},{5,4},{6,7},{7,6},{8,9},{9,8},{10,11... | collective-permute-start | bytes 1572872 | tf_op jit(solution)/shard_map/ppermute | solution.py:699
  82.0 2.1 %collective-permute-start.26 = (bf16[4,48,1024]{2,1,0:T(8,128)(2,1)S(1)}, bf16[4,48,1024]{2,1,0:T(8,128)(2,1)S(1)}, u32[]{:S(2)}, u32[]{:S(2)}) collective-permute-start(bf16[4,48,1024]{2,1,0:T(8,128)(2,1)S(1)} %get-tuple-element.165), channel_id=1, source_target_pairs={{0,1},{1,0},{2,3},{3,2},{4,5},{5,4},{6,7},{7,6},{8,9},{9,8},{10,11... | collective-permute-start | bytes 1179656 | tf_op jit(solution)/shard_map/ppermute | solution.py:699
  84.2 9.0 %collective-permute-start.27 = (bf16[48,1024]{1,0:T(8,128)(2,1)S(1)}, bf16[48,1024]{1,0:T(8,128)(2,1)S(1)}, u32[]{:S(2)}, u32[]{:S(2)}) collective-permute-start(bf16[48,1024]{1,0:T(8,128)(2,1)S(1)} %get-tuple-element.167), channel_id=1, source_target_pairs={{0,2},{2,4},{4,6},{6,0},{1,3},{3,5},{5,7},{7,1},{8,10},{10,12},{12... | collective-permute-start | bytes 294920 | tf_op jit(solution)/shard_map/ppermute | solution.py:699
  84.8 8.4 %collective-permute-start.28 = (bf16[48,1024]{1,0:T(8,128)(2,1)S(1)}, bf16[48,1024]{1,0:T(8,128)(2,1)S(1)}, u32[]{:S(2)}, u32[]{:S(2)}) collective-permute-start(bf16[48,1024]{1,0:T(8,128)(2,1)S(1)} %get-tuple-element.168), channel_id=1, source_target_pairs={{0,4},{2,6},{4,0},{6,2},{1,5},{3,7},{5,1},{7,3},{8,12},{10,14},{12... | collective-permute-start | bytes 294920 | tf_op jit(solution)/shard_map/ppermute | solution.py:699
  86.5 20.5 %collective-permute-start.23 = (bf16[64,1024]{1,0:T(8,128)(2,1)S(1)}, bf16[64,1024]{1,0:T(8,128)(2,1)S(1)}, u32[]{:S(2)}, u32[]{:S(2)}) collective-permute-start(bf16[64,1024]{1,0:T(8,128)(2,1)S(1)} %get-tuple-element.161), channel_id=1, source_target_pairs={{0,2},{2,4},{4,6},{6,0},{1,3},{3,5},{5,7},{7,1},{8,10},{10,12},{12... | collective-permute-start | bytes 393224 | tf_op jit(solution)/shard_map/ppermute | solution.py:699
  88.9 26.9 %collective-permute-start.19 = (bf16[64,2048]{1,0:T(8,128)(2,1)S(1)}, bf16[64,2048]{1,0:T(8,128)(2,1)S(1)}, u32[]{:S(2)}, u32[]{:S(2)}) collective-permute-start(bf16[64,2048]{1,0:T(8,128)(2,1)S(1)} %get-tuple-element.152), channel_id=1, source_target_pairs={{0,2},{2,4},{4,6},{6,0},{1,3},{3,5},{5,7},{7,1},{8,10},{10,12},{12... | collective-permute-start | bytes 786440 | tf_op jit(solution)/shard_map/ppermute | solution.py:699
  89.0 26.8 %collective-permute-start.20 = (bf16[64,2048]{1,0:T(8,128)(2,1)S(1)}, bf16[64,2048]{1,0:T(8,128)(2,1)S(1)}, u32[]{:S(2)}, u32[]{:S(2)}) collective-permute-start(bf16[64,2048]{1,0:T(8,128)(2,1)S(1)} %get-tuple-element.153), channel_id=1, source_target_pairs={{0,4},{2,6},{4,0},{6,2},{1,5},{3,7},{5,1},{7,3},{8,12},{10,14},{12... | collective-permute-start | bytes 786440 | tf_op jit(solution)/shard_map/ppermute | solution.py:699
  93.1 22.6 %collective-permute-start.21 = (bf16[64,2048]{1,0:T(8,128)(2,1)S(1)}, bf16[64,2048]{1,0:T(8,128)(2,1)S(1)}, u32[]{:S(2)}, u32[]{:S(2)}) collective-permute-start(bf16[64,2048]{1,0:T(8,128)(2,1)S(1)} %get-tuple-element.154), channel_id=1, source_target_pairs={{0,6},{2,0},{4,2},{6,4},{1,7},{3,1},{5,3},{7,5},{8,14},{10,8},{12,... | collective-permute-start | bytes 786440 | tf_op jit(solution)/shard_map/ppermute | solution.py:699
  93.2 12.9 %collective-permute-start.29 = (bf16[48,1024]{1,0:T(8,128)(2,1)S(1)}, bf16[48,1024]{1,0:T(8,128)(2,1)S(1)}, u32[]{:S(2)}, u32[]{:S(2)}) collective-permute-start(bf16[48,1024]{1,0:T(8,128)(2,1)S(1)} %get-tuple-element.169), channel_id=1, source_target_pairs={{0,6},{2,0},{4,2},{6,4},{1,7},{3,1},{5,3},{7,5},{8,14},{10,8},{12,... | collective-permute-start | bytes 294920 | tf_op jit(solution)/shard_map/ppermute | solution.py:699
  106.0 6.5 %collective-permute-start.24 = (bf16[64,1024]{1,0:T(8,128)(2,1)S(1)}, bf16[64,1024]{1,0:T(8,128)(2,1)S(1)}, u32[]{:S(2)}, u32[]{:S(2)}) collective-permute-start(bf16[64,1024]{1,0:T(8,128)(2,1)S(1)} %get-tuple-element.162), channel_id=1, source_target_pairs={{0,4},{2,6},{4,0},{6,2},{1,5},{3,7},{5,1},{7,3},{8,12},{10,14},{12... | collective-permute-start | bytes 393224 | tf_op jit(solution)/shard_map/ppermute | solution.py:699
  107.0 8.8 %collective-permute-start.25 = (bf16[64,1024]{1,0:T(8,128)(2,1)S(1)}, bf16[64,1024]{1,0:T(8,128)(2,1)S(1)}, u32[]{:S(2)}, u32[]{:S(2)}) collective-permute-start(bf16[64,1024]{1,0:T(8,128)(2,1)S(1)} %get-tuple-element.163), channel_id=1, source_target_pairs={{0,6},{2,0},{4,2},{6,4},{1,7},{3,1},{5,3},{7,5},{8,14},{10,8},{12,... | collective-permute-start | bytes 393224 | tf_op jit(solution)/shard_map/ppermute | solution.py:699
  116.8 8.3 %collective-permute-start.30 = (bf16[16,4096]{1,0:T(8,128)(2,1)S(1)}, bf16[16,4096]{1,0:T(8,128)(2,1)S(1)}, u32[]{:S(2)}, u32[]{:S(2)}) collective-permute-start(bf16[16,4096]{1,0:T(8,128)(2,1)S(1)} %get-tuple-element.171), channel_id=1, source_target_pairs={{0,8},{8,16},{16,24},{24,0},{32,40},{40,48},{48,56},{56,32},{64,72... | collective-permute-start | bytes 393224 | tf_op jit(solution)/shard_map/ppermute | solution.py:735
  118.4 10.6 %collective-permute-start.31 = (bf16[16,4096]{1,0:T(8,128)(2,1)S(1)}, bf16[16,4096]{1,0:T(8,128)(2,1)S(1)}, u32[]{:S(2)}, u32[]{:S(2)}) collective-permute-start(bf16[16,4096]{1,0:T(8,128)(2,1)S(1)} %get-tuple-element.172), channel_id=1, source_target_pairs={{0,16},{8,24},{16,0},{24,8},{32,48},{40,56},{48,32},{56,40},{64,80... | collective-permute-start | bytes 393224 | tf_op jit(solution)/shard_map/ppermute | solution.py:735
  118.6 10.4 %collective-permute-start.32 = (bf16[16,4096]{1,0:T(8,128)(2,1)S(1)}, bf16[16,4096]{1,0:T(8,128)(2,1)S(1)}, u32[]{:S(2)}, u32[]{:S(2)}) collective-permute-start(bf16[16,4096]{1,0:T(8,128)(2,1)S(1)} %get-tuple-element.173), channel_id=1, source_target_pairs={{0,24},{8,0},{16,8},{24,16},{32,56},{40,32},{48,40},{56,48},{64,88... | collective-permute-start | bytes 393224 | tf_op jit(solution)/shard_map/ppermute | solution.py:735
  120.9 15.9 %collective-permute-start.15 = (bf16[176,256]{1,0:T(8,128)(2,1)S(1)}, bf16[176,256]{1,0:T(8,128)(2,1)S(1)}, u32[]{:S(2)}, u32[]{:S(2)}) collective-permute-start(bf16[176,256]{1,0:T(8,128)(2,1)S(1)} %get-tuple-element.139), channel_id=1, source_target_pairs={{0,8},{8,16},{16,24},{24,32},{32,40},{40,48},{48,56},{56,64},{64,7... | collective-permute-start | bytes 270344 | tf_op jit(solution)/shard_map/ppermute | solution.py:699
  121.3 15.4 %collective-permute-start.16 = (bf16[96,256]{1,0:T(8,128)(2,1)S(1)}, bf16[96,256]{1,0:T(8,128)(2,1)S(1)}, u32[]{:S(2)}, u32[]{:S(2)}) collective-permute-start(bf16[96,256]{1,0:T(8,128)(2,1)S(1)} %get-tuple-element.140), channel_id=1, source_target_pairs={{0,1},{1,2},{2,3},{3,4},{4,5},{5,6},{6,7},{7,0},{8,9},{9,10},{10,1... | collective-permute-start | bytes 147464 | tf_op jit(solution)/shard_map/ppermute | solution.py:699
  125.1 11.2 %collective-permute-start.17 = (bf16[48,256]{1,0:T(8,128)(2,1)S(1)}, bf16[48,256]{1,0:T(8,128)(2,1)S(1)}, u32[]{:S(2)}, u32[]{:S(2)}) collective-permute-start(bf16[48,256]{1,0:T(8,128)(2,1)S(1)} %get-tuple-element.141), channel_id=1, source_target_pairs={{0,9},{1,10},{2,11},{3,12},{4,13},{5,14},{6,15},{7,8},{8,17},{9,18... | collective-permute-start | bytes 73736 | tf_op jit(solution)/shard_map/ppermute | solution.py:709
  129.7 8.7 %collective-permute-start.33 = (bf16[4,4096]{1,0:T(4,128)(2,1)S(1)}, bf16[4,4096]{1,0:T(4,128)(2,1)S(1)}, u32[]{:S(2)}, u32[]{:S(2)}) collective-permute-start(bf16[4,4096]{1,0:T(4,128)(2,1)S(1)} %get-tuple-element.175), channel_id=1, source_target_pairs={{0,32},{8,40},{16,48},{24,56},{32,64},{40,72},{48,80},{56,88},{64,... | collective-permute-start | bytes 98312 | tf_op jit(solution)/shard_map/ppermute | solution.py:699
  130.0 12.7 %collective-permute-start.34 = (bf16[4,4096]{1,0:T(4,128)(2,1)S(1)}, bf16[4,4096]{1,0:T(4,128)(2,1)S(1)}, u32[]{:S(2)}, u32[]{:S(2)}) collective-permute-start(bf16[4,4096]{1,0:T(4,128)(2,1)S(1)} %get-tuple-element.176), channel_id=1, source_target_pairs={{0,64},{8,72},{16,80},{24,88},{32,96},{40,104},{48,112},{56,120},{... | collective-permute-start | bytes 98312 | tf_op jit(solution)/shard_map/ppermute | solution.py:699
  136.3 10.5 %collective-permute-start.35 = (bf16[4,4096]{1,0:T(4,128)(2,1)S(1)}, bf16[4,4096]{1,0:T(4,128)(2,1)S(1)}, u32[]{:S(2)}, u32[]{:S(2)}) collective-permute-start(bf16[4,4096]{1,0:T(4,128)(2,1)S(1)} %get-tuple-element.177), channel_id=1, source_target_pairs={{0,96},{8,104},{16,112},{24,120},{32,0},{40,8},{48,16},{56,24},{64... | collective-permute-start | bytes 98312 | tf_op jit(solution)/shard_map/ppermute | solution.py:699
